TPU v7x, 256 devices: a whole 4x4x8 slice. The times are simulated.
256 devices in a mesh: dp: 2 (over core), expert: 32 (over z_hi, y, x), tensor: 4 (over z_lo).
Axes of the slice: x: 4, y: 4, z: 8 (z_hi: 2, z_lo: 4; z = z_hi * 4 + z_lo), core: 2. Of those that a mesh axis runs over, the one named last changes fastest.
Arguments:
- grad_out: bfloat16 [8192, 3584], P(('dp', 'expert')), may hold values from -6 to 6
- layer_in: bfloat16 [8192, 3584], P(('dp', 'expert')), may hold values from -6 to 6
- routes: int32 [8192, 8], P(('dp', 'expert')), may hold values from 0 to 255, as said below
- combine: float32 [8192, 8], P(('dp', 'expert')), may hold values from 0.2 to 1
- gate_weight: bfloat16 [32, 3584, 1024], P('expert', 'dp', 'tensor'), may hold values from -0.09375 to 0.09375
- up_weight: bfloat16 [32, 3584, 1024], P('expert', 'dp', 'tensor'), may hold values from -0.09375 to 0.09375
- down_weight: bfloat16 [32, 1024, 3584], P('expert', 'tensor', 'dp'), may hold values from -0.1875 to 0.1875
Outputs:
- grad_in: bfloat16 [8192, 3584], P(('dp', 'expert'))
- grad_gate: bfloat16 [32, 3584, 1024], P('expert', 'dp', 'tensor')
- grad_up: bfloat16 [32, 3584, 1024], P('expert', 'dp', 'tensor')
- grad_down: bfloat16 [32, 1024, 3584], P('expert', 'tensor', 'dp')
Inputs may be any that keep to these rules, and one draw needn't show every extreme that they name: `routes`: each row names 8 different experts. In every block of 128 tokens (the tokens of one device) each expert below 32 is named by 1 to 8 tokens, and one such expert, the same for all blocks of a draw, is named by exactly 8 tokens of every block.
All inputs are finite; a program needn't handle non-finite values.
Results may differ from a plain program's by a relative error of at most 0.011.
Values may be sent and summed in bfloat16 or wider, within the bound.
No kernel may reach another device: no remote copies, remote signals or barrier semaphores. Data moves between devices by JAX's collectives and lax.ppermute only.
A program may use at most 128 MiB of HBM per device.

v0:
```python
import jax
import jax.numpy as jnp
from jax import lax
from jax.sharding import Mesh
from jax.sharding import PartitionSpec as P


CAP = 8
BF = jnp.bfloat16
F32 = jnp.float32


def dot(a, b, ca, cb):
    return lax.dot_general(a, b, (((ca,), (cb,)), ((), ())), preferred_element_type=F32)


def slot_tables(routes_t, combine_t, labels):
    tokens = routes_t.shape[1]
    experts = labels.shape[0]
    hits = routes_t[None, :, :] == labels[:, None, None]
    chosen = jnp.sum(hits.astype(F32), axis=1)
    scale = jnp.sum(jnp.where(hits, combine_t[None, :, :], 0.0), axis=1)
    ids = jnp.arange(tokens, dtype=jnp.int32)
    earlier = (ids[:, None] < ids[None, :]).astype(BF)
    before = jnp.dot(chosen.astype(BF), earlier, preferred_element_type=F32)
    slots = jnp.arange(CAP, dtype=F32)
    taken = (before[:, None, :] == slots[None, :, None]) & (chosen[:, None, :] > 0)
    factor = jnp.sum(jnp.where(taken, scale[:, None, :], 0.0), axis=2)
    return taken.astype(BF).reshape(experts * CAP, tokens), factor.reshape(experts * CAP, 1)


def pick(picker, x):
    return jnp.dot(picker, x, preferred_element_type=F32).astype(BF)


def pick_scaled(picker, x, factor):
    return (jnp.dot(picker, x, preferred_element_type=F32) * factor).astype(BF)


def swap(x, axis):
    return lax.ppermute(x, axis, [(0, 1), (1, 0)])


def both_halves(mine, axis):
    other = swap(mine, "dp")
    first = lax.axis_index("dp") == 0
    return jnp.concatenate(
        [jnp.where(first, mine, other), jnp.where(first, other, mine)], axis=axis
    )


def cross_quarter(x, part):
    t = lax.axis_index("tensor")
    n = lax.axis_size("tensor")
    last = n - 1

    def piece(low, high):
        at = jnp.where(t == last, low, high) * part
        return lax.dynamic_slice_in_dim(x, at, part, axis=1)

    out = None
    for k in range(n // 2):
        perm = []
        for z in range(2):
            perm.append((z * n + last, (1 - z) * n + k))
            perm.append((z * n, (1 - z) * n + last - k))
        got = lax.ppermute(piece(k, last - k), ("zh", "tensor"), perm)
        out = got if out is None else out + got
    return out


def gather_quarters(q):
    n = lax.axis_size("tensor")
    tokens, part = q.shape
    full = lax.all_gather(q, "tensor", axis=0, tiled=False)
    return jnp.transpose(full, (1, 0, 2)).reshape(tokens, n * part)


def gradients_of_units(in_rows, grad_rows, gate_full, up_full, down_full):
    gate = dot(in_rows, gate_full, 1, 0)
    up = dot(in_rows, up_full, 1, 0)
    dhid = dot(grad_rows, down_full, 1, 1)
    sigma = jax.nn.sigmoid(gate)
    silu_gate = gate * sigma
    act = (silu_gate * up).astype(BF)
    d_up = (dhid * silu_gate).astype(BF)
    d_gate = (dhid * up * sigma * (1.0 + gate * (1.0 - sigma))).astype(BF)
    return act, d_gate, d_up


def reduced_rows(d_gate, d_up, gate_full, up_full, part):
    n = lax.axis_size("tensor")
    t = lax.axis_index("tensor")

    def row_part(index):
        g = lax.dynamic_slice_in_dim(gate_full, index * part, part, axis=0)
        u = lax.dynamic_slice_in_dim(up_full, index * part, part, axis=0)
        return dot(d_gate, g, 1, 1) + dot(d_up, u, 1, 1)

    received = []
    for step in (2, 1, 3):
        piece = row_part((t + step) % n).astype(BF)
        received.append(lax.ppermute(piece, "tensor", [(i, (i + step) % n) for i in range(n)]))
    total = row_part(t)
    for piece in received:
        total = total + piece.astype(F32)
    return total.astype(BF)


def exchange(x):
    return lax.all_to_all(x, "col", split_axis=0, concat_axis=0, tiled=True)


def inner(grad_out, layer_in, routes, combine, gate_weight, up_weight, down_weight):
    cols = lax.axis_size("col")
    n_tensor = lax.axis_size("tensor")
    _, width = grad_out.shape
    rows = cols * CAP
    half = width // 2
    part = width // n_tensor
    my_dp = lax.axis_index("dp")
    my_zh = lax.axis_index("zh")

    routes_t, combine_t = routes.T, combine.T
    far_routes, far_combine = swap(routes_t, "zh"), swap(combine_t, "zh")
    far_in_q = cross_quarter(layer_in, part)
    far_grad_q = cross_quarter(grad_out, part)

    gate_full = both_halves(gate_weight[0], 0)
    up_full = both_halves(up_weight[0], 0)
    down_full = both_halves(down_weight[0], 1)

    labels = my_zh * cols + jnp.arange(cols, dtype=jnp.int32)
    picker, factor = slot_tables(routes_t, combine_t, labels)
    sent = jnp.concatenate(
        [
            pick(picker, layer_in).reshape(cols, CAP, width),
            pick_scaled(picker, grad_out, factor).reshape(cols, CAP, width),
        ],
        axis=1,
    )
    got = exchange(sent)
    in_rows = got[:, :CAP].reshape(rows, width)
    grad_rows = got[:, CAP:].reshape(rows, width)

    far_picker, far_factor = slot_tables(far_routes, far_combine, labels)
    far_in = pick(far_picker, gather_quarters(far_in_q))
    far_grad = pick_scaled(far_picker, gather_quarters(far_grad_q), far_factor)
    far_sent = [x.reshape(cols, CAP, width) for x in (far_in, far_grad)]
    far_got = exchange(jnp.concatenate(far_sent, axis=1))
    far_in = far_got[:, :CAP].reshape(rows, width)
    far_grad = far_got[:, CAP:].reshape(rows, width)

    act, d_gate, d_up = gradients_of_units(in_rows, grad_rows, gate_full, up_full, down_full)
    near_rows = reduced_rows(d_gate, d_up, gate_full, up_full, part)
    near_back = exchange(near_rows.reshape(cols, CAP, part)).reshape(rows, part)
    near_sum = dot(picker, near_back, 0, 0)

    far_act, far_d_gate, far_d_up = gradients_of_units(
        far_in, far_grad, gate_full, up_full, down_full
    )
    far_rows = reduced_rows(far_d_gate, far_d_up, gate_full, up_full, part)
    far_back = exchange(far_rows.reshape(cols, CAP, part)).reshape(rows, part)
    far_sum = dot(far_picker, far_back, 0, 0).astype(BF)
    total = (near_sum + swap(far_sum, "zh").astype(F32)).astype(BF)

    mine_at = my_dp * half
    other_at = (1 - my_dp) * half

    def columns(x, at):
        return lax.dynamic_slice_in_dim(x, at, half, axis=1)

    def finish(a, b, cut):
        a = jnp.concatenate(a, axis=0)
        b = jnp.concatenate(b, axis=0)

        def term(at):
            left, right = (columns(a, at), b) if cut == 0 else (a, columns(b, at))
            return (dot(left, right, 0, 0) * 0.25).astype(BF)

        got_term = swap(term(other_at), "dp")
        return (term(mine_at).astype(F32) + got_term.astype(F32)).astype(BF)

    grad_gate = finish((in_rows, far_in), (d_gate, far_d_gate), 0)
    grad_up = finish((in_rows, far_in), (d_up, far_d_up), 0)
    grad_down = finish((act, far_act), (grad_rows, far_grad), 1)
    total, grad_gate, grad_up, grad_down = lax.optimization_barrier(
        (total, grad_gate, grad_up, grad_down)
    )
    total = gather_quarters(total)
    return total, grad_gate[None], grad_up[None], grad_down[None]


def solution(mesh):
    n_dp, n_expert, n_tensor = (mesh.shape[a] for a in ("dp", "expert", "tensor"))
    split = Mesh(
        mesh.devices.reshape(n_dp, 2, n_expert // 2, n_tensor), ("dp", "zh", "col", "tensor")
    )
    blocks = P(("dp", "zh", "col"), None)
    by_rows = P(("zh", "col"), "dp", "tensor")
    by_columns = P(("zh", "col"), "tensor", "dp")
    return jax.shard_map(
        inner,
        mesh=split,
        in_specs=(blocks, blocks, blocks, blocks, by_rows, by_rows, by_columns),
        out_specs=(blocks, by_rows, by_rows, by_columns),
        check_vma=False,
    )
```

profile of v0, /device:TPU:1, one launch (start us, length us, event | category | flops | bytes accessed | tf_op | source)
XLA Modules:
  0.0 219.4 jit_solution(14501200235609443897)
XLA Ops:
  0.7 7.8 %collective-permute-start.6 = (s32[8,128]{1,0:T(8,128)}, s32[8,128]{1,0:T(8,128)S(1)}, u32[]{:S(2)}, u32[]{:S(2)}) collective-permute-start(s32[8,128]{1,0:T(8,128)} %bitcast.115), channel_id=1, source_target_pairs={{0,64},{64,0},{1,65},{65,1},{2,66},{66,2},{3,67},{67,3},{4,68},{68... | collective-permute-start | bytes 12296 | tf_op jit(solution)/shard_map/ppermute | solution.py:41
  8.6 1.2 constant_dynamic-slice_fusion
  9.8 6.3 %collective-permute-start.10 = (bf16[128,896]{1,0:T(8,128)(2,1)S(1)}, bf16[128,896]{1,0:T(8,128)(2,1)S(1)}, u32[]{:S(2)}, u32[]{:S(2)}) collective-permute-start(bf16[128,896]{1,0:T(8,128)(2,1)S(1)} %get-tuple-element.30), channel_id=1, source_target_pairs={{3,65},{0,66},{67,1},{64,2},{7,69},{4,70},{71,5},{68,6},{11,73},{8... | collective-permute-start | bytes 688136 | tf_op jit(solution)/shard_map/ppermute | solution.py:67
  16.1 1.9 collective-permute-start.9
  18.0 1.1 constant_dynamic-slice_fusion.2
  19.1 1.3 collective-permute-start.8
  20.6 4.6 %collective-permute-start.7 = (bf16[128,896]{1,0:T(8,128)(2,1)S(1)}, bf16[128,896]{1,0:T(8,128)(2,1)}, u32[]{:S(2)}, u32[]{:S(2)}) collective-permute-start(bf16[128,896]{1,0:T(8,128)(2,1)S(1)} %get-tuple-element.29), channel_id=1, source_target_pairs={{3,64},{0,67},{67,0},{64,3},{7,68},{4,71},{71,4},{68,7},{11,72},{8... | collective-permute-start | bytes 688136 | tf_op jit(solution)/shard_map/ppermute | solution.py:67
  25.9 0.4 fusion.4
  26.3 0.4 fusion.7
  26.8 1.5 pad_maximum_fusion.2
  28.3 2.2 collective-permute-start
  30.7 6.8 %all-to-all-start = ((bf16[16,16,3584]{2,1,0:T(8,128)(2,1)}), bf16[16,16,3584]{2,1,0:T(8,128)(2,1)}, u32[]{:S(2)}, u32[]{:S(2)}) async-start(bf16[16,16,3584]{2,1,0:T(8,128)(2,1)} %pad_maximum_fusion.2), calls=%async_computation | async-start | bytes 3670016 | tf_op jit(solution)/shard_map/all_to_all | solution.py:111
  38.1 1.0 add.172
  39.1 18.6 %all-gather = bf16[512,896]{1,0:T(8,128)(2,1)S(1)} all-gather(bf16[128,896]{1,0:T(8,128)(2,1)S(1)} %add.172), channel_id=2, replica_groups=mesh['dp'=2,'zh'=2,'col'=16,'tensor'=4] {'tensor'}, dimensions={0}, use_global_device_ids=true | all-gather | bytes 1146880 | tf_op jit(solution)/shard_map/all_gather | solution.py:75
  57.8 17.6 %all-gather.1 = bf16[512,896]{1,0:T(8,128)(2,1)S(1)} all-gather(bf16[128,896]{1,0:T(8,128)(2,1)S(1)} %add.173), channel_id=3, replica_groups=mesh['dp'=2,'zh'=2,'col'=16,'tensor'=4] {'tensor'}, dimensions={0}, use_global_device_ids=true | all-gather | bytes 1146880 | tf_op jit(solution)/shard_map/all_gather | solution.py:75
  75.4 0.6 copy.19
  76.0 0.6 copy.20
  77.0 0.4 fusion.6
  77.5 1.4 pad_maximum_fusion.4
  78.9 1.6 broadcast_select_fusion.2
  80.5 6.1 %fusion.55 = (bf16[896,256]{1,0:T(8,128)(2,1)}, bf16[896,256]{1,0:T(8,128)(2,1)S(1)}, bf16[896,256]{1,0:T(8,128)(2,1)S(1)}, bf16[896,256]{1,0:T(8,128)(2,1)S(1)}) fusion(s32[]{:T(128)S(6)} %select_n.130, bf16[1792,256]{1,0:T(8,128)(2,1)S(1)} %get-tuple-element.23, bf16[1792,256]{1,0:T(8,128)(2,1)S(1)} %get-tuple-element.22, s32[]{:T(128)S(6)} %select_n.128, ...), kind=kLoop, calls=%fused_computation.113 | loop fusion | flops 3670016 | bytes 3670032 | tf_op jit(solution)/shard_map/concatenate | solution.py:47
  86.6 2.8 %broadcast_select_fusion.5 = (bf16[256,1792]{1,0:T(8,128)(2,1)}, bf16[256,1792]{1,0:T(8,128)(2,1)}) fusion(bf16[256,1792]{1,0:T(8,128)(2,1)} %collective-permute-done, pred[]{:T(512)S(6)} %eq.102, bf16[1,256,1792]{2,1,0:T(8,128)(2,1)} %param.13), kind=kLoop, calls=%fused_computation.107 | loop fusion | flops 917504 | bytes 3670017 | tf_op jit(solution)/shard_map/jit(_where)/select_n | solution.py:48
  89.4 1.6 broadcast_select_fusion.1
  91.0 6.7 %all-to-all-start.2 = ((bf16[16,16,3584]{2,1,0:T(8,128)(2,1)}), bf16[16,16,3584]{2,1,0:T(8,128)(2,1)}, u32[]{:S(2)}, u32[]{:S(2)}) async-start(bf16[16,16,3584]{2,1,0:T(8,128)(2,1)} %pad_maximum_fusion.4), calls=%async_computation.2 | async-start | bytes 3670016 | tf_op jit(solution)/shard_map/all_to_all | solution.py:111
  97.7 2.4 %fusion.33 = f32[128,256]{1,0:T(8,128)S(1)} fusion(bf16[256,1792]{1,0:T(8,128)(2,1)} %get-tuple-element.27, bf16[256,1792]{1,0:T(8,128)(2,1)} %get-tuple-element.26, bf16[16,16,3584]{2,1,0:T(8,128)(2,1)} %all-to-all-done), kind=kOutput, calls=%fused_computation.85 | convolution fusion | flops 238551040 | bytes 2883584 | tf_op jit(solution)/shard_map/dot_general | solution.py:14
  100.1 1.7 fusion.35
  101.9 2.3 %multiply_convert_fusion.1 = (bf16[128,256]{1,0:T(8,128)(2,1)}, bf16[128,256]{1,0:T(8,128)(2,1)S(1)}, bf16[128,256]{1,0:T(8,128)(2,1)S(1)}) fusion(f32[128,256]{1,0:T(8,128)S(1)} %fusion.35, f32[128,256]{1,0:T(8,128)S(1)} %fusion.33, bf16[1792,256]{1,0:T(8,128)(2,1)S(1)} %copy-done.3, bf16[1792,256]{1,0:T(8,128)(2,1)S(1)} %copy-done.6, ...), kind=kOutput, calls=%fused_computation.121 | convolution fusion | flops 239042560 | bytes 3211264 | tf_op jit(solution)/shard_map/dot_general | solution.py:14
  104.5 1.7 fusion.26
  106.1 0.9 collective-permute-start.3
  107.3 1.7 fusion.27
  109.0 2.2 collective-permute-start.4
  111.5 1.7 fusion.28
  113.1 1.1 fusion.134
  114.2 2.8 %slice_bitcast_fusion.3 = (bf16[128,3584]{1,0:T(8,128)(2,1)}, bf16[128,3584]{1,0:T(8,128)(2,1)}) fusion(bf16[16,16,3584]{2,1,0:T(8,128)(2,1)} %all-to-all-done), kind=kLoop, calls=%fused_computation.101 | loop fusion | bytes 3670016 | tf_op jit(solution)/shard_map/reshape | solution.py:144
  117.0 2.5 %all-to-all-done.2 = bf16[16,16,3584]{2,1,0:T(8,128)(2,1)} async-done(((bf16[16,16,3584]{2,1,0:T(8,128)(2,1)}), bf16[16,16,3584]{2,1,0:T(8,128)(2,1)}, u32[]{:S(2)}, u32[]{:S(2)}) %all-to-all-start.2) | async-done | bytes 1835040 | tf_op jit(solution)/shard_map/all_to_all | solution.py:111
  119.5 2.4 %fusion.32 = f32[128,256]{1,0:T(8,128)S(1)} fusion(bf16[256,1792]{1,0:T(8,128)(2,1)} %get-tuple-element.27, bf16[256,1792]{1,0:T(8,128)(2,1)} %get-tuple-element.26, bf16[16,16,3584]{2,1,0:T(8,128)(2,1)} %all-to-all-done.2), kind=kOutput, calls=%fused_computation.84 | convolution fusion | flops 238551040 | bytes 2883584 | tf_op jit(solution)/shard_map/dot_general | solution.py:14
  122.0 1.7 fusion.34
  123.7 2.3 %multiply_convert_fusion = (bf16[128,256]{1,0:T(8,128)(2,1)}, bf16[128,256]{1,0:T(8,128)(2,1)S(1)}, bf16[128,256]{1,0:T(8,128)(2,1)S(1)}) fusion(f32[128,256]{1,0:T(8,128)S(1)} %fusion.34, f32[128,256]{1,0:T(8,128)S(1)} %fusion.32, bf16[1792,256]{1,0:T(8,128)(2,1)S(1)} %copy-done.4, bf16[1792,256]{1,0:T(8,128)(2,1)S(1)} %copy-done.7, ...), kind=kOutput, calls=%fused_computation.120 | convolution fusion | flops 239042560 | bytes 3211264 | tf_op jit(solution)/shard_map/dot_general | solution.py:14
  126.9 1.0 fusion.29
  127.8 1.2 collective-permute-start.12
  129.0 0.9 fusion.30
  130.0 3.0 %collective-permute-start.13 = (bf16[128,896]{1,0:T(8,128)(2,1)S(1)}, bf16[128,896]{1,0:T(8,128)(2,1)S(1)}, u32[]{:S(2)}, u32[]{:S(2)}) collective-permute-start(bf16[128,896]{1,0:T(8,128)(2,1)S(1)} %fusion.30), channel_id=1, source_target_pairs={{0,1},{1,2},{2,3},{3,0},{4,5},{5,6},{6,7},{7,4},{8,9},{9,10},{10,1... | collective-permute-start | bytes 688136 | tf_op jit(solution)/shard_map/ppermute | solution.py:103
  133.0 0.9 fusion.31
  134.4 2.5 %slice_bitcast_fusion.1 = (bf16[128,3584]{1,0:T(8,128)(2,1)}, bf16[128,3584]{1,0:T(8,128)(2,1)S(1)}) fusion(bf16[16,16,3584]{2,1,0:T(8,128)(2,1)} %all-to-all-done.2), kind=kLoop, calls=%fused_computation.99 | loop fusion | bytes 3670016 | tf_op jit(solution)/shard_map/reshape | solution.py:152
  136.9 1.4 fusion.10
  138.5 2.5 %collective-permute-done.12 = bf16[128,896]{1,0:T(8,128)(2,1)S(1)} collective-permute-done((bf16[128,896]{1,0:T(8,128)(2,1)S(1)}, bf16[128,896]{1,0:T(8,128)(2,1)S(1)}, u32[]{:S(2)}, u32[]{:S(2)}) %collective-permute-start.12) | collective-permute-done | bytes 229408 | tf_op jit(solution)/shard_map/ppermute | solution.py:103
  141.0 1.2 collective-permute-done.14
  142.3 1.7 fusion.38
  144.0 13.2 %all-to-all-start.3 = ((bf16[16,8,896]{2,1,0:T(8,128)(2,1)}), bf16[16,8,896]{2,1,0:T(8,128)(2,1)}, u32[]{:S(2)}, u32[]{:S(2)}) async-start(bf16[16,8,896]{2,1,0:T(8,128)(2,1)} %fusion.38), calls=%async_computation.3 | async-start | bytes 458752 | tf_op jit(solution)/shard_map/all_to_all | solution.py:111
  157.2 2.5 %fusion.13 = bf16[1792,256]{1,0:T(8,128)(2,1)} fusion(bf16[128,256]{1,0:T(8,128)(2,1)S(1)} %get-tuple-element.37, bf16[128,256]{1,0:T(8,128)(2,1)S(1)} %get-tuple-element.34, s32[]{:T(128)S(6)} %select_n.142, bf16[128,3584]{1,0:T(8,128)(2,1)S(1)} %copy-done.12, bf16[128,3584]{1,0:T(8,128)(2,1)} %copy-done.15), kind=kOutput, calls=%fused_computation.41 | convolution fusion | flops 237895680 | bytes 2883588 | tf_op jit(solution)/shard_map/dot_general | solution.py:14
  159.7 2.8 %collective-permute-start.17 = (bf16[1792,256]{1,0:T(8,128)(2,1)}, bf16[1792,256]{1,0:T(8,128)(2,1)}, u32[]{:S(2)}, u32[]{:S(2)}) collective-permute-start(bf16[1792,256]{1,0:T(8,128)(2,1)} %fusion.13), channel_id=1, source_target_pairs={{0,128},{128,0},{1,129},{129,1},{2,130},{130,2},{3,131},{131,3},{4... | collective-permute-start | bytes 2752520 | tf_op jit(solution)/shard_map/ppermute | solution.py:41
  162.5 2.8 %fusion.39 = bf16[16,8,896]{2,1,0:T(8,128)(2,1)} fusion(f32[128,896]{1,0:T(8,128)S(1)} %copy-done.10, bf16[128,256]{1,0:T(8,128)(2,1)S(1)} %get-tuple-element.33, bf16[128,896]{1,0:T(8,128)(2,1)} %collective-permute-done.5, bf16[128,896]{1,0:T(8,128)(2,1)} %collective-permute-done.4, bf16[128,896]{1,0:T(8,128)(2,1)} %collective-permute-done.3, ...), kind=kOutput, calls=%fused_computation.91 | convolution fusion | flops 60555264 | bytes 3276804 | tf_op jit(solution)/shard_map/dot_general | solution.py:14
  165.3 6.9 %all-to-all-start.1 = ((bf16[16,8,896]{2,1,0:T(8,128)(2,1)}), bf16[16,8,896]{2,1,0:T(8,128)(2,1)S(1)}, u32[]{:S(2)}, u32[]{:S(2)}) async-start(bf16[16,8,896]{2,1,0:T(8,128)(2,1)} %fusion.39), calls=%async_computation.1 | async-start | bytes 458752 | tf_op jit(solution)/shard_map/all_to_all | solution.py:111
  172.2 1.2 fusion.25
  173.4 4.6 %collective-permute-start.15 = (bf16[128,896]{1,0:T(8,128)(2,1)S(1)}, bf16[128,896]{1,0:T(8,128)(2,1)}, u32[]{:S(2)}, u32[]{:S(2)}) collective-permute-start(bf16[128,896]{1,0:T(8,128)(2,1)S(1)} %fusion.25), channel_id=1, source_target_pairs={{0,64},{64,0},{1,65},{65,1},{2,66},{66,2},{3,67},{67,3},{4,68},{68... | collective-permute-start | bytes 688136 | tf_op jit(solution)/shard_map/ppermute | solution.py:41
  178.0 2.6 %fusion.16 = bf16[256,1792]{1,0:T(8,128)(2,1)} fusion(s32[]{:T(128)S(6)} %select_n.142, bf16[128,3584]{1,0:T(8,128)(2,1)S(1)} %copy-done.11, bf16[128,3584]{1,0:T(8,128)(2,1)} %get-tuple-element.14, bf16[128,256]{1,0:T(8,128)(2,1)} %get-tuple-element.35, bf16[128,256]{1,0:T(8,128)(2,1)} %get-tuple-element.32), kind=kOutput, calls=%fused_computation.44 | convolution fusion | flops 237895680 | bytes 2883588 | tf_op jit(solution)/shard_map/dot_general | solution.py:14
  180.7 1.1 collective-permute-start.18
  181.7 2.2 %collective-permute-done.15 = bf16[128,896]{1,0:T(8,128)(2,1)} collective-permute-done((bf16[128,896]{1,0:T(8,128)(2,1)S(1)}, bf16[128,896]{1,0:T(8,128)(2,1)}, u32[]{:S(2)}, u32[]{:S(2)}) %collective-permute-start.15) | collective-permute-done | bytes 229408 | tf_op jit(solution)/shard_map/ppermute | solution.py:41
  183.9 1.2 add_convert_fusion.3
  185.2 2.6 %add_convert_fusion.1 = bf16[1792,256]{1,0:T(8,128)(2,1)} fusion(bf16[1792,256]{1,0:T(8,128)(2,1)} %collective-permute-done.17, bf16[128,256]{1,0:T(8,128)(2,1)S(1)} %get-tuple-element.37, bf16[128,256]{1,0:T(8,128)(2,1)S(1)} %get-tuple-element.34, s32[]{:T(128)S(6)} %select_n.141, bf16[128,3584]{1,0:T(8,128)(2,1)S(1)} %copy-done.13, ...), kind=kOutput, calls=%fused_computation.57 | convolution fusion | flops 239730688 | bytes 3801092 | tf_op jit(solution)/shard_map/dot_general | solution.py:14
  187.8 2.7 %add_convert_fusion.2 = bf16[1792,256]{1,0:T(8,128)(2,1)} fusion(bf16[1792,256]{1,0:T(8,128)(2,1)} %collective-permute-done.16, bf16[128,256]{1,0:T(8,128)(2,1)S(1)} %get-tuple-element.36, bf16[128,256]{1,0:T(8,128)(2,1)S(1)} %get-tuple-element.33, s32[]{:T(128)S(6)} %select_n.141, bf16[128,3584]{1,0:T(8,128)(2,1)S(1)} %copy-done.13, ...), kind=kOutput, calls=%fused_computation.58 | convolution fusion | flops 239730688 | bytes 3801092 | tf_op jit(solution)/shard_map/dot_general | solution.py:14
  190.5 2.6 %add_convert_fusion = bf16[256,1792]{1,0:T(8,128)(2,1)} fusion(bf16[256,1792]{1,0:T(8,128)(2,1)} %collective-permute-done.18, s32[]{:T(128)S(6)} %select_n.141, bf16[128,3584]{1,0:T(8,128)(2,1)S(1)} %copy-done.11, bf16[128,3584]{1,0:T(8,128)(2,1)S(1)} %copy-done.14, bf16[128,256]{1,0:T(8,128)(2,1)S(1)} %copy-done.21, bf16[128,256]{1,0:T(8,128)(2,1)S(1)} %copy-done.20), kind=kOutput, calls=%fused_computation.56 | convolution fusion | flops 239730688 | bytes 3801092 | tf_op jit(solution)/shard_map/dot_general | solution.py:14
  193.1 25.3 %all-gather.2 = bf16[512,896]{1,0:T(8,128)(2,1)S(1)} all-gather(bf16[128,896]{1,0:T(8,128)(2,1)S(1)} %add_convert_fusion.3), channel_id=4, replica_groups=mesh['dp'=2,'zh'=2,'col'=16,'tensor'=4] {'tensor'}, dimensions={0}, use_global_device_ids=true | all-gather | bytes 1146880 | tf_op jit(solution)/shard_map/all_gather | solution.py:75
  218.4 1.0 copy.22
  (90 shorter events, 4.7 us)
Async XLA Ops:
  0.6 24.5 %copy-start.18 = (s32[128,8]{0,1:T(8,128)S(1)}, s32[128,8]{0,1:T(8,128)}, u32[]{:S(2)}) copy-start(s32[128,8]{0,1:T(8,128)} %param.9) | copy-start | bytes 12292
  0.6 24.9 %copy-start.19 = (f32[128,8]{0,1:T(8,128)S(1)}, f32[128,8]{0,1:T(8,128)}, u32[]{:S(2)}) copy-start(f32[128,8]{0,1:T(8,128)} %param.10) | copy-start | bytes 12292
  0.7 25.2 %copy-start.8 = (bf16[128,3584]{1,0:T(8,128)(2,1)S(1)}, bf16[128,3584]{1,0:T(8,128)(2,1)}, u32[]{:S(2)}) copy-start(bf16[128,3584]{1,0:T(8,128)(2,1)} %param.8) | copy-start | bytes 2752516
  0.7 19.9 %collective-permute-start.6 = (s32[8,128]{1,0:T(8,128)}, s32[8,128]{1,0:T(8,128)S(1)}, u32[]{:S(2)}, u32[]{:S(2)}) collective-permute-start(s32[8,128]{1,0:T(8,128)} %bitcast.115), channel_id=1, source_target_pairs={{0,64},{64,0},{1,65},{65,1},{2,66},{66,2},{3,67},{67,3},{4,68},{68... | collective-permute-start | bytes 12296 | tf_op jit(solution)/shard_map/ppermute | solution.py:41
  8.5 19.8 %collective-permute-start.11 = (f32[8,128]{1,0:T(8,128)}, f32[8,128]{1,0:T(8,128)S(1)}, u32[]{:S(2)}, u32[]{:S(2)}) collective-permute-start(f32[8,128]{1,0:T(8,128)} %bitcast.118), channel_id=1, source_target_pairs={{0,64},{64,0},{1,65},{65,1},{2,66},{66,2},{3,67},{67,3},{4,68},{68... | collective-permute-start | bytes 12296 | tf_op jit(solution)/shard_map/ppermute | solution.py:41
  8.6 17.8 %copy-start.9 = (bf16[128,3584]{1,0:T(8,128)(2,1)S(1)}, bf16[128,3584]{1,0:T(8,128)(2,1)}, u32[]{:S(2)}) copy-start(bf16[128,3584]{1,0:T(8,128)(2,1)} %param.7) | copy-start | bytes 2752516
  9.8 48.0 %collective-permute-start.10 = (bf16[128,896]{1,0:T(8,128)(2,1)S(1)}, bf16[128,896]{1,0:T(8,128)(2,1)S(1)}, u32[]{:S(2)}, u32[]{:S(2)}) collective-permute-start(bf16[128,896]{1,0:T(8,128)(2,1)S(1)} %get-tuple-element.30), channel_id=1, source_target_pairs={{3,65},{0,66},{67,1},{64,2},{7,69},{4,70},{71,5},{68,6},{11,73},{8... | collective-permute-start | bytes 688136 | tf_op jit(solution)/shard_map/ppermute | solution.py:67
  16.1 41.7 %collective-permute-start.9 = (bf16[128,896]{1,0:T(8,128)(2,1)S(1)}, bf16[128,896]{1,0:T(8,128)(2,1)S(1)}, u32[]{:S(2)}, u32[]{:S(2)}) collective-permute-start(bf16[128,896]{1,0:T(8,128)(2,1)S(1)} %get-tuple-element.31), channel_id=1, source_target_pairs={{3,64},{0,67},{67,0},{64,3},{7,68},{4,71},{71,4},{68,7},{11,72},{8... | collective-permute-start | bytes 688136 | tf_op jit(solution)/shard_map/ppermute | solution.py:67
  19.1 18.4 %collective-permute-start.8 = (bf16[128,896]{1,0:T(8,128)(2,1)S(1)}, bf16[128,896]{1,0:T(8,128)(2,1)S(1)}, u32[]{:S(2)}, u32[]{:S(2)}) collective-permute-start(bf16[128,896]{1,0:T(8,128)(2,1)S(1)} %get-tuple-element.28), channel_id=1, source_target_pairs={{3,65},{0,66},{67,1},{64,2},{7,69},{4,70},{71,5},{68,6},{11,73},{8... | collective-permute-start | bytes 688136 | tf_op jit(solution)/shard_map/ppermute | solution.py:67
  20.6 17.3 %collective-permute-start.7 = (bf16[128,896]{1,0:T(8,128)(2,1)S(1)}, bf16[128,896]{1,0:T(8,128)(2,1)}, u32[]{:S(2)}, u32[]{:S(2)}) collective-permute-start(bf16[128,896]{1,0:T(8,128)(2,1)S(1)} %get-tuple-element.29), channel_id=1, source_target_pairs={{3,64},{0,67},{67,0},{64,3},{7,68},{4,71},{71,4},{68,7},{11,72},{8... | collective-permute-start | bytes 688136 | tf_op jit(solution)/shard_map/ppermute | solution.py:67
  28.3 58.3 %collective-permute-start = (bf16[256,1792]{1,0:T(8,128)(2,1)}, bf16[256,1792]{1,0:T(8,128)(2,1)}, u32[]{:S(2)}, u32[]{:S(2)}) collective-permute-start(bf16[256,1792]{1,0:T(8,128)(2,1)} %bitcast.7), channel_id=1, source_target_pairs={{0,128},{128,0},{1,129},{129,1},{2,130},{130,2},{3,131},{131,3},{4... | collective-permute-start | bytes 2752520 | tf_op jit(solution)/shard_map/ppermute | solution.py:41
  30.7 60.3 %all-to-all-start = ((bf16[16,16,3584]{2,1,0:T(8,128)(2,1)}), bf16[16,16,3584]{2,1,0:T(8,128)(2,1)}, u32[]{:S(2)}, u32[]{:S(2)}) async-start(bf16[16,16,3584]{2,1,0:T(8,128)(2,1)} %pad_maximum_fusion.2), calls=%async_computation | async-start | bytes 3670016 | tf_op jit(solution)/shard_map/all_to_all | solution.py:111
  37.5 41.4 %collective-permute-start.1 = (bf16[1792,256]{1,0:T(8,128)(2,1)}, bf16[1792,256]{1,0:T(8,128)(2,1)}, u32[]{:S(2)}, u32[]{:S(2)}) collective-permute-start(bf16[1792,256]{1,0:T(8,128)(2,1)} %bitcast.9), channel_id=1, source_target_pairs={{0,128},{128,0},{1,129},{129,1},{2,130},{130,2},{3,131},{131,3},{4... | collective-permute-start | bytes 2752520 | tf_op jit(solution)/shard_map/ppermute | solution.py:41
  37.9 51.5 %collective-permute-start.2 = (bf16[1792,256]{1,0:T(8,128)(2,1)}, bf16[1792,256]{1,0:T(8,128)(2,1)}, u32[]{:S(2)}, u32[]{:S(2)}) collective-permute-start(bf16[1792,256]{1,0:T(8,128)(2,1)} %bitcast.10), channel_id=1, source_target_pairs={{0,128},{128,0},{1,129},{129,1},{2,130},{130,2},{3,131},{131,3},{4... | collective-permute-start | bytes 2752520 | tf_op jit(solution)/shard_map/ppermute | solution.py:41
  80.5 6.1 %copy-start.2 = (bf16[1792,256]{1,0:T(8,128)(2,1)}, bf16[1792,256]{1,0:T(8,128)(2,1)S(1)}, u32[]{:S(2)}) copy-start(bf16[1792,256]{1,0:T(8,128)(2,1)S(1)} %get-tuple-element.22) | copy-start | bytes 2752516
  80.5 6.1 %copy-start.5 = (bf16[1792,256]{1,0:T(8,128)(2,1)}, bf16[1792,256]{1,0:T(8,128)(2,1)S(1)}, u32[]{:S(2)}) copy-start(bf16[1792,256]{1,0:T(8,128)(2,1)S(1)} %get-tuple-element.23) | copy-start | bytes 2752516
  91.0 28.5 %all-to-all-start.2 = ((bf16[16,16,3584]{2,1,0:T(8,128)(2,1)}), bf16[16,16,3584]{2,1,0:T(8,128)(2,1)}, u32[]{:S(2)}, u32[]{:S(2)}) async-start(bf16[16,16,3584]{2,1,0:T(8,128)(2,1)} %pad_maximum_fusion.4), calls=%async_computation.2 | async-start | bytes 3670016 | tf_op jit(solution)/shard_map/all_to_all | solution.py:111
  100.1 1.8 copy-start.3
  100.1 1.8 copy-start.6
  101.9 2.3 %copy-start = (bf16[896,256]{1,0:T(8,128)(2,1)S(1)}, bf16[896,256]{1,0:T(8,128)(2,1)}, u32[]{:S(2)}) copy-start(bf16[896,256]{1,0:T(8,128)(2,1)} %get-tuple-element.18) | copy-start | bytes 1376260
  106.1 56.3 %collective-permute-start.3 = (bf16[128,896]{1,0:T(8,128)(2,1)}, bf16[128,896]{1,0:T(8,128)(2,1)}, u32[]{:S(2)}, u32[]{:S(2)}) collective-permute-start(bf16[128,896]{1,0:T(8,128)(2,1)} %fusion.26), channel_id=1, source_target_pairs={{0,2},{1,3},{2,0},{3,1},{4,6},{5,7},{6,4},{7,5},{8,10},{9,11},{10,... | collective-permute-start | bytes 688136 | tf_op jit(solution)/shard_map/ppermute | solution.py:103
  109.0 53.5 %collective-permute-start.4 = (bf16[128,896]{1,0:T(8,128)(2,1)}, bf16[128,896]{1,0:T(8,128)(2,1)}, u32[]{:S(2)}, u32[]{:S(2)}) collective-permute-start(bf16[128,896]{1,0:T(8,128)(2,1)} %fusion.27), channel_id=1, source_target_pairs={{0,1},{1,2},{2,3},{3,0},{4,5},{5,6},{6,7},{7,4},{8,9},{9,10},{10,1... | collective-permute-start | bytes 688136 | tf_op jit(solution)/shard_map/ppermute | solution.py:103
  121.9 1.8 copy-start.4
  121.9 1.7 copy-start.7
  123.7 2.3 %copy-start.1 = (bf16[896,256]{1,0:T(8,128)(2,1)S(1)}, bf16[896,256]{1,0:T(8,128)(2,1)}, u32[]{:S(2)}) copy-start(bf16[896,256]{1,0:T(8,128)(2,1)} %get-tuple-element.18) | copy-start | bytes 1376260
  127.8 13.2 %collective-permute-start.12 = (bf16[128,896]{1,0:T(8,128)(2,1)S(1)}, bf16[128,896]{1,0:T(8,128)(2,1)S(1)}, u32[]{:S(2)}, u32[]{:S(2)}) collective-permute-start(bf16[128,896]{1,0:T(8,128)(2,1)S(1)} %fusion.29), channel_id=1, source_target_pairs={{0,2},{1,3},{2,0},{3,1},{4,6},{5,7},{6,4},{7,5},{8,10},{9,11},{10,... | collective-permute-start | bytes 688136 | tf_op jit(solution)/shard_map/ppermute | solution.py:103
  130.0 11.1 %collective-permute-start.13 = (bf16[128,896]{1,0:T(8,128)(2,1)S(1)}, bf16[128,896]{1,0:T(8,128)(2,1)S(1)}, u32[]{:S(2)}, u32[]{:S(2)}) collective-permute-start(bf16[128,896]{1,0:T(8,128)(2,1)S(1)} %fusion.30), channel_id=1, source_target_pairs={{0,1},{1,2},{2,3},{3,0},{4,5},{5,6},{6,7},{7,4},{8,9},{9,10},{10,1... | collective-permute-start | bytes 688136 | tf_op jit(solution)/shard_map/ppermute | solution.py:103
  134.0 2.9 %copy-start.12 = (bf16[128,3584]{1,0:T(8,128)(2,1)S(1)}, bf16[128,3584]{1,0:T(8,128)(2,1)}, u32[]{:S(2)}) copy-start(bf16[128,3584]{1,0:T(8,128)(2,1)} %get-tuple-element.17) | copy-start | bytes 2752516
  134.0 8.3 %collective-permute-start.14 = (bf16[128,896]{1,0:T(8,128)(2,1)S(1)}, bf16[128,896]{1,0:T(8,128)(2,1)S(1)}, u32[]{:S(2)}, u32[]{:S(2)}) collective-permute-start(bf16[128,896]{1,0:T(8,128)(2,1)S(1)} %fusion.31), channel_id=1, source_target_pairs={{0,3},{1,0},{2,1},{3,2},{4,7},{5,4},{6,5},{7,6},{8,11},{9,8},{10,9... | collective-permute-start | bytes 688136 | tf_op jit(solution)/shard_map/ppermute | solution.py:103
  136.8 1.4 copy-start.15
  141.0 21.4 %collective-permute-start.5 = (bf16[128,896]{1,0:T(8,128)(2,1)}, bf16[128,896]{1,0:T(8,128)(2,1)}, u32[]{:S(2)}, u32[]{:S(2)}) collective-permute-start(bf16[128,896]{1,0:T(8,128)(2,1)} %fusion.28), channel_id=1, source_target_pairs={{0,3},{1,0},{2,1},{3,2},{4,7},{5,4},{6,5},{7,6},{8,11},{9,8},{10,9... | collective-permute-start | bytes 688136 | tf_op jit(solution)/shard_map/ppermute | solution.py:103
  144.0 21.4 %all-to-all-start.3 = ((bf16[16,8,896]{2,1,0:T(8,128)(2,1)}), bf16[16,8,896]{2,1,0:T(8,128)(2,1)}, u32[]{:S(2)}, u32[]{:S(2)}) async-start(bf16[16,8,896]{2,1,0:T(8,128)(2,1)} %fusion.38), calls=%async_computation.3 | async-start | bytes 458752 | tf_op jit(solution)/shard_map/all_to_all | solution.py:111
  157.2 5.3 %copy-start.10 = (f32[128,896]{1,0:T(8,128)S(1)}, f32[128,896]{1,0:T(8,128)}, u32[]{:S(2)}) copy-start(f32[128,896]{1,0:T(8,128)} %fusion.134) | copy-start | bytes 1376260
  159.7 18.4 %copy-start.11 = (bf16[128,3584]{1,0:T(8,128)(2,1)S(1)}, bf16[128,3584]{1,0:T(8,128)(2,1)}, u32[]{:S(2)}) copy-start(bf16[128,3584]{1,0:T(8,128)(2,1)} %get-tuple-element.16) | copy-start | bytes 2752516
  159.7 25.5 %collective-permute-start.17 = (bf16[1792,256]{1,0:T(8,128)(2,1)}, bf16[1792,256]{1,0:T(8,128)(2,1)}, u32[]{:S(2)}, u32[]{:S(2)}) collective-permute-start(bf16[1792,256]{1,0:T(8,128)(2,1)} %fusion.13), channel_id=1, source_target_pairs={{0,128},{128,0},{1,129},{129,1},{2,130},{130,2},{3,131},{131,3},{4... | collective-permute-start | bytes 2752520 | tf_op jit(solution)/shard_map/ppermute | solution.py:41
  162.5 25.4 %collective-permute-start.16 = (bf16[1792,256]{1,0:T(8,128)(2,1)}, bf16[1792,256]{1,0:T(8,128)(2,1)}, u32[]{:S(2)}, u32[]{:S(2)}) collective-permute-start(bf16[1792,256]{1,0:T(8,128)(2,1)} %fusion.10), channel_id=1, source_target_pairs={{0,128},{128,0},{1,129},{129,1},{2,130},{130,2},{3,131},{131,3},{4... | collective-permute-start | bytes 2752520 | tf_op jit(solution)/shard_map/ppermute | solution.py:41
  165.3 16.4 %all-to-all-start.1 = ((bf16[16,8,896]{2,1,0:T(8,128)(2,1)}), bf16[16,8,896]{2,1,0:T(8,128)(2,1)S(1)}, u32[]{:S(2)}, u32[]{:S(2)}) async-start(bf16[16,8,896]{2,1,0:T(8,128)(2,1)} %fusion.39), calls=%async_computation.1 | async-start | bytes 458752 | tf_op jit(solution)/shard_map/all_to_all | solution.py:111
  173.4 10.5 %collective-permute-start.15 = (bf16[128,896]{1,0:T(8,128)(2,1)S(1)}, bf16[128,896]{1,0:T(8,128)(2,1)}, u32[]{:S(2)}, u32[]{:S(2)}) collective-permute-start(bf16[128,896]{1,0:T(8,128)(2,1)S(1)} %fusion.25), channel_id=1, source_target_pairs={{0,64},{64,0},{1,65},{65,1},{2,66},{66,2},{3,67},{67,3},{4,68},{68... | collective-permute-start | bytes 688136 | tf_op jit(solution)/shard_map/ppermute | solution.py:41
  178.0 7.1 %copy-start.13 = (bf16[128,3584]{1,0:T(8,128)(2,1)S(1)}, bf16[128,3584]{1,0:T(8,128)(2,1)}, u32[]{:S(2)}) copy-start(bf16[128,3584]{1,0:T(8,128)(2,1)} %get-tuple-element.17) | copy-start | bytes 2752516
  178.0 7.1 %copy-start.16 = (bf16[128,3584]{1,0:T(8,128)(2,1)S(1)}, bf16[128,3584]{1,0:T(8,128)(2,1)}, u32[]{:S(2)}) copy-start(bf16[128,3584]{1,0:T(8,128)(2,1)} %copy-done.15) | copy-start | bytes 2752516
  180.7 9.9 %collective-permute-start.18 = (bf16[256,1792]{1,0:T(8,128)(2,1)}, bf16[256,1792]{1,0:T(8,128)(2,1)}, u32[]{:S(2)}, u32[]{:S(2)}) collective-permute-start(bf16[256,1792]{1,0:T(8,128)(2,1)} %fusion.16), channel_id=1, source_target_pairs={{0,128},{128,0},{1,129},{129,1},{2,130},{130,2},{3,131},{131,3},{4... | collective-permute-start | bytes 2752520 | tf_op jit(solution)/shard_map/ppermute | solution.py:41
  185.1 2.7 %copy-start.17 = (bf16[128,3584]{1,0:T(8,128)(2,1)S(1)}, bf16[128,3584]{1,0:T(8,128)(2,1)}, u32[]{:S(2)}) copy-start(bf16[128,3584]{1,0:T(8,128)(2,1)} %copy-done.15) | copy-start | bytes 2752516
  187.8 2.7 %copy-start.14 = (bf16[128,3584]{1,0:T(8,128)(2,1)S(1)}, bf16[128,3584]{1,0:T(8,128)(2,1)}, u32[]{:S(2)}) copy-start(bf16[128,3584]{1,0:T(8,128)(2,1)} %get-tuple-element.14) | copy-start | bytes 2752516
  187.8 2.7 %copy-start.20 = (bf16[128,256]{1,0:T(8,128)(2,1)S(1)}, bf16[128,256]{1,0:T(8,128)(2,1)}, u32[]{:S(2)}) copy-start(bf16[128,256]{1,0:T(8,128)(2,1)} %get-tuple-element.32) | copy-start | bytes 196612
  187.8 2.7 %copy-start.21 = (bf16[128,256]{1,0:T(8,128)(2,1)S(1)}, bf16[128,256]{1,0:T(8,128)(2,1)}, u32[]{:S(2)}) copy-start(bf16[128,256]{1,0:T(8,128)(2,1)} %get-tuple-element.35) | copy-start | bytes 196612
where the time goes:
time: 223 us; the launch traced here: 219 us
  starting transfers between devices  74.4 us (33%)
  blocking collectives  61.5 us (28%)
  matrix products  47.1 us (21%)
  other arithmetic  16.4 us (7%)
  local copies, waits for them, and re-layouts  10.2 us (5%)
  waiting for transfers between devices  8.43 us (4%)
    all_gather x3, blocking collectives, gather_quarters(): full = lax.all_gather(q, 'tensor', axis=0, tiled=False)  61.5 us
    dot_general x30, matrix products, dot(): lax.dot_general(a, b, (((ca,), (cb,)), ((), ())), preferred_element_type=...  45.1 us
    all_to_all x4, starting transfers between devices, exchange(): return lax.all_to_all(x, 'col', split_axis=0, concat_axis=0, tiled=True)  33.6 us
    ppermute x9, starting transfers between devices, swap(): return lax.ppermute(x, axis, [(0, 1), (1, 0)])  19.1 us
    ppermute x4, starting transfers between devices, cross_quarter(): got = lax.ppermute(piece(k, last - k), ('zh', 'tensor'), perm)  14.1 us
    ppermute x6, starting transfers between devices, reduced_rows(): lax.ppermute(piece, 'tensor', [(i, (i + step) % n) for i in range(n)])  7.66 us
    concatenate x1, other arithmetic, both_halves(): jnp.concatenate([jnp.where(first, mine, other), jnp.where(first, other, m...  6.08 us
  transfers between devices with their start and end apart: 23, of which 4 were waited for; matrix products, arithmetic and copies ran while one was open for 32% of the time, Pallas kernels for 0%

commit v1 on v0

--- a/solution.py
+++ b/solution.py
@@ -44,29 +44,22 @@
 def both_halves(mine, axis):
     other = swap(mine, "dp")
     first = lax.axis_index("dp") == 0
-    return jnp.concatenate(
-        [jnp.where(first, mine, other), jnp.where(first, other, mine)], axis=axis
-    )
-
-
-def cross_quarter(x, part):
+    return lax.optimization_barrier(
+        jnp.concatenate(
+            [jnp.where(first, mine, other), jnp.where(first, other, mine)], axis=axis
+        )
+    )
+
+
+def tokens_of_far_half(layer_in, grad_out):
     t = lax.axis_index("tensor")
     n = lax.axis_size("tensor")
-    last = n - 1
-
-    def piece(low, high):
-        at = jnp.where(t == last, low, high) * part
-        return lax.dynamic_slice_in_dim(x, at, part, axis=1)
-
-    out = None
-    for k in range(n // 2):
-        perm = []
-        for z in range(2):
-            perm.append((z * n + last, (1 - z) * n + k))
-            perm.append((z * n, (1 - z) * n + last - k))
-        got = lax.ppermute(piece(k, last - k), ("zh", "tensor"), perm)
-        out = got if out is None else out + got
-    return out
+    tokens, width = layer_in.shape
+    share = tokens // n
+    mine = [lax.dynamic_slice_in_dim(x, t * share, share, axis=0) for x in (layer_in, grad_out)]
+    both = lax.all_gather(jnp.stack(mine), ("zh", "tensor"), axis=0, tiled=False)
+    far = lax.dynamic_slice_in_dim(both, (1 - lax.axis_index("zh")) * n, n, axis=0)
+    return [far[:, k].reshape(tokens, width) for k in range(2)]
 
 
 def gather_quarters(q):
@@ -123,9 +116,7 @@
 
     routes_t, combine_t = routes.T, combine.T
     far_routes, far_combine = swap(routes_t, "zh"), swap(combine_t, "zh")
-    far_in_q = cross_quarter(layer_in, part)
-    far_grad_q = cross_quarter(grad_out, part)
-
+    far_layer_in, far_grad_out = tokens_of_far_half(layer_in, grad_out)
     gate_full = both_halves(gate_weight[0], 0)
     up_full = both_halves(up_weight[0], 0)
     down_full = both_halves(down_weight[0], 1)
@@ -143,9 +134,10 @@
     in_rows = got[:, :CAP].reshape(rows, width)
     grad_rows = got[:, CAP:].reshape(rows, width)
 
+    far_routes, far_combine, _ = lax.optimization_barrier((far_routes, far_combine, sent))
     far_picker, far_factor = slot_tables(far_routes, far_combine, labels)
-    far_in = pick(far_picker, gather_quarters(far_in_q))
-    far_grad = pick_scaled(far_picker, gather_quarters(far_grad_q), far_factor)
+    far_in = pick(far_picker, far_layer_in)
+    far_grad = pick_scaled(far_picker, far_grad_out, far_factor)
     far_sent = [x.reshape(cols, CAP, width) for x in (far_in, far_grad)]
     far_got = exchange(jnp.concatenate(far_sent, axis=1))
     far_in = far_got[:, :CAP].reshape(rows, width)

time: 223 us -> 214 us (0.960)
  blocking collectives: 61.5 us -> 18 us
  waiting for transfers between devices: 8.43 us -> 45.5 us
  between operations: 1.27 us -> 14.5 us
  other arithmetic: 16.4 us -> 10.1 us
  matrix products: 47.1 us -> 41.9 us
  starting transfers between devices: 74.4 us -> 72 us
    all_gather x3 -> x1, blocking collectives: 61.5 us -> 18 us  [gather_quarters(): full = lax.all_gather(q, 'tensor', axis=0, tiled=False)]
    all_to_all x4, waiting for transfers between devices: 2.46 us -> 37.8 us  [exchange(): return lax.all_to_all(x, 'col', split_axis=0, concat_axis=0, tiled=True)]
    ppermute x9, starting transfers between devices: 19.1 us -> 34.2 us  [swap(): return lax.ppermute(x, axis, [(0, 1), (1, 0)])]
    ppermute x4 -> x0, starting transfers between devices: 14.1 us -> none  [cross_quarter(): got = lax.ppermute(piece(k, last - k), ('zh', 'tensor'), perm)]
    all_to_all x4, starting transfers between devices: 33.6 us -> 26.6 us  [exchange(): return lax.all_to_all(x, 'col', split_axis=0, concat_axis=0, tiled=True)]
    dot_general x30, matrix products: 45.1 us -> 39.9 us  [dot(): lax.dot_general(a, b, (((ca,), (cb,)), ((), ())), preferred_element_type=...]
    ppermute x9, waiting for transfers between devices: 2.23 us -> 7.03 us  [swap(): return lax.ppermute(x, axis, [(0, 1), (1, 0)])]
    ppermute x6, starting transfers between devices: 7.66 us -> 11.1 us  [reduced_rows(): lax.ppermute(piece, 'tensor', [(i, (i + step) % n) for i in range(n)])]
  transfers between devices with their start and end apart: 23 -> 20, of which waited for: 4 -> 6; matrix products, arithmetic and copies ran while one was open for 32% -> 27% of each run, Pallas kernels for 0% -> 0%
where the time goes in v1:
time: 214 us; the launch traced here: 211 us
  starting transfers between devices  72 us (34%)
  waiting for transfers between devices  45.5 us (21%)
  matrix products  41.9 us (20%)
  blocking collectives  18 us (8%)
  between operations  14.5 us (7%)
  other arithmetic  10.1 us (5%)
  local copies, waits for them, and re-layouts  9.09 us (4%)
    dot_general x30, matrix products, dot(): lax.dot_general(a, b, (((ca,), (cb,)), ((), ())), preferred_element_type=...  39.9 us
    all_to_all x4, waiting for transfers between devices, exchange(): return lax.all_to_all(x, 'col', split_axis=0, concat_axis=0, tiled=True)  37.8 us
    ppermute x9, starting transfers between devices, swap(): return lax.ppermute(x, axis, [(0, 1), (1, 0)])  34.2 us
    all_to_all x4, starting transfers between devices, exchange(): return lax.all_to_all(x, 'col', split_axis=0, concat_axis=0, tiled=True)  26.6 us
    all_gather x1, blocking collectives, gather_quarters(): full = lax.all_gather(q, 'tensor', axis=0, tiled=False)  18 us
    ppermute x6, starting transfers between devices, reduced_rows(): lax.ppermute(piece, 'tensor', [(i, (i + step) % n) for i in range(n)])  11.1 us
    ppermute x9, waiting for transfers between devices, swap(): return lax.ppermute(x, axis, [(0, 1), (1, 0)])  7.03 us
  transfers between devices with their start and end apart: 20, of which 6 were waited for; matrix products, arithmetic and copies ran while one was open for 27% of the time, Pallas kernels for 0%

profile of v1, /device:TPU:1, one launch (start us, length us, event | category | flops | bytes accessed | tf_op | source)
XLA Modules:
  0.0 211.1 jit_solution(4629729940871494822)
XLA Ops:
  7.3 7.8 %collective-permute-start.6 = (s32[8,128]{1,0:T(8,128)}, s32[8,128]{1,0:T(8,128)S(1)}, u32[]{:S(2)}, u32[]{:S(2)}) collective-permute-start(s32[8,128]{1,0:T(8,128)} %bitcast.114), channel_id=1, source_target_pairs={{0,64},{64,0},{1,65},{65,1},{2,66},{66,2},{3,67},{67,3},{4,68},{68... | collective-permute-start | bytes 12296 | tf_op jit(solution)/shard_map/ppermute | solution.py:41
  15.2 1.1 dynamic-slice_bitcast_fusion
  16.3 0.8 pad_maximum_fusion.5
  17.1 1.4 collective-permute-start
  19.1 0.4 fusion.4
  19.6 0.4 fusion.7
  20.1 1.4 pad_maximum_fusion
  21.5 6.6 %all-to-all-start = ((bf16[16,16,3584]{2,1,0:T(8,128)(2,1)}), bf16[16,16,3584]{2,1,0:T(8,128)(2,1)}, u32[]{:S(2)}, u32[]{:S(2)}) async-start(bf16[16,16,3584]{2,1,0:T(8,128)(2,1)} %pad_maximum_fusion), calls=%async_computation | async-start | bytes 3670016 | tf_op jit(solution)/shard_map/all_to_all | solution.py:104
  28.1 0.4 collective-permute-start.1
  29.2 1.3 broadcast_select_fusion.5
  30.5 1.4 pad_maximum_fusion.1
  32.1 1.7 broadcast_select_fusion.1
  33.9 1.4 pad_maximum_fusion.2
  35.3 22.3 %all-to-all-done = bf16[16,16,3584]{2,1,0:T(8,128)(2,1)} async-done(((bf16[16,16,3584]{2,1,0:T(8,128)(2,1)}), bf16[16,16,3584]{2,1,0:T(8,128)(2,1)}, u32[]{:S(2)}, u32[]{:S(2)}) %all-to-all-start) | async-done | bytes 1835040 | tf_op jit(solution)/shard_map/all_to_all | solution.py:104
  57.6 2.5 %fusion.140 = f32[128,256]{1,0:T(8,128)S(1)} fusion(bf16[256,3584]{1,0:T(8,128)(2,1)} %pad_maximum_fusion.1, bf16[16,16,3584]{2,1,0:T(8,128)(2,1)} %all-to-all-done), kind=kOutput, calls=%fused_computation.202 | convolution fusion | flops 234881024 | bytes 2883584 | tf_op jit(solution)/shard_map/dot_general | solution.py:14
  60.2 1.7 fusion.142
  62.0 2.2 %multiply_convert_fusion.1 = (bf16[128,256]{1,0:T(8,128)(2,1)}, bf16[128,256]{1,0:T(8,128)(2,1)S(1)}, bf16[128,256]{1,0:T(8,128)(2,1)S(1)}) fusion(f32[128,256]{1,0:T(8,128)S(1)} %fusion.142, f32[128,256]{1,0:T(8,128)S(1)} %fusion.140, bf16[3584,256]{1,0:T(8,128)(2,1)S(1)} %copy-done, bf16[16,16,3584]{2,1,0:T(8,128)(2,1)} %all-to-all-done), kind=kOutput, calls=%fused_computation.118 | convolution fusion | flops 235372544 | bytes 3211264 | tf_op jit(solution)/shard_map/dot_general | solution.py:14
  64.5 1.0 fusion.28
  65.5 3.0 %collective-permute-start.5 = (bf16[128,896]{1,0:T(8,128)(2,1)}, bf16[128,896]{1,0:T(8,128)(2,1)}, u32[]{:S(2)}, u32[]{:S(2)}) collective-permute-start(bf16[128,896]{1,0:T(8,128)(2,1)} %fusion.28), channel_id=1, source_target_pairs={{0,3},{1,0},{2,1},{3,2},{4,7},{5,4},{6,5},{7,6},{8,11},{9,8},{10,9... | collective-permute-start | bytes 688136 | tf_op jit(solution)/shard_map/ppermute | solution.py:96
  68.8 1.6 constant_dynamic-slice_fusion
  70.4 0.4 fusion.5
  70.8 0.4 fusion.6
  71.2 1.4 pad_maximum_fusion.4
  72.6 6.6 %all-to-all-start.2 = ((bf16[16,16,3584]{2,1,0:T(8,128)(2,1)}), bf16[16,16,3584]{2,1,0:T(8,128)(2,1)}, u32[]{:S(2)}, u32[]{:S(2)}) async-start(bf16[16,16,3584]{2,1,0:T(8,128)(2,1)} %pad_maximum_fusion.4), calls=%async_computation.2 | async-start | bytes 3670016 | tf_op jit(solution)/shard_map/all_to_all | solution.py:104
  79.2 1.0 fusion.27
  80.2 1.5 collective-permute-start.4
  81.7 1.3 fusion.58
  83.0 1.3 fusion.64
  84.4 1.0 fusion.26
  85.4 2.5 %slice_bitcast_fusion.3 = (bf16[128,3584]{1,0:T(8,128)(2,1)S(1)}, bf16[128,3584]{1,0:T(8,128)(2,1)}) fusion(bf16[16,16,3584]{2,1,0:T(8,128)(2,1)} %all-to-all-done), kind=kLoop, calls=%fused_computation.79 | loop fusion | bytes 3670016 | tf_op jit(solution)/shard_map/reshape | solution.py:135
  87.9 13.9 %all-to-all-done.2 = bf16[16,16,3584]{2,1,0:T(8,128)(2,1)} async-done(((bf16[16,16,3584]{2,1,0:T(8,128)(2,1)}), bf16[16,16,3584]{2,1,0:T(8,128)(2,1)}, u32[]{:S(2)}, u32[]{:S(2)}) %all-to-all-start.2) | async-done | bytes 1835040 | tf_op jit(solution)/shard_map/all_to_all | solution.py:104
  101.8 2.5 %fusion.141 = f32[128,256]{1,0:T(8,128)S(1)} fusion(bf16[256,3584]{1,0:T(8,128)(2,1)} %pad_maximum_fusion.1, bf16[16,16,3584]{2,1,0:T(8,128)(2,1)} %all-to-all-done.2), kind=kOutput, calls=%fused_computation.203 | convolution fusion | flops 234881024 | bytes 2883584 | tf_op jit(solution)/shard_map/dot_general | solution.py:14
  104.3 1.7 fusion.144
  106.1 2.2 %multiply_convert_fusion = (bf16[128,256]{1,0:T(8,128)(2,1)}, bf16[128,256]{1,0:T(8,128)(2,1)S(1)}, bf16[128,256]{1,0:T(8,128)(2,1)S(1)}) fusion(f32[128,256]{1,0:T(8,128)S(1)} %fusion.144, f32[128,256]{1,0:T(8,128)S(1)} %fusion.141, bf16[3584,256]{1,0:T(8,128)(2,1)S(1)} %copy-done.1, bf16[16,16,3584]{2,1,0:T(8,128)(2,1)} %all-to-all-done.2), kind=kOutput, calls=%fused_computation.117 | convolution fusion | flops 235372544 | bytes 3211264 | tf_op jit(solution)/shard_map/dot_general | solution.py:14
  108.3 0.3 fusion.44
  108.6 0.3 fusion.50
  108.9 0.3 fusion.56
  109.2 0.3 fusion.31
  109.5 3.5 %collective-permute-start.10 = (bf16[128,896]{1,0:T(8,128)(2,1)S(1)}, bf16[128,896]{1,0:T(8,128)(2,1)S(1)}, u32[]{:S(2)}, u32[]{:S(2)}) collective-permute-start(bf16[128,896]{1,0:T(8,128)(2,1)S(1)} %fusion.31), channel_id=1, source_target_pairs={{0,3},{1,0},{2,1},{3,2},{4,7},{5,4},{6,5},{7,6},{8,11},{9,8},{10,9... | collective-permute-start | bytes 688136 | tf_op jit(solution)/shard_map/ppermute | solution.py:96
  113.0 0.3 fusion.30
  113.4 0.3 fusion.29
  113.7 2.8 %collective-permute-start.8 = (bf16[128,896]{1,0:T(8,128)(2,1)S(1)}, bf16[128,896]{1,0:T(8,128)(2,1)S(1)}, u32[]{:S(2)}, u32[]{:S(2)}) collective-permute-start(bf16[128,896]{1,0:T(8,128)(2,1)S(1)} %fusion.29), channel_id=1, source_target_pairs={{0,2},{1,3},{2,0},{3,1},{4,6},{5,7},{6,4},{7,5},{8,10},{9,11},{10,... | collective-permute-start | bytes 688136 | tf_op jit(solution)/shard_map/ppermute | solution.py:96
  116.6 2.5 %slice_bitcast_fusion.1 = (bf16[128,3584]{1,0:T(8,128)(2,1)}, bf16[128,3584]{1,0:T(8,128)(2,1)S(1)}) fusion(bf16[16,16,3584]{2,1,0:T(8,128)(2,1)} %all-to-all-done.2), kind=kLoop, calls=%fused_computation.77 | loop fusion | bytes 3670016 | tf_op jit(solution)/shard_map/reshape | solution.py:144
  119.5 1.4 fusion.13
  120.9 0.6 collective-permute-done.9
  121.6 16.3 %collective-permute-start.13 = (bf16[1792,256]{1,0:T(8,128)(2,1)}, bf16[1792,256]{1,0:T(8,128)(2,1)}, u32[]{:S(2)}, u32[]{:S(2)}) collective-permute-start(bf16[1792,256]{1,0:T(8,128)(2,1)} %fusion.13), channel_id=1, source_target_pairs={{0,128},{128,0},{1,129},{129,1},{2,130},{130,2},{3,131},{131,3},{4... | collective-permute-start | bytes 2752520 | tf_op jit(solution)/shard_map/ppermute | solution.py:41
  137.9 1.0 fusion.32
  138.9 8.1 %all-to-all-start.3 = ((bf16[16,8,896]{2,1,0:T(8,128)(2,1)}), bf16[16,8,896]{2,1,0:T(8,128)(2,1)}, u32[]{:S(2)}, u32[]{:S(2)}) async-start(bf16[16,8,896]{2,1,0:T(8,128)(2,1)} %fusion.32), calls=%async_computation.3 | async-start | bytes 458752 | tf_op jit(solution)/shard_map/all_to_all | solution.py:104
  147.1 2.3 %fusion.33 = bf16[16,8,896]{2,1,0:T(8,128)(2,1)} fusion(f32[128,896]{1,0:T(8,128)S(1)} %fusion.64, bf16[128,256]{1,0:T(8,128)(2,1)S(1)} %get-tuple-element.29, bf16[128,896]{1,0:T(8,128)(2,1)} %collective-permute-done.5, bf16[128,896]{1,0:T(8,128)(2,1)} %collective-permute-done.4, bf16[128,896]{1,0:T(8,128)(2,1)} %collective-permute-done.3, ...), kind=kOutput, calls=%fused_computation.69 | convolution fusion | flops 59637760 | bytes 1900548 | tf_op jit(solution)/shard_map/dot_general | solution.py:14
  149.4 1.4 fusion.10
  150.7 2.1 %collective-permute-start.12 = (bf16[1792,256]{1,0:T(8,128)(2,1)}, bf16[1792,256]{1,0:T(8,128)(2,1)}, u32[]{:S(2)}, u32[]{:S(2)}) collective-permute-start(bf16[1792,256]{1,0:T(8,128)(2,1)} %fusion.10), channel_id=1, source_target_pairs={{0,128},{128,0},{1,129},{129,1},{2,130},{130,2},{3,131},{131,3},{4... | collective-permute-start | bytes 2752520 | tf_op jit(solution)/shard_map/ppermute | solution.py:41
  152.9 1.6 all-to-all-done.3
  154.4 5.3 %all-to-all-start.1 = ((bf16[16,8,896]{2,1,0:T(8,128)(2,1)}), bf16[16,8,896]{2,1,0:T(8,128)(2,1)S(1)}, u32[]{:S(2)}, u32[]{:S(2)}) async-start(bf16[16,8,896]{2,1,0:T(8,128)(2,1)} %fusion.33), calls=%async_computation.1 | async-start | bytes 458752 | tf_op jit(solution)/shard_map/all_to_all | solution.py:104
  159.8 1.2 fusion.25
  161.0 4.1 %collective-permute-start.11 = (bf16[128,896]{1,0:T(8,128)(2,1)S(1)}, bf16[128,896]{1,0:T(8,128)(2,1)}, u32[]{:S(2)}, u32[]{:S(2)}) collective-permute-start(bf16[128,896]{1,0:T(8,128)(2,1)S(1)} %fusion.25), channel_id=1, source_target_pairs={{0,64},{64,0},{1,65},{65,1},{2,66},{66,2},{3,67},{67,3},{4,68},{68... | collective-permute-start | bytes 688136 | tf_op jit(solution)/shard_map/ppermute | solution.py:41
  165.1 2.3 %fusion.16 = bf16[256,1792]{1,0:T(8,128)(2,1)} fusion(s32[]{:T(128)S(6)} %select_n.130, bf16[128,3584]{1,0:T(8,128)(2,1)S(1)} %get-tuple-element.20, bf16[128,3584]{1,0:T(8,128)(2,1)S(1)} %copy-done.7, bf16[128,256]{1,0:T(8,128)(2,1)} %get-tuple-element.31, bf16[128,256]{1,0:T(8,128)(2,1)} %get-tuple-element.28), kind=kOutput, calls=%fused_computation.26 | convolution fusion | flops 237895680 | bytes 2883588 | tf_op jit(solution)/shard_map/dot_general | solution.py:14
  167.4 1.8 collective-permute-start.14
  169.2 6.8 %collective-permute-done.11 = bf16[128,896]{1,0:T(8,128)(2,1)} collective-permute-done((bf16[128,896]{1,0:T(8,128)(2,1)S(1)}, bf16[128,896]{1,0:T(8,128)(2,1)}, u32[]{:S(2)}, u32[]{:S(2)}) %collective-permute-start.11) | collective-permute-done | bytes 229408 | tf_op jit(solution)/shard_map/ppermute | solution.py:41
  176.0 1.2 add_convert_fusion.3
  177.3 2.8 %add_convert_fusion.1 = bf16[1792,256]{1,0:T(8,128)(2,1)} fusion(bf16[1792,256]{1,0:T(8,128)(2,1)} %collective-permute-done.13, bf16[128,256]{1,0:T(8,128)(2,1)S(1)} %get-tuple-element.33, bf16[128,256]{1,0:T(8,128)(2,1)S(1)} %get-tuple-element.30, s32[]{:T(128)S(6)} %select_n.129, bf16[128,3584]{1,0:T(8,128)(2,1)S(1)} %copy-done.6, ...), kind=kOutput, calls=%fused_computation.41 | convolution fusion | flops 239730688 | bytes 3801092 | tf_op jit(solution)/shard_map/dot_general | solution.py:14
  180.1 2.6 %add_convert_fusion.2 = bf16[1792,256]{1,0:T(8,128)(2,1)} fusion(bf16[1792,256]{1,0:T(8,128)(2,1)} %collective-permute-done.12, bf16[128,256]{1,0:T(8,128)(2,1)S(1)} %get-tuple-element.32, bf16[128,256]{1,0:T(8,128)(2,1)S(1)} %get-tuple-element.29, s32[]{:T(128)S(6)} %select_n.129, bf16[128,3584]{1,0:T(8,128)(2,1)S(1)} %copy-done.6, ...), kind=kOutput, calls=%fused_computation.42 | convolution fusion | flops 239730688 | bytes 3801092 | tf_op jit(solution)/shard_map/dot_general | solution.py:14
  182.7 2.6 %add_convert_fusion = bf16[256,1792]{1,0:T(8,128)(2,1)} fusion(bf16[256,1792]{1,0:T(8,128)(2,1)} %collective-permute-done.14, s32[]{:T(128)S(6)} %select_n.129, bf16[128,3584]{1,0:T(8,128)(2,1)S(1)} %get-tuple-element.20, bf16[128,3584]{1,0:T(8,128)(2,1)S(1)} %copy-done.7, bf16[128,256]{1,0:T(8,128)(2,1)S(1)} %copy-done.17, bf16[128,256]{1,0:T(8,128)(2,1)S(1)} %copy-done.16), kind=kOutput, calls=%fused_computation.40 | convolution fusion | flops 239730688 | bytes 3801092 | tf_op jit(solution)/shard_map/dot_general | solution.py:14
  185.2 18.0 %all-gather.1 = bf16[512,896]{1,0:T(8,128)(2,1)S(1)} all-gather(bf16[128,896]{1,0:T(8,128)(2,1)S(1)} %add_convert_fusion.3), channel_id=3, replica_groups=mesh['dp'=2,'zh'=2,'col'=16,'tensor'=4] {'tensor'}, dimensions={0}, use_global_device_ids=true | all-gather | bytes 1146880 | tf_op jit(solution)/shard_map/all_gather | solution.py:68
  203.3 1.0 copy.20
  (74 shorter events, 3.1 us)
Async XLA Ops:
  7.2 11.3 %copy-start.14 = (s32[128,8]{0,1:T(8,128)S(1)}, s32[128,8]{0,1:T(8,128)}, u32[]{:S(2)}) copy-start(s32[128,8]{0,1:T(8,128)} %param.9) | copy-start | bytes 12292
  7.2 11.6 %copy-start.15 = (f32[128,8]{0,1:T(8,128)S(1)}, f32[128,8]{0,1:T(8,128)}, u32[]{:S(2)}) copy-start(f32[128,8]{0,1:T(8,128)} %param.10) | copy-start | bytes 12292
  7.2 11.9 %copy-start.2 = (bf16[128,3584]{1,0:T(8,128)(2,1)S(1)}, bf16[128,3584]{1,0:T(8,128)(2,1)}, u32[]{:S(2)}) copy-start(bf16[128,3584]{1,0:T(8,128)(2,1)} %param.8) | copy-start | bytes 2752516
  7.2 9.9 %copy-start.11 = (bf16[1,256,1792]{2,1,0:T(8,128)(2,1)S(1)}, bf16[1,256,1792]{2,1,0:T(8,128)(2,1)}, u32[]{:S(2)}) copy-start(bf16[1,256,1792]{2,1,0:T(8,128)(2,1)} %param.13) | copy-start | bytes 2752516
  7.2 61.6 %all-gather.4.cloned.1.call-start = ((), (), s32[]{:S(2)}) async-start(), calls=%async_computation.4 | async-start | bytes 4128768 | tf_op jit(solution)/shard_map/all_gather | solution.py:60
  7.3 21.4 %collective-permute-start.6 = (s32[8,128]{1,0:T(8,128)}, s32[8,128]{1,0:T(8,128)S(1)}, u32[]{:S(2)}, u32[]{:S(2)}) collective-permute-start(s32[8,128]{1,0:T(8,128)} %bitcast.114), channel_id=1, source_target_pairs={{0,64},{64,0},{1,65},{65,1},{2,66},{66,2},{3,67},{67,3},{4,68},{68... | collective-permute-start | bytes 12296 | tf_op jit(solution)/shard_map/ppermute | solution.py:41
  15.1 13.6 %collective-permute-start.7 = (f32[8,128]{1,0:T(8,128)}, f32[8,128]{1,0:T(8,128)S(1)}, u32[]{:S(2)}, u32[]{:S(2)}) collective-permute-start(f32[8,128]{1,0:T(8,128)} %bitcast.117), channel_id=1, source_target_pairs={{0,64},{64,0},{1,65},{65,1},{2,66},{66,2},{3,67},{67,3},{4,68},{68... | collective-permute-start | bytes 12296 | tf_op jit(solution)/shard_map/ppermute | solution.py:41
  16.2 3.3 %copy-start.3 = (bf16[128,3584]{1,0:T(8,128)(2,1)S(1)}, bf16[128,3584]{1,0:T(8,128)(2,1)}, u32[]{:S(2)}) copy-start(bf16[128,3584]{1,0:T(8,128)(2,1)} %param.7) | copy-start | bytes 2752516
  17.1 12.1 %collective-permute-start = (bf16[256,1792]{1,0:T(8,128)(2,1)S(1)}, bf16[256,1792]{1,0:T(8,128)(2,1)}, u32[]{:S(2)}, u32[]{:S(2)}) collective-permute-start(bf16[256,1792]{1,0:T(8,128)(2,1)S(1)} %bitcast.111), channel_id=1, source_target_pairs={{0,128},{128,0},{1,129},{129,1},{2,130},{130,2},{3,131},{131,3},{4... | collective-permute-start | bytes 2752520 | tf_op jit(solution)/shard_map/ppermute | solution.py:41
  21.5 6.6 %copy-start.13 = (bf16[1,1792,256]{2,1,0:T(8,128)(2,1)S(1)}, bf16[1,1792,256]{2,1,0:T(8,128)(2,1)}, u32[]{:S(2)}) copy-start(bf16[1,1792,256]{2,1,0:T(8,128)(2,1)} %param.12) | copy-start | bytes 2752516
  21.5 7.0 %copy-start.12 = (bf16[1,1792,256]{2,1,0:T(8,128)(2,1)S(1)}, bf16[1,1792,256]{2,1,0:T(8,128)(2,1)}, u32[]{:S(2)}) copy-start(bf16[1,1792,256]{2,1,0:T(8,128)(2,1)} %param.11) | copy-start | bytes 2752516
  21.5 36.1 %all-to-all-start = ((bf16[16,16,3584]{2,1,0:T(8,128)(2,1)}), bf16[16,16,3584]{2,1,0:T(8,128)(2,1)}, u32[]{:S(2)}, u32[]{:S(2)}) async-start(bf16[16,16,3584]{2,1,0:T(8,128)(2,1)} %pad_maximum_fusion), calls=%async_computation | async-start | bytes 3670016 | tf_op jit(solution)/shard_map/all_to_all | solution.py:104
  28.1 3.8 %collective-permute-start.1 = (bf16[1792,256]{1,0:T(8,128)(2,1)S(1)}, bf16[1792,256]{1,0:T(8,128)(2,1)}, u32[]{:S(2)}, u32[]{:S(2)}) collective-permute-start(bf16[1792,256]{1,0:T(8,128)(2,1)S(1)} %bitcast.113), channel_id=1, source_target_pairs={{0,128},{128,0},{1,129},{129,1},{2,130},{130,2},{3,131},{131,3},{4... | collective-permute-start | bytes 2752520 | tf_op jit(solution)/shard_map/ppermute | solution.py:41
  28.5 3.6 %collective-permute-start.2 = (bf16[1792,256]{1,0:T(8,128)(2,1)S(1)}, bf16[1792,256]{1,0:T(8,128)(2,1)}, u32[]{:S(2)}, u32[]{:S(2)}) collective-permute-start(bf16[1792,256]{1,0:T(8,128)(2,1)S(1)} %bitcast.112), channel_id=1, source_target_pairs={{0,128},{128,0},{1,129},{129,1},{2,130},{130,2},{3,131},{131,3},{4... | collective-permute-start | bytes 2752520 | tf_op jit(solution)/shard_map/ppermute | solution.py:41
  60.1 1.8 copy-start
  65.5 81.6 %collective-permute-start.5 = (bf16[128,896]{1,0:T(8,128)(2,1)}, bf16[128,896]{1,0:T(8,128)(2,1)}, u32[]{:S(2)}, u32[]{:S(2)}) collective-permute-start(bf16[128,896]{1,0:T(8,128)(2,1)} %fusion.28), channel_id=1, source_target_pairs={{0,3},{1,0},{2,1},{3,2},{4,7},{5,4},{6,5},{7,6},{8,11},{9,8},{10,9... | collective-permute-start | bytes 688136 | tf_op jit(solution)/shard_map/ppermute | solution.py:96
  72.6 29.2 %all-to-all-start.2 = ((bf16[16,16,3584]{2,1,0:T(8,128)(2,1)}), bf16[16,16,3584]{2,1,0:T(8,128)(2,1)}, u32[]{:S(2)}, u32[]{:S(2)}) async-start(bf16[16,16,3584]{2,1,0:T(8,128)(2,1)} %pad_maximum_fusion.4), calls=%async_computation.2 | async-start | bytes 3670016 | tf_op jit(solution)/shard_map/all_to_all | solution.py:104
  80.2 66.9 %collective-permute-start.4 = (bf16[128,896]{1,0:T(8,128)(2,1)}, bf16[128,896]{1,0:T(8,128)(2,1)}, u32[]{:S(2)}, u32[]{:S(2)}) collective-permute-start(bf16[128,896]{1,0:T(8,128)(2,1)} %fusion.27), channel_id=1, source_target_pairs={{0,1},{1,2},{2,3},{3,0},{4,5},{5,6},{6,7},{7,4},{8,9},{9,10},{10,1... | collective-permute-start | bytes 688136 | tf_op jit(solution)/shard_map/ppermute | solution.py:96
  104.3 1.8 copy-start.1
  109.5 9.9 %collective-permute-start.10 = (bf16[128,896]{1,0:T(8,128)(2,1)S(1)}, bf16[128,896]{1,0:T(8,128)(2,1)S(1)}, u32[]{:S(2)}, u32[]{:S(2)}) collective-permute-start(bf16[128,896]{1,0:T(8,128)(2,1)S(1)} %fusion.31), channel_id=1, source_target_pairs={{0,3},{1,0},{2,1},{3,2},{4,7},{5,4},{6,5},{7,6},{8,11},{9,8},{10,9... | collective-permute-start | bytes 688136 | tf_op jit(solution)/shard_map/ppermute | solution.py:96
  113.3 8.3 %collective-permute-start.9 = (bf16[128,896]{1,0:T(8,128)(2,1)S(1)}, bf16[128,896]{1,0:T(8,128)(2,1)S(1)}, u32[]{:S(2)}, u32[]{:S(2)}) collective-permute-start(bf16[128,896]{1,0:T(8,128)(2,1)S(1)} %fusion.30), channel_id=1, source_target_pairs={{0,1},{1,2},{2,3},{3,0},{4,5},{5,6},{6,7},{7,4},{8,9},{9,10},{10,1... | collective-permute-start | bytes 688136 | tf_op jit(solution)/shard_map/ppermute | solution.py:96
  113.7 5.8 %copy-start.4 = (bf16[128,3584]{1,0:T(8,128)(2,1)S(1)}, bf16[128,3584]{1,0:T(8,128)(2,1)}, u32[]{:S(2)}) copy-start(bf16[128,3584]{1,0:T(8,128)(2,1)} %get-tuple-element.21) | copy-start | bytes 2752516
  113.7 24.2 %collective-permute-start.8 = (bf16[128,896]{1,0:T(8,128)(2,1)S(1)}, bf16[128,896]{1,0:T(8,128)(2,1)S(1)}, u32[]{:S(2)}, u32[]{:S(2)}) collective-permute-start(bf16[128,896]{1,0:T(8,128)(2,1)S(1)} %fusion.29), channel_id=1, source_target_pairs={{0,2},{1,3},{2,0},{3,1},{4,6},{5,7},{6,4},{7,5},{8,10},{9,11},{10,... | collective-permute-start | bytes 688136 | tf_op jit(solution)/shard_map/ppermute | solution.py:96
  119.1 1.9 copy-start.8
  119.4 27.7 %collective-permute-start.3 = (bf16[128,896]{1,0:T(8,128)(2,1)}, bf16[128,896]{1,0:T(8,128)(2,1)}, u32[]{:S(2)}, u32[]{:S(2)}) collective-permute-start(bf16[128,896]{1,0:T(8,128)(2,1)} %fusion.26), channel_id=1, source_target_pairs={{0,2},{1,3},{2,0},{3,1},{4,6},{5,7},{6,4},{7,5},{8,10},{9,11},{10,... | collective-permute-start | bytes 688136 | tf_op jit(solution)/shard_map/ppermute | solution.py:96
  121.6 55.7 %collective-permute-start.13 = (bf16[1792,256]{1,0:T(8,128)(2,1)}, bf16[1792,256]{1,0:T(8,128)(2,1)}, u32[]{:S(2)}, u32[]{:S(2)}) collective-permute-start(bf16[1792,256]{1,0:T(8,128)(2,1)} %fusion.13), channel_id=1, source_target_pairs={{0,128},{128,0},{1,129},{129,1},{2,130},{130,2},{3,131},{131,3},{4... | collective-permute-start | bytes 2752520 | tf_op jit(solution)/shard_map/ppermute | solution.py:41
  138.9 15.6 %all-to-all-start.3 = ((bf16[16,8,896]{2,1,0:T(8,128)(2,1)}), bf16[16,8,896]{2,1,0:T(8,128)(2,1)}, u32[]{:S(2)}, u32[]{:S(2)}) async-start(bf16[16,8,896]{2,1,0:T(8,128)(2,1)} %fusion.32), calls=%async_computation.3 | async-start | bytes 458752 | tf_op jit(solution)/shard_map/all_to_all | solution.py:104
  147.0 2.3 %copy-start.5 = (bf16[128,3584]{1,0:T(8,128)(2,1)S(1)}, bf16[128,3584]{1,0:T(8,128)(2,1)}, u32[]{:S(2)}) copy-start(bf16[128,3584]{1,0:T(8,128)(2,1)} %get-tuple-element.21) | copy-start | bytes 2752516
  147.0 2.3 %copy-start.9 = (bf16[128,3584]{1,0:T(8,128)(2,1)S(1)}, bf16[128,3584]{1,0:T(8,128)(2,1)}, u32[]{:S(2)}) copy-start(bf16[128,3584]{1,0:T(8,128)(2,1)} %copy-done.8) | copy-start | bytes 2752516
  149.4 15.7 %copy-start.7 = (bf16[128,3584]{1,0:T(8,128)(2,1)S(1)}, bf16[128,3584]{1,0:T(8,128)(2,1)}, u32[]{:S(2)}) copy-start(bf16[128,3584]{1,0:T(8,128)(2,1)} %get-tuple-element.18) | copy-start | bytes 2752516
  150.7 29.3 %collective-permute-start.12 = (bf16[1792,256]{1,0:T(8,128)(2,1)}, bf16[1792,256]{1,0:T(8,128)(2,1)}, u32[]{:S(2)}, u32[]{:S(2)}) collective-permute-start(bf16[1792,256]{1,0:T(8,128)(2,1)} %fusion.10), channel_id=1, source_target_pairs={{0,128},{128,0},{1,129},{129,1},{2,130},{130,2},{3,131},{131,3},{4... | collective-permute-start | bytes 2752520 | tf_op jit(solution)/shard_map/ppermute | solution.py:41
  154.4 14.7 %all-to-all-start.1 = ((bf16[16,8,896]{2,1,0:T(8,128)(2,1)}), bf16[16,8,896]{2,1,0:T(8,128)(2,1)S(1)}, u32[]{:S(2)}, u32[]{:S(2)}) async-start(bf16[16,8,896]{2,1,0:T(8,128)(2,1)} %fusion.33), calls=%async_computation.1 | async-start | bytes 458752 | tf_op jit(solution)/shard_map/all_to_all | solution.py:104
  161.0 15.0 %collective-permute-start.11 = (bf16[128,896]{1,0:T(8,128)(2,1)S(1)}, bf16[128,896]{1,0:T(8,128)(2,1)}, u32[]{:S(2)}, u32[]{:S(2)}) collective-permute-start(bf16[128,896]{1,0:T(8,128)(2,1)S(1)} %fusion.25), channel_id=1, source_target_pairs={{0,64},{64,0},{1,65},{65,1},{2,66},{66,2},{3,67},{67,3},{4,68},{68... | collective-permute-start | bytes 688136 | tf_op jit(solution)/shard_map/ppermute | solution.py:41
  165.1 12.2 %copy-start.6 = (bf16[128,3584]{1,0:T(8,128)(2,1)S(1)}, bf16[128,3584]{1,0:T(8,128)(2,1)}, u32[]{:S(2)}) copy-start(bf16[128,3584]{1,0:T(8,128)(2,1)} %get-tuple-element.21) | copy-start | bytes 2752516
  167.4 15.3 %collective-permute-start.14 = (bf16[256,1792]{1,0:T(8,128)(2,1)}, bf16[256,1792]{1,0:T(8,128)(2,1)}, u32[]{:S(2)}, u32[]{:S(2)}) collective-permute-start(bf16[256,1792]{1,0:T(8,128)(2,1)} %fusion.16), channel_id=1, source_target_pairs={{0,128},{128,0},{1,129},{129,1},{2,130},{130,2},{3,131},{131,3},{4... | collective-permute-start | bytes 2752520 | tf_op jit(solution)/shard_map/ppermute | solution.py:41
  177.2 2.8 %copy-start.10 = (bf16[128,3584]{1,0:T(8,128)(2,1)S(1)}, bf16[128,3584]{1,0:T(8,128)(2,1)}, u32[]{:S(2)}) copy-start(bf16[128,3584]{1,0:T(8,128)(2,1)} %copy-done.8) | copy-start | bytes 2752516
  180.0 2.6 %copy-start.16 = (bf16[128,256]{1,0:T(8,128)(2,1)S(1)}, bf16[128,256]{1,0:T(8,128)(2,1)}, u32[]{:S(2)}) copy-start(bf16[128,256]{1,0:T(8,128)(2,1)} %get-tuple-element.28) | copy-start | bytes 196612
  180.0 2.6 %copy-start.17 = (bf16[128,256]{1,0:T(8,128)(2,1)S(1)}, bf16[128,256]{1,0:T(8,128)(2,1)}, u32[]{:S(2)}) copy-start(bf16[128,256]{1,0:T(8,128)(2,1)} %get-tuple-element.31) | copy-start | bytes 196612
Sparse Core Ops, SparseCore 0:
  17.2 51.4 all-gather.3

commit v2 on v1

v2 whole, which is shorter than its diff:
```python
import jax
import jax.numpy as jnp
from jax import lax
from jax.sharding import Mesh
from jax.sharding import PartitionSpec as P


CAP = 8
BF = jnp.bfloat16
F32 = jnp.float32


def dot(a, b, ca, cb):
    return lax.dot_general(a, b, (((ca,), (cb,)), ((), ())), preferred_element_type=F32)


def cut(x, index, size, axis):
    return lax.dynamic_slice_in_dim(x, index * size, size, axis=axis)


def slot_tables(routes_t, combine_t, labels):
    tokens = routes_t.shape[1]
    experts = labels.shape[0]
    hits = routes_t[None, :, :] == labels[:, None, None]
    chosen = jnp.sum(hits.astype(F32), axis=1)
    scale = jnp.sum(jnp.where(hits, combine_t[None, :, :], 0.0), axis=1)
    ids = jnp.arange(tokens, dtype=jnp.int32)
    earlier = (ids[:, None] < ids[None, :]).astype(BF)
    before = jnp.dot(chosen.astype(BF), earlier, preferred_element_type=F32)
    slots = jnp.arange(CAP, dtype=F32)
    taken = (before[:, None, :] == slots[None, :, None]) & (chosen[:, None, :] > 0)
    factor = jnp.sum(jnp.where(taken, scale[:, None, :], 0.0), axis=2)
    return taken.astype(BF).reshape(experts * CAP, tokens), factor.reshape(experts * CAP, 1)


def picked(picker, factor, layer_in, grad_out, cols):
    width = layer_in.shape[1]
    in_rows = jnp.dot(picker, layer_in, preferred_element_type=F32).astype(BF)
    grad_rows = (jnp.dot(picker, grad_out, preferred_element_type=F32) * factor).astype(BF)
    return jnp.concatenate(
        [in_rows.reshape(cols, CAP, width), grad_rows.reshape(cols, CAP, width)], axis=1
    )


def swap(x, axis):
    return lax.ppermute(x, axis, [(0, 1), (1, 0)])


def both_halves(mine, axis):
    other = swap(mine, "dp")
    first = lax.axis_index("dp") == 0
    return lax.optimization_barrier(
        jnp.concatenate(
            [jnp.where(first, mine, other), jnp.where(first, other, mine)], axis=axis
        )
    )


def exchange(x, axes):
    return lax.all_to_all(x, axes, split_axis=0, concat_axis=0, tiled=True)


def rotated(x, step):
    n = lax.axis_size("tensor")
    return lax.ppermute(x, "tensor", [(i, (i + step) % n) for i in range(n)])


def unit_gradients(gate, up, dhid):
    sigma = jax.nn.sigmoid(gate)
    silu_gate = gate * sigma
    act = (silu_gate * up).astype(BF)
    d_up = (dhid * silu_gate).astype(BF)
    d_gate = (dhid * up * sigma * (1.0 + gate * (1.0 - sigma))).astype(BF)
    return act, d_gate, d_up


def reduced_rows(d_gate, d_up, gate_full, up_full, part):
    n = lax.axis_size("tensor")
    t = lax.axis_index("tensor")

    def row_part(index):
        return dot(d_gate, cut(gate_full, index, part, 0), 1, 1) + dot(
            d_up, cut(up_full, index, part, 0), 1, 1
        )

    received = [rotated(row_part((t + s) % n).astype(BF), s) for s in (2, 1, 3)]
    total = row_part(t)
    for piece in received:
        total = total + piece.astype(F32)
    return total.astype(BF)


def inner(grad_out, layer_in, routes, combine, gate_weight, up_weight, down_weight):
    cols = lax.axis_size("col")
    n = lax.axis_size("tensor")
    tokens, width = grad_out.shape
    rows = cols * CAP
    half = width // 2
    part = width // n
    per_half = half // part
    my_dp = lax.axis_index("dp")
    my_zh = lax.axis_index("zh")
    t = lax.axis_index("tensor")

    ids = jnp.arange(cols, dtype=jnp.int32)
    labels = jnp.concatenate([my_zh * cols + ids, (1 - my_zh) * cols + ids])
    picker, factor = slot_tables(routes.T, combine.T, labels)
    near_picker, far_picker = picker[:rows], picker[rows:]

    far_sent = picked(
        far_picker, factor[rows:], cut(layer_in, t, part, 1), cut(grad_out, t, part, 1), cols
    )
    far_got = exchange(far_sent, "col")
    far_in = swap(far_got[:, :CAP].reshape(rows, part), "zh")
    far_grad = swap(far_got[:, CAP:].reshape(rows, part), "zh")

    near_got = exchange(picked(near_picker, factor[:rows], layer_in, grad_out, cols), "col")
    near_in = near_got[:, :CAP].reshape(rows, width)
    near_grad = near_got[:, CAP:].reshape(rows, width)

    gate_full = both_halves(gate_weight[0], 0)
    up_full = both_halves(up_weight[0], 0)
    down_full = both_halves(down_weight[0], 1)

    far_ins = [far_in] + [rotated(far_in, s) for s in range(1, n)]
    far_grads = [far_grad] + [rotated(far_grad, s) for s in range(1, n)]

    act, d_gate, d_up = unit_gradients(
        dot(near_in, gate_full, 1, 0),
        dot(near_in, up_full, 1, 0),
        dot(near_grad, down_full, 1, 1),
    )
    near_rows = reduced_rows(d_gate, d_up, gate_full, up_full, part)

    gate = up = dhid = 0.0
    for s in range(n):
        q = (t - s) % n
        gate = gate + dot(far_ins[s], cut(gate_full, q, part, 0), 1, 0)
        up = up + dot(far_ins[s], cut(up_full, q, part, 0), 1, 0)
        dhid = dhid + dot(far_grads[s], cut(down_full, q, part, 1), 1, 1)
    far_act, far_d_gate, far_d_up = unit_gradients(gate, up, dhid)
    far_rows = reduced_rows(far_d_gate, far_d_up, gate_full, up_full, part)

    first = my_zh == 0
    back = jnp.stack(
        [jnp.where(first, near_rows, far_rows), jnp.where(first, far_rows, near_rows)]
    )
    back = exchange(back.reshape(2 * cols, CAP, part), ("zh", "col"))
    back = back.reshape(2, rows, part)
    total = dot(near_picker, cut(back, my_zh, 1, 0)[0], 0, 0) + dot(
        far_picker, cut(back, 1 - my_zh, 1, 0)[0], 0, 0
    )
    total = total.astype(BF)

    far_in_all, far_grad_all = jnp.stack(far_ins), jnp.stack(far_grads)

    def quarter(stacked, q):
        return cut(stacked, (t - q) % n, 1, 0)[0]

    def in_term(h, near_d, far_d):
        near = dot(cut(near_in, h, half, 1), near_d, 0, 0)
        far = [dot(quarter(far_in_all, per_half * h + k), far_d, 0, 0) for k in range(per_half)]
        return ((near + jnp.concatenate(far, axis=0)) * 0.25).astype(BF)

    def down_term(h, near_a, far_a):
        near = dot(near_a, cut(near_grad, h, half, 1), 0, 0)
        far = [dot(far_a, quarter(far_grad_all, per_half * h + k), 0, 0) for k in range(per_half)]
        return ((near + jnp.concatenate(far, axis=1)) * 0.25).astype(BF)

    def finish(term, near_side, far_side):
        got_term = swap(term(1 - my_dp, near_side, far_side), "dp")
        return (term(my_dp, near_side, far_side).astype(F32) + got_term.astype(F32)).astype(BF)

    grad_gate = finish(in_term, d_gate, far_d_gate)
    grad_up = finish(in_term, d_up, far_d_up)
    grad_down = finish(down_term, act, far_act)
    total, grad_gate, grad_up, grad_down = lax.optimization_barrier(
        (total, grad_gate, grad_up, grad_down)
    )
    total = lax.all_gather(total, "tensor", axis=0, tiled=False)
    total = jnp.transpose(total, (1, 0, 2)).reshape(tokens, width)
    return total, grad_gate[None], grad_up[None], grad_down[None]


def solution(mesh):
    n_dp, n_expert, n_tensor = (mesh.shape[a] for a in ("dp", "expert", "tensor"))
    split = Mesh(
        mesh.devices.reshape(n_dp, 2, n_expert // 2, n_tensor), ("dp", "zh", "col", "tensor")
    )
    blocks = P(("dp", "zh", "col"), None)
    by_rows = P(("zh", "col"), "dp", "tensor")
    by_columns = P(("zh", "col"), "tensor", "dp")
    return jax.shard_map(
        inner,
        mesh=split,
        in_specs=(blocks, blocks, blocks, blocks, by_rows, by_rows, by_columns),
        out_specs=(blocks, by_rows, by_rows, by_columns),
        check_vma=False,
    )
```

time: 214 us -> 202 us (0.944)
  the two profiles are of different devices: /device:TPU:1 before, /device:TPU:2 now
where the time goes in v2:
time: 202 us; the launch traced here: 201 us
  waiting for transfers between devices  58 us (29%)
  starting transfers between devices  48.1 us (24%)
  matrix products  44.3 us (22%)
  blocking collectives  36.1 us (18%)
  other arithmetic  7.23 us (4%)
  local copies, waits for them, and re-layouts  5.72 us (3%)
    ppermute x12, waiting for transfers between devices, rotated(): return lax.ppermute(x, 'tensor', [(i, (i + step) % n) for i in range(n)])  45 us
    dot_general x51, matrix products, dot(): lax.dot_general(a, b, (((ca,), (cb,)), ((), ())), preferred_element_type=...  42 us
    ppermute x12, starting transfers between devices, rotated(): return lax.ppermute(x, 'tensor', [(i, (i + step) % n) for i in range(n)])  23.9 us
    all_gather x1, blocking collectives, inner(): total = lax.all_gather(total, 'tensor', axis=0, tiled=False)  19.2 us
    all_to_all x1, blocking collectives, exchange(): return lax.all_to_all(x, axes, split_axis=0, concat_axis=0, tiled=True)  16.8 us
    all_to_all x2, starting transfers between devices, exchange(): return lax.all_to_all(x, axes, split_axis=0, concat_axis=0, tiled=True)  16.8 us
    ppermute x8, waiting for transfers between devices, swap(): return lax.ppermute(x, axis, [(0, 1), (1, 0)])  7.69 us
    ppermute x8, starting transfers between devices, swap(): return lax.ppermute(x, axis, [(0, 1), (1, 0)])  7.39 us
  transfers between devices with their start and end apart: 22, of which 11 were waited for; matrix products, arithmetic and copies ran while one was open for 21% of the time, Pallas kernels for 0%

profile of v2, /device:TPU:2, one launch (start us, length us, event | category | flops | bytes accessed | tf_op | source)
XLA Modules:
  0.0 200.8 jit_solution(1508388640451797599)
XLA Ops:
  0.7 0.9 fusion.134
  1.8 0.9 fusion.199
  2.8 1.2 fusion.36
  4.3 16.8 %all_to_all.15 = bf16[16,16,896]{2,1,0:T(8,128)(2,1)S(1)} all-to-all(bf16[16,16,896]{2,1,0:T(8,128)(2,1)S(1)} %pad_maximum_fusion.6), channel_id=1, replica_groups=mesh['dp'=2,'zh'=2,'col'=16,'tensor'=4] {'col'}, dimensions={0} | all-to-all | bytes 917504 | tf_op jit(solution)/shard_map/all_to_all | solution.py:60
  21.1 7.3 %collective-permute-start.10 = (bf16[128,896]{1,0:T(8,128)(2,1)S(1)}, bf16[128,896]{1,0:T(8,128)(2,1)S(1)}, u32[]{:S(2)}, u32[]{:S(2)}) collective-permute-start(bf16[128,896]{1,0:T(8,128)(2,1)S(1)} %get-tuple-element.22), channel_id=1, source_target_pairs={{0,64},{64,0},{1,65},{65,1},{2,66},{66,2},{3,67},{67,3},{4,68},{68... | collective-permute-start | bytes 688136 | tf_op jit(solution)/shard_map/ppermute | solution.py:46
  28.6 6.9 %collective-permute-done.10 = bf16[128,896]{1,0:T(8,128)(2,1)S(1)} collective-permute-done((bf16[128,896]{1,0:T(8,128)(2,1)S(1)}, bf16[128,896]{1,0:T(8,128)(2,1)S(1)}, u32[]{:S(2)}, u32[]{:S(2)}) %collective-permute-start.10) | collective-permute-done | bytes 229408 | tf_op jit(solution)/shard_map/ppermute | solution.py:46
  35.5 6.4 %collective-permute-start.13 = (bf16[128,896]{1,0:T(8,128)(2,1)S(1)}, bf16[128,896]{1,0:T(8,128)(2,1)S(1)}, u32[]{:S(2)}, u32[]{:S(2)}) collective-permute-start(bf16[128,896]{1,0:T(8,128)(2,1)S(1)} %collective-permute-done.10), channel_id=1, source_target_pairs={{0,3},{1,0},{2,1},{3,2},{4,7},{5,4},{6,5},{7,6},{8,11},{9,8},{10,9... | collective-permute-start | bytes 688136 | tf_op jit(solution)/shard_map/ppermute | solution.py:65
  41.9 3.6 %collective-permute-start.11 = (bf16[128,896]{1,0:T(8,128)(2,1)S(1)}, bf16[128,896]{1,0:T(8,128)(2,1)S(1)}, u32[]{:S(2)}, u32[]{:S(2)}) collective-permute-start(bf16[128,896]{1,0:T(8,128)(2,1)S(1)} %collective-permute-done.10), channel_id=1, source_target_pairs={{0,1},{1,2},{2,3},{3,0},{4,5},{5,6},{6,7},{7,4},{8,9},{9,10},{10,1... | collective-permute-start | bytes 688136 | tf_op jit(solution)/shard_map/ppermute | solution.py:65
  45.5 1.9 collective-permute-start.12
  47.4 0.4 fusion.3
  47.8 0.8 collective-permute-done.6
  48.6 0.4 fusion.2
  49.0 10.6 %collective-permute-done.13 = bf16[128,896]{1,0:T(8,128)(2,1)S(1)} collective-permute-done((bf16[128,896]{1,0:T(8,128)(2,1)S(1)}, bf16[128,896]{1,0:T(8,128)(2,1)S(1)}, u32[]{:S(2)}, u32[]{:S(2)}) %collective-permute-start.13) | collective-permute-done | bytes 229408 | tf_op jit(solution)/shard_map/ppermute | solution.py:65
  59.6 5.0 %collective-permute-start.7 = (bf16[128,896]{1,0:T(8,128)(2,1)S(1)}, bf16[128,896]{1,0:T(8,128)(2,1)S(1)}, u32[]{:S(2)}, u32[]{:S(2)}) collective-permute-start(bf16[128,896]{1,0:T(8,128)(2,1)S(1)} %collective-permute-done.6), channel_id=1, source_target_pairs={{0,1},{1,2},{2,3},{3,0},{4,5},{5,6},{6,7},{7,4},{8,9},{9,10},{10,1... | collective-permute-start | bytes 688136 | tf_op jit(solution)/shard_map/ppermute | solution.py:65
  64.6 9.3 %collective-permute-done.12 = bf16[128,896]{1,0:T(8,128)(2,1)S(1)} collective-permute-done((bf16[128,896]{1,0:T(8,128)(2,1)S(1)}, bf16[128,896]{1,0:T(8,128)(2,1)S(1)}, u32[]{:S(2)}, u32[]{:S(2)}) %collective-permute-start.12) | collective-permute-done | bytes 229408 | tf_op jit(solution)/shard_map/ppermute | solution.py:65
  73.9 1.4 pad_maximum_fusion
  75.3 5.6 %all-to-all-start = ((bf16[16,16,3584]{2,1,0:T(8,128)(2,1)}), bf16[16,16,3584]{2,1,0:T(8,128)(2,1)}, u32[]{:S(2)}, u32[]{:S(2)}) async-start(bf16[16,16,3584]{2,1,0:T(8,128)(2,1)} %pad_maximum_fusion), calls=%async_computation | async-start | bytes 3670016 | tf_op jit(solution)/shard_map/all_to_all | solution.py:60
  81.1 1.1 copy-done.32
  82.2 5.4 %collective-permute-done.8 = bf16[128,896]{1,0:T(8,128)(2,1)S(1)} collective-permute-done((bf16[128,896]{1,0:T(8,128)(2,1)S(1)}, bf16[128,896]{1,0:T(8,128)(2,1)S(1)}, u32[]{:S(2)}, u32[]{:S(2)}) %collective-permute-start.8) | collective-permute-done | bytes 229408 | tf_op jit(solution)/shard_map/ppermute | solution.py:65
  87.7 2.3 %broadcast_select_fusion.1 = (bf16[1792,256]{1,0:T(8,128)(2,1)S(1)}, bf16[1792,256]{1,0:T(8,128)(2,1)S(1)}, bf16[1792,256]{1,0:T(8,128)(2,1)S(1)}, bf16[1792,256]{1,0:T(8,128)(2,1)S(1)}) fusion(bf16[1792,256]{1,0:T(8,128)(2,1)} %collective-permute-done.2, pred[]{:T(512)S(6)} %eq.64, bf16[1,1792,256]{2,1,0:T(8,128)(2,1)} %param.11, ...), kind=kLoop, calls=%fused_computation.78 | loop fusion | flops 1835008 | bytes 7340033 | tf_op jit(solution)/shard_map/jit(_where)/select_n | solution.py:54
  91.1 0.5 copy-done.27
  93.1 0.3 convolution_add_fusion.20
  94.0 0.3 fusion.39
  94.6 1.2 fusion.99
  95.8 1.2 fusion.103
  97.0 1.3 fusion.97
  98.3 1.3 fusion.101
  99.6 1.2 fusion.107
  100.9 1.3 fusion.105
  102.7 2.5 %collective-permute-start.16 = (bf16[128,896]{1,0:T(8,128)(2,1)S(1)}, bf16[128,896]{1,0:T(8,128)(2,1)S(1)}, u32[]{:S(2)}, u32[]{:S(2)}) collective-permute-start(bf16[128,896]{1,0:T(8,128)(2,1)S(1)} %fusion.34), channel_id=1, source_target_pairs={{0,3},{1,0},{2,1},{3,2},{4,7},{5,4},{6,5},{7,6},{8,11},{9,8},{10,9... | collective-permute-start | bytes 688136 | tf_op jit(solution)/shard_map/ppermute | solution.py:65
  106.5 0.6 collective-permute-start.14
  107.2 1.2 fusion.111
  108.4 1.2 fusion.109
  109.6 1.3 fusion.89
  110.9 1.2 fusion.91
  112.1 1.2 fusion.93
  113.7 3.0 %collective-permute-done.15 = bf16[128,896]{1,0:T(8,128)(2,1)S(1)} collective-permute-done((bf16[128,896]{1,0:T(8,128)(2,1)S(1)}, bf16[128,896]{1,0:T(8,128)(2,1)S(1)}, u32[]{:S(2)}, u32[]{:S(2)}) %collective-permute-start.15) | collective-permute-done | bytes 229408 | tf_op jit(solution)/shard_map/ppermute | solution.py:65
  116.7 8.0 %collective-permute-done.14 = bf16[128,896]{1,0:T(8,128)(2,1)S(1)} collective-permute-done((bf16[128,896]{1,0:T(8,128)(2,1)S(1)}, bf16[128,896]{1,0:T(8,128)(2,1)S(1)}, u32[]{:S(2)}, u32[]{:S(2)}) %collective-permute-start.14) | collective-permute-done | bytes 229408 | tf_op jit(solution)/shard_map/ppermute | solution.py:65
  124.7 1.0 fusion.26
  125.7 1.7 fusion.196
  127.5 2.0 %fusion.195 = f32[128,256]{1,0:T(8,128)S(1)} fusion(bf16[256,3584]{1,0:T(8,128)(2,1)S(1)} %copy-done.4, bf16[16,16,3584]{2,1,0:T(8,128)(2,1)} %all-to-all-done), kind=kOutput, calls=%fused_computation.261 | convolution fusion | flops 234881024 | bytes 2883584 | tf_op jit(solution)/shard_map/dot_general | solution.py:14
  129.5 1.6 multiply_convert_fusion.1
  132.3 2.8 %collective-permute-start.5 = (bf16[128,896]{1,0:T(8,128)(2,1)S(1)}, bf16[128,896]{1,0:T(8,128)(2,1)S(1)}, u32[]{:S(2)}, u32[]{:S(2)}) collective-permute-start(bf16[128,896]{1,0:T(8,128)(2,1)S(1)} %fusion.31), channel_id=1, source_target_pairs={{0,3},{1,0},{2,1},{3,2},{4,7},{5,4},{6,5},{7,6},{8,11},{9,8},{10,9... | collective-permute-start | bytes 688136 | tf_op jit(solution)/shard_map/ppermute | solution.py:65
  135.5 0.3 fusion.29
  135.9 0.9 collective-permute-start.3
  136.7 1.6 slice_bitcast_fusion.1
  138.4 1.4 fusion.12
  139.7 0.5 copy-done.14
  140.2 0.6 copy-done.15
  140.8 1.4 fusion.15
  142.2 1.4 fusion.18
  143.8 1.5 collective-permute-done.5
  145.3 0.8 collective-permute-done.4
  146.1 6.6 %collective-permute-done.3 = bf16[128,896]{1,0:T(8,128)(2,1)S(1)} collective-permute-done((bf16[128,896]{1,0:T(8,128)(2,1)S(1)}, bf16[128,896]{1,0:T(8,128)(2,1)S(1)}, u32[]{:S(2)}, u32[]{:S(2)}) %collective-permute-start.3) | collective-permute-done | bytes 229408 | tf_op jit(solution)/shard_map/ppermute | solution.py:65
  152.6 0.4 select_bitcast_fusion.1
  153.0 0.9 pad_maximum_fusion.7
  153.9 11.2 %all-to-all-start.2 = ((bf16[32,8,896]{2,1,0:T(8,128)(2,1)}), bf16[32,8,896]{2,1,0:T(8,128)(2,1)S(1)}, u32[]{:S(2)}, u32[]{:S(2)}) async-start(bf16[32,8,896]{2,1,0:T(8,128)(2,1)} %bitcast.17), calls=%async_computation.2 | async-start | bytes 917504 | tf_op jit(solution)/shard_map/all_to_all | solution.py:60
  165.1 1.3 fusion.95
  166.4 3.0 %add_convert_fusion.2 = bf16[1792,256]{1,0:T(8,128)(2,1)} fusion(bf16[1792,256]{1,0:T(8,128)(2,1)} %collective-permute-done.17, f32[896,256]{1,0:T(8,128)S(1)} %copy-done.10, f32[896,256]{1,0:T(8,128)} %fusion.111, bf16[128,256]{1,0:T(8,128)(2,1)S(1)} %get-tuple-element.28, bf16[128,3584]{1,0:T(8,128)(2,1)S(1)} %copy-done.6, s32[]{:T(128)S(6)} %select_n.233), kind=kOutput, calls=%fused_computation.33 | convolution fusion | flops 121110528 | bytes 4194308 | tf_op jit(solution)/shard_map/dot_general | solution.py:14
  169.4 2.7 %add_convert_fusion.1 = bf16[1792,256]{1,0:T(8,128)(2,1)} fusion(bf16[1792,256]{1,0:T(8,128)(2,1)} %collective-permute-done.18, f32[896,256]{1,0:T(8,128)S(1)} %copy-done.9, f32[896,256]{1,0:T(8,128)S(1)} %copy-done.12, bf16[128,256]{1,0:T(8,128)(2,1)S(1)} %get-tuple-element.29, bf16[128,3584]{1,0:T(8,128)(2,1)S(1)} %copy-done.6, s32[]{:T(128)S(6)} %select_n.233), kind=kOutput, calls=%fused_computation.32 | convolution fusion | flops 121110528 | bytes 4194308 | tf_op jit(solution)/shard_map/dot_general | solution.py:14
  172.1 2.6 %add_convert_fusion = bf16[256,1792]{1,0:T(8,128)(2,1)} fusion(bf16[256,1792]{1,0:T(8,128)(2,1)} %collective-permute-done.19, f32[256,896]{1,0:T(8,128)S(1)} %copy-done.11, f32[256,896]{1,0:T(8,128)S(1)} %fusion.95, bf16[128,256]{1,0:T(8,128)(2,1)S(1)} %get-tuple-element.27, bf16[128,3584]{1,0:T(8,128)(2,1)S(1)} %copy-done.8, s32[]{:T(128)S(6)} %select_n.233), kind=kOutput, calls=%fused_computation.31 | convolution fusion | flops 121110528 | bytes 4194308 | tf_op jit(solution)/shard_map/dot_general | solution.py:14
  174.7 5.3 %all-to-all-done.2 = bf16[32,8,896]{2,1,0:T(8,128)(2,1)S(1)} async-done(((bf16[32,8,896]{2,1,0:T(8,128)(2,1)}), bf16[32,8,896]{2,1,0:T(8,128)(2,1)S(1)}, u32[]{:S(2)}, u32[]{:S(2)}) %all-to-all-start.2) | async-done | bytes 458784 | tf_op jit(solution)/shard_map/all_to_all | solution.py:60
  180.6 19.2 %all-gather = bf16[512,896]{1,0:T(8,128)(2,1)S(1)} all-gather(bf16[128,896]{1,0:T(8,128)(2,1)S(1)} %fusion.28), channel_id=2, replica_groups=mesh['dp'=2,'zh'=2,'col'=16,'tensor'=4] {'tensor'}, dimensions={0}, use_global_device_ids=true | all-gather | bytes 1146880 | tf_op jit(solution)/shard_map/all_gather | solution.py:180
  199.8 1.0 copy.14
  (128 shorter events, 9.0 us)
Async XLA Ops:
  0.6 3.3 %copy-start = (bf16[128,3584]{1,0:T(8,128)(2,1)S(1)}, bf16[128,3584]{1,0:T(8,128)(2,1)}, u32[]{:S(2)}) copy-start(bf16[128,3584]{1,0:T(8,128)(2,1)} %param.7) | copy-start | bytes 2752516
  4.3 44.4 %copy-start.20 = (bf16[128,3584]{1,0:T(8,128)(2,1)S(1)}, bf16[128,3584]{1,0:T(8,128)(2,1)}, u32[]{:S(2)}) copy-start(bf16[128,3584]{1,0:T(8,128)(2,1)} %param.8) | copy-start | bytes 2752516
  21.1 14.3 %collective-permute-start.10 = (bf16[128,896]{1,0:T(8,128)(2,1)S(1)}, bf16[128,896]{1,0:T(8,128)(2,1)S(1)}, u32[]{:S(2)}, u32[]{:S(2)}) collective-permute-start(bf16[128,896]{1,0:T(8,128)(2,1)S(1)} %get-tuple-element.22), channel_id=1, source_target_pairs={{0,64},{64,0},{1,65},{65,1},{2,66},{66,2},{3,67},{67,3},{4,68},{68... | collective-permute-start | bytes 688136 | tf_op jit(solution)/shard_map/ppermute | solution.py:46
  28.4 20.2 %collective-permute-start.6 = (bf16[128,896]{1,0:T(8,128)(2,1)S(1)}, bf16[128,896]{1,0:T(8,128)(2,1)S(1)}, u32[]{:S(2)}, u32[]{:S(2)}) collective-permute-start(bf16[128,896]{1,0:T(8,128)(2,1)S(1)} %get-tuple-element.23), channel_id=1, source_target_pairs={{0,64},{64,0},{1,65},{65,1},{2,66},{66,2},{3,67},{67,3},{4,68},{68... | collective-permute-start | bytes 688136 | tf_op jit(solution)/shard_map/ppermute | solution.py:46
  28.5 59.2 %collective-permute-start.2 = (bf16[1792,256]{1,0:T(8,128)(2,1)}, bf16[1792,256]{1,0:T(8,128)(2,1)}, u32[]{:S(2)}, u32[]{:S(2)}) collective-permute-start(bf16[1792,256]{1,0:T(8,128)(2,1)} %bitcast.9), channel_id=1, source_target_pairs={{0,128},{128,0},{1,129},{129,1},{2,130},{130,2},{3,131},{131,3},{4... | collective-permute-start | bytes 2752520 | tf_op jit(solution)/shard_map/ppermute | solution.py:46
  35.5 24.1 %collective-permute-start.13 = (bf16[128,896]{1,0:T(8,128)(2,1)S(1)}, bf16[128,896]{1,0:T(8,128)(2,1)S(1)}, u32[]{:S(2)}, u32[]{:S(2)}) collective-permute-start(bf16[128,896]{1,0:T(8,128)(2,1)S(1)} %collective-permute-done.10), channel_id=1, source_target_pairs={{0,3},{1,0},{2,1},{3,2},{4,7},{5,4},{6,5},{7,6},{8,11},{9,8},{10,9... | collective-permute-start | bytes 688136 | tf_op jit(solution)/shard_map/ppermute | solution.py:65
  41.9 17.7 %collective-permute-start.11 = (bf16[128,896]{1,0:T(8,128)(2,1)S(1)}, bf16[128,896]{1,0:T(8,128)(2,1)S(1)}, u32[]{:S(2)}, u32[]{:S(2)}) collective-permute-start(bf16[128,896]{1,0:T(8,128)(2,1)S(1)} %collective-permute-done.10), channel_id=1, source_target_pairs={{0,1},{1,2},{2,3},{3,0},{4,5},{5,6},{6,7},{7,4},{8,9},{9,10},{10,1... | collective-permute-start | bytes 688136 | tf_op jit(solution)/shard_map/ppermute | solution.py:65
  45.5 28.4 %collective-permute-start.12 = (bf16[128,896]{1,0:T(8,128)(2,1)S(1)}, bf16[128,896]{1,0:T(8,128)(2,1)S(1)}, u32[]{:S(2)}, u32[]{:S(2)}) collective-permute-start(bf16[128,896]{1,0:T(8,128)(2,1)S(1)} %collective-permute-done.10), channel_id=1, source_target_pairs={{0,2},{1,3},{2,0},{3,1},{4,6},{5,7},{6,4},{7,5},{8,10},{9,11},{10,... | collective-permute-start | bytes 688136 | tf_op jit(solution)/shard_map/ppermute | solution.py:65
  48.6 38.9 %copy-start.22 = (bf16[128,896]{1,0:T(8,128)(2,1)}, bf16[128,896]{1,0:T(8,128)(2,1)S(1)}, u32[]{:S(2)}) copy-start(bf16[128,896]{1,0:T(8,128)(2,1)S(1)} %collective-permute-done.6) | copy-start | bytes 688132
  48.6 39.1 %collective-permute-start.1 = (bf16[1792,256]{1,0:T(8,128)(2,1)}, bf16[1792,256]{1,0:T(8,128)(2,1)}, u32[]{:S(2)}, u32[]{:S(2)}) collective-permute-start(bf16[1792,256]{1,0:T(8,128)(2,1)} %bitcast.169), channel_id=1, source_target_pairs={{0,128},{128,0},{1,129},{129,1},{2,130},{130,2},{3,131},{131,3},{4... | collective-permute-start | bytes 2752520 | tf_op jit(solution)/shard_map/ppermute | solution.py:46
  59.6 21.5 %collective-permute-start.9 = (bf16[128,896]{1,0:T(8,128)(2,1)S(1)}, bf16[128,896]{1,0:T(8,128)(2,1)S(1)}, u32[]{:S(2)}, u32[]{:S(2)}) collective-permute-start(bf16[128,896]{1,0:T(8,128)(2,1)S(1)} %collective-permute-done.6), channel_id=1, source_target_pairs={{0,3},{1,0},{2,1},{3,2},{4,7},{5,4},{6,5},{7,6},{8,11},{9,8},{10,9... | collective-permute-start | bytes 688136 | tf_op jit(solution)/shard_map/ppermute | solution.py:65
  59.6 22.6 %collective-permute-start.7 = (bf16[128,896]{1,0:T(8,128)(2,1)S(1)}, bf16[128,896]{1,0:T(8,128)(2,1)S(1)}, u32[]{:S(2)}, u32[]{:S(2)}) collective-permute-start(bf16[128,896]{1,0:T(8,128)(2,1)S(1)} %collective-permute-done.6), channel_id=1, source_target_pairs={{0,1},{1,2},{2,3},{3,0},{4,5},{5,6},{6,7},{7,4},{8,9},{9,10},{10,1... | collective-permute-start | bytes 688136 | tf_op jit(solution)/shard_map/ppermute | solution.py:65
  73.9 7.0 %copy-start.28 = (bf16[128,896]{1,0:T(8,128)(2,1)}, bf16[128,896]{1,0:T(8,128)(2,1)S(1)}, u32[]{:S(2)}) copy-start(bf16[128,896]{1,0:T(8,128)(2,1)S(1)} %collective-permute-done.12) | copy-start | bytes 688132
  73.9 13.7 %collective-permute-start.8 = (bf16[128,896]{1,0:T(8,128)(2,1)S(1)}, bf16[128,896]{1,0:T(8,128)(2,1)S(1)}, u32[]{:S(2)}, u32[]{:S(2)}) collective-permute-start(bf16[128,896]{1,0:T(8,128)(2,1)S(1)} %collective-permute-done.6), channel_id=1, source_target_pairs={{0,2},{1,3},{2,0},{3,1},{4,6},{5,7},{6,4},{7,5},{8,10},{9,11},{10,... | collective-permute-start | bytes 688136 | tf_op jit(solution)/shard_map/ppermute | solution.py:65
  75.3 50.4 %all-to-all-start = ((bf16[16,16,3584]{2,1,0:T(8,128)(2,1)}), bf16[16,16,3584]{2,1,0:T(8,128)(2,1)}, u32[]{:S(2)}, u32[]{:S(2)}) async-start(bf16[16,16,3584]{2,1,0:T(8,128)(2,1)} %pad_maximum_fusion), calls=%async_computation | async-start | bytes 3670016 | tf_op jit(solution)/shard_map/all_to_all | solution.py:60
  80.9 1.3 copy-start.32
  80.9 6.8 %copy-start.33 = (bf16[1,1792,256]{2,1,0:T(8,128)(2,1)S(1)}, bf16[1,1792,256]{2,1,0:T(8,128)(2,1)}, u32[]{:S(2)}) copy-start(bf16[1,1792,256]{2,1,0:T(8,128)(2,1)} %param.12) | copy-start | bytes 2752516
  81.1 8.9 %copy-start.26 = (bf16[128,896]{1,0:T(8,128)(2,1)}, bf16[128,896]{1,0:T(8,128)(2,1)S(1)}, u32[]{:S(2)}) copy-start(bf16[128,896]{1,0:T(8,128)(2,1)S(1)} %collective-permute-done.9) | copy-start | bytes 688132
  82.2 8.0 %collective-permute-start = (bf16[256,1792]{1,0:T(8,128)(2,1)S(1)}, bf16[256,1792]{1,0:T(8,128)(2,1)S(1)}, u32[]{:S(2)}, u32[]{:S(2)}) collective-permute-start(bf16[256,1792]{1,0:T(8,128)(2,1)S(1)} %bitcast.168), channel_id=1, source_target_pairs={{0,128},{128,0},{1,129},{129,1},{2,130},{130,2},{3,131},{131,3},{4... | collective-permute-start | bytes 2752520 | tf_op jit(solution)/shard_map/ppermute | solution.py:46
  82.2 7.8 %copy-start.24 = (bf16[128,896]{1,0:T(8,128)(2,1)}, bf16[128,896]{1,0:T(8,128)(2,1)S(1)}, u32[]{:S(2)}) copy-start(bf16[128,896]{1,0:T(8,128)(2,1)S(1)} %collective-permute-done.7) | copy-start | bytes 688132
  87.5 2.5 %copy-start.30 = (bf16[128,896]{1,0:T(8,128)(2,1)}, bf16[128,896]{1,0:T(8,128)(2,1)S(1)}, u32[]{:S(2)}) copy-start(bf16[128,896]{1,0:T(8,128)(2,1)S(1)} %collective-permute-done.8) | copy-start | bytes 688132
  87.7 24.5 %copy-start.13 = (bf16[4,128,896]{2,1,0:T(8,128)(2,1)}, bf16[4,128,896]{2,1,0:T(8,128)(2,1)S(1)}, u32[]{:S(2)}) copy-start(bf16[4,128,896]{2,1,0:T(8,128)(2,1)S(1)} %pad_maximum_fusion.5) | copy-start | bytes 2752516
  90.4 3.5 %copy-start.3 = (bf16[256,3584]{1,0:T(8,128)(2,1)}, bf16[256,3584]{1,0:T(8,128)(2,1)S(1)}, u32[]{:S(2)}) copy-start(bf16[256,3584]{1,0:T(8,128)(2,1)S(1)} %pad_maximum_fusion.1) | copy-start | bytes 5505028
  90.5 1.2 copy-start.27
  90.6 22.8 %copy-start.1 = (bf16[3584,256]{1,0:T(8,128)(2,1)}, bf16[3584,256]{1,0:T(8,128)(2,1)S(1)}, u32[]{:S(2)}) copy-start(bf16[3584,256]{1,0:T(8,128)(2,1)S(1)} %pad_maximum_fusion.2) | copy-start | bytes 5505028
  90.6 1.4 copy-start.23
  92.0 1.1 copy-start.25
  92.6 1.1 copy-start.29
  92.9 1.1 copy-start.31
  102.7 10.9 %collective-permute-start.16 = (bf16[128,896]{1,0:T(8,128)(2,1)S(1)}, bf16[128,896]{1,0:T(8,128)(2,1)S(1)}, u32[]{:S(2)}, u32[]{:S(2)}) collective-permute-start(bf16[128,896]{1,0:T(8,128)(2,1)S(1)} %fusion.34), channel_id=1, source_target_pairs={{0,3},{1,0},{2,1},{3,2},{4,7},{5,4},{6,5},{7,6},{8,11},{9,8},{10,9... | collective-permute-start | bytes 688136 | tf_op jit(solution)/shard_map/ppermute | solution.py:65
  105.8 10.9 %collective-permute-start.15 = (bf16[128,896]{1,0:T(8,128)(2,1)S(1)}, bf16[128,896]{1,0:T(8,128)(2,1)S(1)}, u32[]{:S(2)}, u32[]{:S(2)}) collective-permute-start(bf16[128,896]{1,0:T(8,128)(2,1)S(1)} %fusion.33), channel_id=1, source_target_pairs={{0,1},{1,2},{2,3},{3,0},{4,5},{5,6},{6,7},{7,4},{8,9},{9,10},{10,1... | collective-permute-start | bytes 688136 | tf_op jit(solution)/shard_map/ppermute | solution.py:65
  106.5 18.2 %collective-permute-start.14 = (bf16[128,896]{1,0:T(8,128)(2,1)S(1)}, bf16[128,896]{1,0:T(8,128)(2,1)S(1)}, u32[]{:S(2)}, u32[]{:S(2)}) collective-permute-start(bf16[128,896]{1,0:T(8,128)(2,1)S(1)} %fusion.32), channel_id=1, source_target_pairs={{0,2},{1,3},{2,0},{3,1},{4,6},{5,7},{6,4},{7,5},{8,10},{9,11},{10,... | collective-permute-start | bytes 688136 | tf_op jit(solution)/shard_map/ppermute | solution.py:65
  125.7 1.8 copy-start.4
  127.5 2.0 %copy-start.2 = (bf16[3584,256]{1,0:T(8,128)(2,1)S(1)}, bf16[3584,256]{1,0:T(8,128)(2,1)}, u32[]{:S(2)}) copy-start(bf16[3584,256]{1,0:T(8,128)(2,1)} %copy-done.1) | copy-start | bytes 5505028
  132.3 13.0 %collective-permute-start.5 = (bf16[128,896]{1,0:T(8,128)(2,1)S(1)}, bf16[128,896]{1,0:T(8,128)(2,1)S(1)}, u32[]{:S(2)}, u32[]{:S(2)}) collective-permute-start(bf16[128,896]{1,0:T(8,128)(2,1)S(1)} %fusion.31), channel_id=1, source_target_pairs={{0,3},{1,0},{2,1},{3,2},{4,7},{5,4},{6,5},{7,6},{8,11},{9,8},{10,9... | collective-permute-start | bytes 688136 | tf_op jit(solution)/shard_map/ppermute | solution.py:65
  135.4 10.6 %collective-permute-start.4 = (bf16[128,896]{1,0:T(8,128)(2,1)S(1)}, bf16[128,896]{1,0:T(8,128)(2,1)S(1)}, u32[]{:S(2)}, u32[]{:S(2)}) collective-permute-start(bf16[128,896]{1,0:T(8,128)(2,1)S(1)} %fusion.30), channel_id=1, source_target_pairs={{0,1},{1,2},{2,3},{3,0},{4,5},{5,6},{6,7},{7,4},{8,9},{9,10},{10,1... | collective-permute-start | bytes 688136 | tf_op jit(solution)/shard_map/ppermute | solution.py:65
  135.9 2.5 %copy-start.16 = (f32[896,256]{1,0:T(8,128)S(1)}, f32[896,256]{1,0:T(8,128)}, u32[]{:S(2)}) copy-start(f32[896,256]{1,0:T(8,128)} %fusion.99) | copy-start | bytes 2752516
  135.9 2.5 %copy-start.17 = (f32[896,256]{1,0:T(8,128)S(1)}, f32[896,256]{1,0:T(8,128)}, u32[]{:S(2)}) copy-start(f32[896,256]{1,0:T(8,128)} %fusion.103) | copy-start | bytes 2752516
  135.9 16.7 %collective-permute-start.3 = (bf16[128,896]{1,0:T(8,128)(2,1)S(1)}, bf16[128,896]{1,0:T(8,128)(2,1)S(1)}, u32[]{:S(2)}, u32[]{:S(2)}) collective-permute-start(bf16[128,896]{1,0:T(8,128)(2,1)S(1)} %fusion.29), channel_id=1, source_target_pairs={{0,2},{1,3},{2,0},{3,1},{4,6},{5,7},{6,4},{7,5},{8,10},{9,11},{10,... | collective-permute-start | bytes 688136 | tf_op jit(solution)/shard_map/ppermute | solution.py:65
  138.3 3.8 %copy-start.5 = (bf16[128,3584]{1,0:T(8,128)(2,1)}, bf16[128,3584]{1,0:T(8,128)(2,1)S(1)}, u32[]{:S(2)}) copy-start(bf16[128,3584]{1,0:T(8,128)(2,1)S(1)} %get-tuple-element.13) | copy-start | bytes 2752516
  138.3 3.8 %copy-start.7 = (bf16[128,3584]{1,0:T(8,128)(2,1)}, bf16[128,3584]{1,0:T(8,128)(2,1)S(1)}, u32[]{:S(2)}) copy-start(bf16[128,3584]{1,0:T(8,128)(2,1)S(1)} %get-tuple-element.12) | copy-start | bytes 2752516
  138.3 1.9 copy-start.14
  138.3 2.4 %copy-start.15 = (f32[896,256]{1,0:T(8,128)S(1)}, f32[896,256]{1,0:T(8,128)}, u32[]{:S(2)}) copy-start(f32[896,256]{1,0:T(8,128)} %fusion.101) | copy-start | bytes 2752516
  139.7 2.4 %copy-start.18 = (f32[256,896]{1,0:T(8,128)S(1)}, f32[256,896]{1,0:T(8,128)}, u32[]{:S(2)}) copy-start(f32[256,896]{1,0:T(8,128)} %fusion.89) | copy-start | bytes 2752516
  139.7 2.4 %copy-start.19 = (f32[256,896]{1,0:T(8,128)S(1)}, f32[256,896]{1,0:T(8,128)}, u32[]{:S(2)}) copy-start(f32[256,896]{1,0:T(8,128)} %fusion.91) | copy-start | bytes 2752516
  139.7 26.6 %collective-permute-start.17 = (bf16[1792,256]{1,0:T(8,128)(2,1)}, bf16[1792,256]{1,0:T(8,128)(2,1)}, u32[]{:S(2)}, u32[]{:S(2)}) collective-permute-start(bf16[1792,256]{1,0:T(8,128)(2,1)} %fusion.12), channel_id=1, source_target_pairs={{0,128},{128,0},{1,129},{129,1},{2,130},{130,2},{3,131},{131,3},{4... | collective-permute-start | bytes 2752520 | tf_op jit(solution)/shard_map/ppermute | solution.py:46
  142.1 27.2 %collective-permute-start.18 = (bf16[1792,256]{1,0:T(8,128)(2,1)}, bf16[1792,256]{1,0:T(8,128)(2,1)}, u32[]{:S(2)}, u32[]{:S(2)}) collective-permute-start(bf16[1792,256]{1,0:T(8,128)(2,1)} %fusion.15), channel_id=1, source_target_pairs={{0,128},{128,0},{1,129},{129,1},{2,130},{130,2},{3,131},{131,3},{4... | collective-permute-start | bytes 2752520 | tf_op jit(solution)/shard_map/ppermute | solution.py:46
  142.2 10.4 %copy-start.21 = (bf16[128,896]{1,0:T(8,128)(2,1)S(1)}, bf16[128,896]{1,0:T(8,128)(2,1)}, u32[]{:S(2)}) copy-start(bf16[128,896]{1,0:T(8,128)(2,1)} %fusion.26) | copy-start | bytes 688132
  145.3 26.8 %collective-permute-start.19 = (bf16[256,1792]{1,0:T(8,128)(2,1)}, bf16[256,1792]{1,0:T(8,128)(2,1)}, u32[]{:S(2)}, u32[]{:S(2)}) collective-permute-start(bf16[256,1792]{1,0:T(8,128)(2,1)} %fusion.18), channel_id=1, source_target_pairs={{0,128},{128,0},{1,129},{129,1},{2,130},{130,2},{3,131},{131,3},{4... | collective-permute-start | bytes 2752520 | tf_op jit(solution)/shard_map/ppermute | solution.py:46
  153.0 13.3 %copy-start.6 = (bf16[128,3584]{1,0:T(8,128)(2,1)S(1)}, bf16[128,3584]{1,0:T(8,128)(2,1)}, u32[]{:S(2)}) copy-start(bf16[128,3584]{1,0:T(8,128)(2,1)} %copy-done.5) | copy-start | bytes 2752516
  153.0 13.3 %copy-start.10 = (f32[896,256]{1,0:T(8,128)S(1)}, f32[896,256]{1,0:T(8,128)}, u32[]{:S(2)}) copy-start(f32[896,256]{1,0:T(8,128)} %fusion.107) | copy-start | bytes 2752516
  153.9 26.1 %all-to-all-start.2 = ((bf16[32,8,896]{2,1,0:T(8,128)(2,1)}), bf16[32,8,896]{2,1,0:T(8,128)(2,1)S(1)}, u32[]{:S(2)}, u32[]{:S(2)}) async-start(bf16[32,8,896]{2,1,0:T(8,128)(2,1)} %bitcast.17), calls=%async_computation.2 | async-start | bytes 917504 | tf_op jit(solution)/shard_map/all_to_all | solution.py:60
  166.3 3.0 %copy-start.9 = (f32[896,256]{1,0:T(8,128)S(1)}, f32[896,256]{1,0:T(8,128)}, u32[]{:S(2)}) copy-start(f32[896,256]{1,0:T(8,128)} %fusion.105) | copy-start | bytes 2752516
  166.3 3.0 %copy-start.12 = (f32[896,256]{1,0:T(8,128)S(1)}, f32[896,256]{1,0:T(8,128)}, u32[]{:S(2)}) copy-start(f32[896,256]{1,0:T(8,128)} %fusion.109) | copy-start | bytes 2752516
  169.3 2.8 %copy-start.8 = (bf16[128,3584]{1,0:T(8,128)(2,1)S(1)}, bf16[128,3584]{1,0:T(8,128)(2,1)}, u32[]{:S(2)}) copy-start(bf16[128,3584]{1,0:T(8,128)(2,1)} %copy-done.7) | copy-start | bytes 2752516
  169.3 2.8 %copy-start.11 = (f32[256,896]{1,0:T(8,128)S(1)}, f32[256,896]{1,0:T(8,128)}, u32[]{:S(2)}) copy-start(f32[256,896]{1,0:T(8,128)} %fusion.93) | copy-start | bytes 2752516

commit v3 on v2

--- a/solution.py
+++ b/solution.py
@@ -23,23 +23,25 @@
     experts = labels.shape[0]
     hits = routes_t[None, :, :] == labels[:, None, None]
     chosen = jnp.sum(hits.astype(F32), axis=1)
-    scale = jnp.sum(jnp.where(hits, combine_t[None, :, :], 0.0), axis=1)
     ids = jnp.arange(tokens, dtype=jnp.int32)
     earlier = (ids[:, None] < ids[None, :]).astype(BF)
     before = jnp.dot(chosen.astype(BF), earlier, preferred_element_type=F32)
     slots = jnp.arange(CAP, dtype=F32)
     taken = (before[:, None, :] == slots[None, :, None]) & (chosen[:, None, :] > 0)
+    picker = taken.astype(BF).reshape(experts * CAP, tokens)
+    if combine_t is None:
+        return picker, None
+    scale = jnp.sum(jnp.where(hits, combine_t[None, :, :], 0.0), axis=1)
     factor = jnp.sum(jnp.where(taken, scale[:, None, :], 0.0), axis=2)
-    return taken.astype(BF).reshape(experts * CAP, tokens), factor.reshape(experts * CAP, 1)
-
-
-def picked(picker, factor, layer_in, grad_out, cols):
-    width = layer_in.shape[1]
-    in_rows = jnp.dot(picker, layer_in, preferred_element_type=F32).astype(BF)
-    grad_rows = (jnp.dot(picker, grad_out, preferred_element_type=F32) * factor).astype(BF)
-    return jnp.concatenate(
-        [in_rows.reshape(cols, CAP, width), grad_rows.reshape(cols, CAP, width)], axis=1
-    )
+    return picker, factor.reshape(experts * CAP, 1)
+
+
+def pick(picker, x):
+    return jnp.dot(picker, x, preferred_element_type=F32).astype(BF)
+
+
+def pick_scaled(picker, x, factor):
+    return (jnp.dot(picker, x, preferred_element_type=F32) * factor).astype(BF)
 
 
 def swap(x, axis):
@@ -60,9 +62,25 @@
     return lax.all_to_all(x, axes, split_axis=0, concat_axis=0, tiled=True)
 
 
-def rotated(x, step):
+def along_line(x, pairs):
+    return lax.ppermute(x, "tensor", pairs)
+
+
+def line_steps():
     n = lax.axis_size("tensor")
-    return lax.ppermute(x, "tensor", [(i, (i + step) % n) for i in range(n)])
+    right = [(i, i + 1) for i in range(n - 1)]
+    left = [(i + 1, i) for i in range(n - 1)]
+    twice = [(i, (i + 2) % n) for i in range(n)]
+    return n, right, left, twice
+
+
+def line_gather(x):
+    n, right, left, twice = line_steps()
+    t = lax.axis_index("tensor")
+    two = along_line(x, twice)
+    from_left, from_right = along_line(x, right), along_line(x, left)
+    three = along_line(two, [(n - 2, n - 1), (1, 0)])
+    return [x, jnp.where(t == 0, three, from_left), two, jnp.where(t == n - 1, three, from_right)]
 
 
 def unit_gradients(gate, up, dhid):
@@ -83,10 +101,15 @@
             d_up, cut(up_full, index, part, 0), 1, 1
         )
 
-    received = [rotated(row_part((t + s) % n).astype(BF), s) for s in (2, 1, 3)]
-    total = row_part(t)
-    for piece in received:
-        total = total + piece.astype(F32)
+    n, right, left, twice = line_steps()
+    edge = row_part(jnp.where(t == 0, n - 1, 0)).astype(BF)
+    edge = along_line(edge, [(0, 1), (n - 1, n - 2)])
+    from_left = along_line(row_part((t + 1) % n).astype(BF), right)
+    from_right = along_line(row_part((t - 1) % n).astype(BF), left)
+    own_two = row_part((t + 2) % n)
+    own = row_part(t)
+    from_two = along_line((own_two + edge.astype(F32)).astype(BF), twice)
+    total = own + from_left.astype(F32) + from_right.astype(F32) + from_two.astype(F32)
     return total.astype(BF)
 
 
@@ -102,19 +125,35 @@
     my_zh = lax.axis_index("zh")
     t = lax.axis_index("tensor")
 
+    routes_t = routes.T
+    far_routes = swap(routes_t, "zh")
+    far_tokens = swap(cut(layer_in, t, part, 1), "zh")
+
     ids = jnp.arange(cols, dtype=jnp.int32)
-    labels = jnp.concatenate([my_zh * cols + ids, (1 - my_zh) * cols + ids])
-    picker, factor = slot_tables(routes.T, combine.T, labels)
+    near_labels = my_zh * cols + ids
+    labels = jnp.concatenate([near_labels, (1 - my_zh) * cols + ids])
+    picker, factor = slot_tables(routes_t, combine.T, labels)
     near_picker, far_picker = picker[:rows], picker[rows:]
 
-    far_sent = picked(
-        far_picker, factor[rows:], cut(layer_in, t, part, 1), cut(grad_out, t, part, 1), cols
-    )
-    far_got = exchange(far_sent, "col")
-    far_in = swap(far_got[:, :CAP].reshape(rows, part), "zh")
-    far_grad = swap(far_got[:, CAP:].reshape(rows, part), "zh")
-
-    near_got = exchange(picked(near_picker, factor[:rows], layer_in, grad_out, cols), "col")
+    def sent(x):
+        return x.reshape(cols, CAP, x.shape[1])
+
+    far_grad = pick_scaled(far_picker, cut(grad_out, t, part, 1), factor[rows:])
+    far_grad = exchange(sent(far_grad), "col").reshape(rows, part)
+    far_grad = swap(far_grad, "zh")
+
+    near_sent = jnp.concatenate(
+        [
+            sent(pick(near_picker, layer_in)),
+            sent(pick_scaled(near_picker, grad_out, factor[:rows])),
+        ],
+        axis=1,
+    )
+    far_routes, _ = lax.optimization_barrier((far_routes, far_picker))
+    arriving_picker, _ = slot_tables(far_routes, None, near_labels)
+    far_in = exchange(sent(pick(arriving_picker, far_tokens)), "col")
+    far_in = far_in.reshape(rows, part)
+    near_got = exchange(near_sent, "col")
     near_in = near_got[:, :CAP].reshape(rows, width)
     near_grad = near_got[:, CAP:].reshape(rows, width)
 
@@ -122,8 +161,8 @@
     up_full = both_halves(up_weight[0], 0)
     down_full = both_halves(down_weight[0], 1)
 
-    far_ins = [far_in] + [rotated(far_in, s) for s in range(1, n)]
-    far_grads = [far_grad] + [rotated(far_grad, s) for s in range(1, n)]
+    far_ins = line_gather(far_in)
+    far_grads = line_gather(far_grad)
 
     act, d_gate, d_up = unit_gradients(
         dot(near_in, gate_full, 1, 0),
@@ -133,7 +172,7 @@
     near_rows = reduced_rows(d_gate, d_up, gate_full, up_full, part)
 
     gate = up = dhid = 0.0
-    for s in range(n):
+    for s in (0, 2, 1, 3):
         q = (t - s) % n
         gate = gate + dot(far_ins[s], cut(gate_full, q, part, 0), 1, 0)
         up = up + dot(far_ins[s], cut(up_full, q, part, 0), 1, 0)
@@ -152,7 +191,8 @@
     )
     total = total.astype(BF)
 
-    far_in_all, far_grad_all = jnp.stack(far_ins), jnp.stack(far_grads)
+    far_in_all = jnp.stack(far_ins)
+    far_grad_all = jnp.stack(far_grads)
 
     def quarter(stacked, q):
         return cut(stacked, (t - q) % n, 1, 0)[0]

time: 202 us -> 218 us (1.079)
  the two profiles are of different devices: /device:TPU:2 before, /device:TPU:1 now
where the time goes in v3:
time: 218 us; the launch traced here: 215 us
  starting transfers between devices  79.8 us (37%)
  waiting for transfers between devices  58.1 us (27%)
  matrix products  46.4 us (21%)
  blocking collectives  16.1 us (7%)
  other arithmetic  8.81 us (4%)
  local copies, waits for them, and re-layouts  4.17 us (2%)
    ppermute x16, waiting for transfers between devices, along_line(): return lax.ppermute(x, 'tensor', pairs)  45.9 us
    dot_general x55, matrix products, dot(): lax.dot_general(a, b, (((ca,), (cb,)), ((), ())), preferred_element_type=...  42.5 us
    ppermute x16, starting transfers between devices, along_line(): return lax.ppermute(x, 'tensor', pairs)  35.3 us
    all_to_all x4, starting transfers between devices, exchange(): return lax.all_to_all(x, axes, split_axis=0, concat_axis=0, tiled=True)  24.1 us
    ppermute x9, starting transfers between devices, swap(): return lax.ppermute(x, axis, [(0, 1), (1, 0)])  20.4 us
    all_gather x1, blocking collectives, inner(): total = lax.all_gather(total, 'tensor', axis=0, tiled=False)  16.1 us
    all_to_all x4, waiting for transfers between devices, exchange(): return lax.all_to_all(x, axes, split_axis=0, concat_axis=0, tiled=True)  12.1 us
  transfers between devices with their start and end apart: 29, of which 8 were waited for; matrix products, arithmetic and copies ran while one was open for 23% of the time, Pallas kernels for 0%

profile of v3, /device:TPU:1, one launch (start us, length us, event | category | flops | bytes accessed | tf_op | source)
XLA Modules:
  0.0 215.1 jit_solution(12254386054261063301)
XLA Ops:
  0.7 1.2 copy-done
  1.8 7.8 %collective-permute-start.13 = (bf16[128,896]{1,0:T(8,128)(2,1)S(1)}, bf16[128,896]{1,0:T(8,128)(2,1)S(1)}, u32[]{:S(2)}, u32[]{:S(2)}) collective-permute-start(bf16[128,896]{1,0:T(8,128)(2,1)S(1)} %constant_dynamic-slice_fusion), channel_id=1, source_target_pairs={{0,64},{64,0},{1,65},{65,1},{2,66},{66,2},{3,67},{67,3},{4,68},{68... | collective-permute-start | bytes 688136 | tf_op jit(solution)/shard_map/ppermute | solution.py:48
  10.8 0.9 fusion.231
  11.9 1.9 fusion.39
  13.8 6.8 %all-to-all-start.1 = ((bf16[16,8,896]{2,1,0:T(8,128)(2,1)}), bf16[16,8,896]{2,1,0:T(8,128)(2,1)}, u32[]{:S(2)}, u32[]{:S(2)}) async-start(bf16[16,8,896]{2,1,0:T(8,128)(2,1)} %fusion.39), calls=%async_computation.1 | async-start | bytes 458752 | tf_op jit(solution)/shard_map/all_to_all | solution.py:62
  20.9 1.0 fusion.40
  21.9 6.2 %all-to-all-done.1 = bf16[16,8,896]{2,1,0:T(8,128)(2,1)} async-done(((bf16[16,8,896]{2,1,0:T(8,128)(2,1)}), bf16[16,8,896]{2,1,0:T(8,128)(2,1)}, u32[]{:S(2)}, u32[]{:S(2)}) %all-to-all-start.1) | async-done | bytes 229408 | tf_op jit(solution)/shard_map/all_to_all | solution.py:62
  28.1 3.5 %all-to-all-start.2 = ((bf16[16,8,896]{2,1,0:T(8,128)(2,1)}), bf16[16,8,896]{2,1,0:T(8,128)(2,1)S(1)}, u32[]{:S(2)}, u32[]{:S(2)}) async-start(bf16[16,8,896]{2,1,0:T(8,128)(2,1)} %fusion.40), calls=%async_computation.2 | async-start | bytes 458752 | tf_op jit(solution)/shard_map/all_to_all | solution.py:62
  31.7 2.3 %collective-permute-start.2 = (bf16[1792,256]{1,0:T(8,128)(2,1)}, bf16[1792,256]{1,0:T(8,128)(2,1)}, u32[]{:S(2)}, u32[]{:S(2)}) collective-permute-start(bf16[1792,256]{1,0:T(8,128)(2,1)} %bitcast.9), channel_id=1, source_target_pairs={{0,128},{128,0},{1,129},{129,1},{2,130},{130,2},{3,131},{131,3},{4... | collective-permute-start | bytes 2752520 | tf_op jit(solution)/shard_map/ppermute | solution.py:48
  34.1 5.6 %collective-permute-start.7 = (bf16[128,896]{1,0:T(8,128)(2,1)}, bf16[128,896]{1,0:T(8,128)(2,1)S(1)}, u32[]{:S(2)}, u32[]{:S(2)}) collective-permute-start(bf16[128,896]{1,0:T(8,128)(2,1)} %bitcast.12), channel_id=1, source_target_pairs={{0,64},{64,0},{1,65},{65,1},{2,66},{66,2},{3,67},{67,3},{4,68},{68... | collective-permute-start | bytes 688136 | tf_op jit(solution)/shard_map/ppermute | solution.py:48
  39.7 1.2 collective-permute-start.14
  40.9 3.7 %collective-permute-start.16 = (bf16[128,896]{1,0:T(8,128)(2,1)S(1)}, bf16[128,896]{1,0:T(8,128)(2,1)}, u32[]{:S(2)}, u32[]{:S(2)}) collective-permute-start(bf16[128,896]{1,0:T(8,128)(2,1)S(1)} %bitcast.168), channel_id=1, source_target_pairs={{0,1},{1,2},{2,3},{4,5},{5,6},{6,7},{8,9},{9,10},{10,11},{12,13},{... | collective-permute-start | bytes 688136 | tf_op jit(solution)/shard_map/ppermute | solution.py:66
  45.5 1.3 collective-permute-start.17
  46.8 14.5 %collective-permute-done.14 = bf16[128,896]{1,0:T(8,128)(2,1)S(1)} collective-permute-done((bf16[128,896]{1,0:T(8,128)(2,1)S(1)}, bf16[128,896]{1,0:T(8,128)(2,1)S(1)}, u32[]{:S(2)}, u32[]{:S(2)}) %collective-permute-start.14) | collective-permute-done | bytes 229408 | tf_op jit(solution)/shard_map/ppermute | solution.py:66
  61.3 1.3 collective-permute-start.15
  62.5 1.4 pad_maximum_fusion
  64.0 6.8 %all-to-all-start = ((bf16[16,16,3584]{2,1,0:T(8,128)(2,1)}), bf16[16,16,3584]{2,1,0:T(8,128)(2,1)}, u32[]{:S(2)}, u32[]{:S(2)}) async-start(bf16[16,16,3584]{2,1,0:T(8,128)(2,1)} %pad_maximum_fusion), calls=%async_computation | async-start | bytes 3670016 | tf_op jit(solution)/shard_map/all_to_all | solution.py:62
  71.0 1.3 collective-permute-start.11
  72.3 3.7 %collective-permute-done.8 = bf16[128,896]{1,0:T(8,128)(2,1)S(1)} collective-permute-done((bf16[128,896]{1,0:T(8,128)(2,1)S(1)}, bf16[128,896]{1,0:T(8,128)(2,1)S(1)}, u32[]{:S(2)}, u32[]{:S(2)}) %collective-permute-start.8) | collective-permute-done | bytes 229408 | tf_op jit(solution)/shard_map/ppermute | solution.py:66
  76.0 7.9 %collective-permute-start.10 = (bf16[128,896]{1,0:T(8,128)(2,1)S(1)}, bf16[128,896]{1,0:T(8,128)(2,1)S(1)}, u32[]{:S(2)}, u32[]{:S(2)}) collective-permute-start(bf16[128,896]{1,0:T(8,128)(2,1)S(1)} %collective-permute-done.7), channel_id=1, source_target_pairs={{0,1},{1,2},{2,3},{4,5},{5,6},{6,7},{8,9},{9,10},{10,11},{12,13},{... | collective-permute-start | bytes 688136 | tf_op jit(solution)/shard_map/ppermute | solution.py:66
  84.0 1.3 collective-permute-start.9
  85.5 1.7 collective-permute-done.11
  87.2 1.3 collective-permute-start
  88.5 3.9 %collective-permute-done.9 = bf16[128,896]{1,0:T(8,128)(2,1)S(1)} collective-permute-done((bf16[128,896]{1,0:T(8,128)(2,1)S(1)}, bf16[128,896]{1,0:T(8,128)(2,1)S(1)}, u32[]{:S(2)}, u32[]{:S(2)}) %collective-permute-start.9) | collective-permute-done | bytes 229408 | tf_op jit(solution)/shard_map/ppermute | solution.py:66
  92.6 2.6 %broadcast_select_fusion.1 = (bf16[1792,256]{1,0:T(8,128)(2,1)S(1)}, bf16[1792,256]{1,0:T(8,128)(2,1)S(1)}, bf16[1792,256]{1,0:T(8,128)(2,1)S(1)}, bf16[1792,256]{1,0:T(8,128)(2,1)S(1)}) fusion(bf16[1792,256]{1,0:T(8,128)(2,1)} %collective-permute-done.2, pred[]{:T(512)S(6)} %eq.107, bf16[1,1792,256]{2,1,0:T(8,128)(2,1)} %param.11, ...), kind=kLoop, calls=%fused_computation.82 | loop fusion | flops 1835008 | bytes 7340033 | tf_op jit(solution)/shard_map/jit(_where)/select_n | solution.py:56
  96.0 1.3 broadcast_select_fusion.5
  100.5 1.3 fusion.115
  101.8 1.2 fusion.117
  103.1 1.2 fusion.121
  104.3 1.3 fusion.119
  105.6 1.2 fusion.125
  106.8 1.3 fusion.123
  108.1 1.2 fusion.129
  109.3 1.2 fusion.127
  111.2 1.3 collective-permute-start.20
  112.8 1.3 collective-permute-start.19
  114.7 4.0 %collective-permute-start.18 = (bf16[128,896]{1,0:T(8,128)(2,1)S(1)}, bf16[128,896]{1,0:T(8,128)(2,1)S(1)}, u32[]{:S(2)}, u32[]{:S(2)}) collective-permute-start(bf16[128,896]{1,0:T(8,128)(2,1)S(1)} %fusion.36), channel_id=1, source_target_pairs={{0,1},{1,2},{2,3},{4,5},{5,6},{6,7},{8,9},{9,10},{10,11},{12,13},{... | collective-permute-start | bytes 688136 | tf_op jit(solution)/shard_map/ppermute | solution.py:66
  118.7 1.2 fusion.107
  120.0 1.2 fusion.109
  121.2 1.3 fusion.111
  123.1 3.9 %collective-permute-start.21 = (bf16[128,896]{1,0:T(8,128)(2,1)S(1)}, bf16[128,896]{1,0:T(8,128)(2,1)S(1)}, u32[]{:S(2)}, u32[]{:S(2)}) collective-permute-start(bf16[128,896]{1,0:T(8,128)(2,1)S(1)} %fusion.30), channel_id=1, source_target_pairs={{0,2},{1,3},{2,0},{3,1},{4,6},{5,7},{6,4},{7,5},{8,10},{9,11},{10,... | collective-permute-start | bytes 688136 | tf_op jit(solution)/shard_map/ppermute | solution.py:66
  127.4 9.8 %collective-permute-done.21 = bf16[128,896]{1,0:T(8,128)(2,1)S(1)} collective-permute-done((bf16[128,896]{1,0:T(8,128)(2,1)S(1)}, bf16[128,896]{1,0:T(8,128)(2,1)S(1)}, u32[]{:S(2)}, u32[]{:S(2)}) %collective-permute-start.21) | collective-permute-done | bytes 229408 | tf_op jit(solution)/shard_map/ppermute | solution.py:66
  137.4 1.7 fusion.228
  139.2 2.0 fusion.227
  141.3 1.6 multiply_convert_fusion.1
  144.1 1.3 collective-permute-start.5
  145.7 1.3 collective-permute-start.4
  147.3 4.1 %collective-permute-start.3 = (bf16[128,896]{1,0:T(8,128)(2,1)S(1)}, bf16[128,896]{1,0:T(8,128)(2,1)S(1)}, u32[]{:S(2)}, u32[]{:S(2)}) collective-permute-start(bf16[128,896]{1,0:T(8,128)(2,1)S(1)} %fusion.33), channel_id=1, source_target_pairs={{0,1},{1,2},{2,3},{4,5},{5,6},{6,7},{8,9},{9,10},{10,11},{12,13},{... | collective-permute-start | bytes 688136 | tf_op jit(solution)/shard_map/ppermute | solution.py:66
  151.5 1.6 slice_bitcast_fusion.1
  153.1 1.4 fusion.12
  154.5 2.0 collective-permute-start.22
  156.4 1.4 fusion.15
  157.8 1.0 collective-permute-start.23
  158.8 1.3 fusion.18
  161.3 12.4 %collective-permute-done.6 = bf16[128,896]{1,0:T(8,128)(2,1)S(1)} collective-permute-done((bf16[128,896]{1,0:T(8,128)(2,1)S(1)}, bf16[128,896]{1,0:T(8,128)(2,1)S(1)}, u32[]{:S(2)}, u32[]{:S(2)}) %collective-permute-start.6) | collective-permute-done | bytes 229408 | tf_op jit(solution)/shard_map/ppermute | solution.py:66
  174.1 0.9 pad_maximum_fusion.6
  175.0 6.9 %all-to-all-start.3 = ((bf16[32,8,896]{2,1,0:T(8,128)(2,1)}), bf16[32,8,896]{2,1,0:T(8,128)(2,1)S(1)}, u32[]{:S(2)}, u32[]{:S(2)}) async-start(bf16[32,8,896]{2,1,0:T(8,128)(2,1)} %bitcast.19), calls=%async_computation.3 | async-start | bytes 917504 | tf_op jit(solution)/shard_map/all_to_all | solution.py:62
  181.9 1.3 fusion.113
  183.2 3.0 %add_convert_fusion.2 = bf16[1792,256]{1,0:T(8,128)(2,1)} fusion(bf16[1792,256]{1,0:T(8,128)(2,1)} %collective-permute-done.22, f32[896,256]{1,0:T(8,128)S(1)} %copy-done.11, f32[896,256]{1,0:T(8,128)} %fusion.129, bf16[128,256]{1,0:T(8,128)(2,1)S(1)} %get-tuple-element.26, bf16[128,3584]{1,0:T(8,128)(2,1)S(1)} %copy-done.6, s32[]{:T(128)S(6)} %select_n.266), kind=kOutput, calls=%fused_computation.33 | convolution fusion | flops 121110528 | bytes 4194308 | tf_op jit(solution)/shard_map/dot_general | solution.py:14
  186.2 2.7 %add_convert_fusion.1 = bf16[1792,256]{1,0:T(8,128)(2,1)} fusion(bf16[1792,256]{1,0:T(8,128)(2,1)} %collective-permute-done.23, f32[896,256]{1,0:T(8,128)S(1)} %copy-done.9, f32[896,256]{1,0:T(8,128)S(1)} %copy-done.10, bf16[128,256]{1,0:T(8,128)(2,1)S(1)} %get-tuple-element.27, bf16[128,3584]{1,0:T(8,128)(2,1)S(1)} %copy-done.6, s32[]{:T(128)S(6)} %select_n.266), kind=kOutput, calls=%fused_computation.32 | convolution fusion | flops 121110528 | bytes 4194308 | tf_op jit(solution)/shard_map/dot_general | solution.py:14
  189.0 2.6 %add_convert_fusion = bf16[256,1792]{1,0:T(8,128)(2,1)} fusion(bf16[256,1792]{1,0:T(8,128)(2,1)} %collective-permute-done.24, f32[256,896]{1,0:T(8,128)S(1)} %copy-done.12, f32[256,896]{1,0:T(8,128)S(1)} %fusion.113, bf16[128,256]{1,0:T(8,128)(2,1)S(1)} %get-tuple-element.25, bf16[128,3584]{1,0:T(8,128)(2,1)S(1)} %copy-done.8, s32[]{:T(128)S(6)} %select_n.266), kind=kOutput, calls=%fused_computation.31 | convolution fusion | flops 121110528 | bytes 4194308 | tf_op jit(solution)/shard_map/dot_general | solution.py:14
  191.6 5.9 %all-to-all-done.3 = bf16[32,8,896]{2,1,0:T(8,128)(2,1)S(1)} async-done(((bf16[32,8,896]{2,1,0:T(8,128)(2,1)}), bf16[32,8,896]{2,1,0:T(8,128)(2,1)S(1)}, u32[]{:S(2)}, u32[]{:S(2)}) %all-to-all-start.3) | async-done | bytes 458784 | tf_op jit(solution)/shard_map/all_to_all | solution.py:62
  198.0 16.1 %all-gather = bf16[512,896]{1,0:T(8,128)(2,1)S(1)} all-gather(bf16[128,896]{1,0:T(8,128)(2,1)S(1)} %fusion.32), channel_id=2, replica_groups=mesh['dp'=2,'zh'=2,'col'=16,'tensor'=4] {'tensor'}, dimensions={0}, use_global_device_ids=true | all-gather | bytes 1146880 | tf_op jit(solution)/shard_map/all_gather | solution.py:220
  214.1 1.0 copy.14
  (130 shorter events, 13.4 us)
Async XLA Ops:
  0.6 1.2 copy-start
  1.8 19.1 %collective-permute-start.13 = (bf16[128,896]{1,0:T(8,128)(2,1)S(1)}, bf16[128,896]{1,0:T(8,128)(2,1)S(1)}, u32[]{:S(2)}, u32[]{:S(2)}) collective-permute-start(bf16[128,896]{1,0:T(8,128)(2,1)S(1)} %constant_dynamic-slice_fusion), channel_id=1, source_target_pairs={{0,64},{64,0},{1,65},{65,1},{2,66},{66,2},{3,67},{67,3},{4,68},{68... | collective-permute-start | bytes 688136 | tf_op jit(solution)/shard_map/ppermute | solution.py:48
  9.7 11.0 %collective-permute-start.12 = (s32[8,128]{1,0:T(8,128)}, s32[8,128]{1,0:T(8,128)S(1)}, u32[]{:S(2)}, u32[]{:S(2)}) collective-permute-start(s32[8,128]{1,0:T(8,128)} %bitcast.183), channel_id=1, source_target_pairs={{0,64},{64,0},{1,65},{65,1},{2,66},{66,2},{3,67},{67,3},{4,68},{68... | collective-permute-start | bytes 12296 | tf_op jit(solution)/shard_map/ppermute | solution.py:48
  11.8 33.2 %copy-start.20 = (bf16[128,3584]{1,0:T(8,128)(2,1)S(1)}, bf16[128,3584]{1,0:T(8,128)(2,1)}, u32[]{:S(2)}) copy-start(bf16[128,3584]{1,0:T(8,128)(2,1)} %param.7) | copy-start | bytes 2752516
  13.8 14.4 %all-to-all-start.1 = ((bf16[16,8,896]{2,1,0:T(8,128)(2,1)}), bf16[16,8,896]{2,1,0:T(8,128)(2,1)}, u32[]{:S(2)}, u32[]{:S(2)}) async-start(bf16[16,8,896]{2,1,0:T(8,128)(2,1)} %fusion.39), calls=%async_computation.1 | async-start | bytes 458752 | tf_op jit(solution)/shard_map/all_to_all | solution.py:62
  28.1 11.5 %all-to-all-start.2 = ((bf16[16,8,896]{2,1,0:T(8,128)(2,1)}), bf16[16,8,896]{2,1,0:T(8,128)(2,1)S(1)}, u32[]{:S(2)}, u32[]{:S(2)}) async-start(bf16[16,8,896]{2,1,0:T(8,128)(2,1)} %fusion.40), calls=%async_computation.2 | async-start | bytes 458752 | tf_op jit(solution)/shard_map/all_to_all | solution.py:62
  31.7 60.9 %collective-permute-start.2 = (bf16[1792,256]{1,0:T(8,128)(2,1)}, bf16[1792,256]{1,0:T(8,128)(2,1)}, u32[]{:S(2)}, u32[]{:S(2)}) collective-permute-start(bf16[1792,256]{1,0:T(8,128)(2,1)} %bitcast.9), channel_id=1, source_target_pairs={{0,128},{128,0},{1,129},{129,1},{2,130},{130,2},{3,131},{131,3},{4... | collective-permute-start | bytes 2752520 | tf_op jit(solution)/shard_map/ppermute | solution.py:48
  34.0 58.6 %collective-permute-start.1 = (bf16[1792,256]{1,0:T(8,128)(2,1)}, bf16[1792,256]{1,0:T(8,128)(2,1)}, u32[]{:S(2)}, u32[]{:S(2)}) collective-permute-start(bf16[1792,256]{1,0:T(8,128)(2,1)} %bitcast.8), channel_id=1, source_target_pairs={{0,128},{128,0},{1,129},{129,1},{2,130},{130,2},{3,131},{131,3},{4... | collective-permute-start | bytes 2752520 | tf_op jit(solution)/shard_map/ppermute | solution.py:48
  34.1 11.3 %collective-permute-start.7 = (bf16[128,896]{1,0:T(8,128)(2,1)}, bf16[128,896]{1,0:T(8,128)(2,1)S(1)}, u32[]{:S(2)}, u32[]{:S(2)}) collective-permute-start(bf16[128,896]{1,0:T(8,128)(2,1)} %bitcast.12), channel_id=1, source_target_pairs={{0,64},{64,0},{1,65},{65,1},{2,66},{66,2},{3,67},{67,3},{4,68},{68... | collective-permute-start | bytes 688136 | tf_op jit(solution)/shard_map/ppermute | solution.py:48
  39.7 21.6 %collective-permute-start.14 = (bf16[128,896]{1,0:T(8,128)(2,1)S(1)}, bf16[128,896]{1,0:T(8,128)(2,1)S(1)}, u32[]{:S(2)}, u32[]{:S(2)}) collective-permute-start(bf16[128,896]{1,0:T(8,128)(2,1)S(1)} %bitcast.167), channel_id=1, source_target_pairs={{0,2},{1,3},{2,0},{3,1},{4,6},{5,7},{6,4},{7,5},{8,10},{9,11},{10,... | collective-permute-start | bytes 688136 | tf_op jit(solution)/shard_map/ppermute | solution.py:66
  40.9 20.4 %collective-permute-start.16 = (bf16[128,896]{1,0:T(8,128)(2,1)S(1)}, bf16[128,896]{1,0:T(8,128)(2,1)}, u32[]{:S(2)}, u32[]{:S(2)}) collective-permute-start(bf16[128,896]{1,0:T(8,128)(2,1)S(1)} %bitcast.168), channel_id=1, source_target_pairs={{0,1},{1,2},{2,3},{4,5},{5,6},{6,7},{8,9},{9,10},{10,11},{12,13},{... | collective-permute-start | bytes 688136 | tf_op jit(solution)/shard_map/ppermute | solution.py:66
  45.5 25.5 %collective-permute-start.17 = (bf16[128,896]{1,0:T(8,128)(2,1)S(1)}, bf16[128,896]{1,0:T(8,128)(2,1)S(1)}, u32[]{:S(2)}, u32[]{:S(2)}) collective-permute-start(bf16[128,896]{1,0:T(8,128)(2,1)S(1)} %bitcast.169), channel_id=1, source_target_pairs={{1,0},{2,1},{3,2},{5,4},{6,5},{7,6},{9,8},{10,9},{11,10},{13,12},{... | collective-permute-start | bytes 688136 | tf_op jit(solution)/shard_map/ppermute | solution.py:66
  61.2 14.8 %collective-permute-start.8 = (bf16[128,896]{1,0:T(8,128)(2,1)S(1)}, bf16[128,896]{1,0:T(8,128)(2,1)S(1)}, u32[]{:S(2)}, u32[]{:S(2)}) collective-permute-start(bf16[128,896]{1,0:T(8,128)(2,1)S(1)} %collective-permute-done.7), channel_id=1, source_target_pairs={{0,2},{1,3},{2,0},{3,1},{4,6},{5,7},{6,4},{7,5},{8,10},{9,11},{10,... | collective-permute-start | bytes 688136 | tf_op jit(solution)/shard_map/ppermute | solution.py:66
  61.3 22.7 %collective-permute-start.15 = (bf16[128,896]{1,0:T(8,128)(2,1)S(1)}, bf16[128,896]{1,0:T(8,128)(2,1)S(1)}, u32[]{:S(2)}, u32[]{:S(2)}) collective-permute-start(bf16[128,896]{1,0:T(8,128)(2,1)S(1)} %collective-permute-done.14), channel_id=1, source_target_pairs={{2,3},{1,0},{6,7},{5,4},{10,11},{9,8},{14,15},{13,12},{18,19},{17,... | collective-permute-start | bytes 688136 | tf_op jit(solution)/shard_map/ppermute | solution.py:66
  64.0 73.5 %all-to-all-start = ((bf16[16,16,3584]{2,1,0:T(8,128)(2,1)}), bf16[16,16,3584]{2,1,0:T(8,128)(2,1)}, u32[]{:S(2)}, u32[]{:S(2)}) async-start(bf16[16,16,3584]{2,1,0:T(8,128)(2,1)} %pad_maximum_fusion), calls=%async_computation | async-start | bytes 3670016 | tf_op jit(solution)/shard_map/all_to_all | solution.py:62
  71.0 16.2 %collective-permute-start.11 = (bf16[128,896]{1,0:T(8,128)(2,1)S(1)}, bf16[128,896]{1,0:T(8,128)(2,1)S(1)}, u32[]{:S(2)}, u32[]{:S(2)}) collective-permute-start(bf16[128,896]{1,0:T(8,128)(2,1)S(1)} %collective-permute-done.7), channel_id=1, source_target_pairs={{1,0},{2,1},{3,2},{5,4},{6,5},{7,6},{9,8},{10,9},{11,10},{13,12},{... | collective-permute-start | bytes 688136 | tf_op jit(solution)/shard_map/ppermute | solution.py:66
  76.0 16.4 %copy-start.21 = (bf16[128,896]{1,0:T(8,128)(2,1)}, bf16[128,896]{1,0:T(8,128)(2,1)S(1)}, u32[]{:S(2)}) copy-start(bf16[128,896]{1,0:T(8,128)(2,1)S(1)} %collective-permute-done.8) | copy-start | bytes 688132
  76.0 12.5 %collective-permute-start.10 = (bf16[128,896]{1,0:T(8,128)(2,1)S(1)}, bf16[128,896]{1,0:T(8,128)(2,1)S(1)}, u32[]{:S(2)}, u32[]{:S(2)}) collective-permute-start(bf16[128,896]{1,0:T(8,128)(2,1)S(1)} %collective-permute-done.7), channel_id=1, source_target_pairs={{0,1},{1,2},{2,3},{4,5},{5,6},{6,7},{8,9},{9,10},{10,11},{12,13},{... | collective-permute-start | bytes 688136 | tf_op jit(solution)/shard_map/ppermute | solution.py:66
  84.0 8.4 %collective-permute-start.9 = (bf16[128,896]{1,0:T(8,128)(2,1)S(1)}, bf16[128,896]{1,0:T(8,128)(2,1)S(1)}, u32[]{:S(2)}, u32[]{:S(2)}) collective-permute-start(bf16[128,896]{1,0:T(8,128)(2,1)S(1)} %collective-permute-done.8), channel_id=1, source_target_pairs={{2,3},{1,0},{6,7},{5,4},{10,11},{9,8},{14,15},{13,12},{18,19},{17,... | collective-permute-start | bytes 688136 | tf_op jit(solution)/shard_map/ppermute | solution.py:66
  87.2 8.8 %collective-permute-start = (bf16[256,1792]{1,0:T(8,128)(2,1)}, bf16[256,1792]{1,0:T(8,128)(2,1)S(1)}, u32[]{:S(2)}, u32[]{:S(2)}) collective-permute-start(bf16[256,1792]{1,0:T(8,128)(2,1)} %bitcast.6), channel_id=1, source_target_pairs={{0,128},{128,0},{1,129},{129,1},{2,130},{130,2},{3,131},{131,3},{4... | collective-permute-start | bytes 2752520 | tf_op jit(solution)/shard_map/ppermute | solution.py:48
  92.6 28.6 %copy-start.13 = (bf16[4,128,896]{2,1,0:T(8,128)(2,1)}, bf16[4,128,896]{2,1,0:T(8,128)(2,1)S(1)}, u32[]{:S(2)}) copy-start(bf16[4,128,896]{2,1,0:T(8,128)(2,1)S(1)} %pad_maximum_fusion.5) | copy-start | bytes 2752516
  95.3 31.7 %copy-start.1 = (bf16[3584,256]{1,0:T(8,128)(2,1)}, bf16[3584,256]{1,0:T(8,128)(2,1)S(1)}, u32[]{:S(2)}) copy-start(bf16[3584,256]{1,0:T(8,128)(2,1)S(1)} %pad_maximum_fusion.2) | copy-start | bytes 5505028
  97.4 2.5 %copy-start.3 = (bf16[256,3584]{1,0:T(8,128)(2,1)}, bf16[256,3584]{1,0:T(8,128)(2,1)S(1)}, u32[]{:S(2)}) copy-start(bf16[256,3584]{1,0:T(8,128)(2,1)S(1)} %pad_maximum_fusion.1) | copy-start | bytes 5505028
  98.4 1.1 copy-start.22
  111.2 11.6 %collective-permute-start.20 = (bf16[128,896]{1,0:T(8,128)(2,1)S(1)}, bf16[128,896]{1,0:T(8,128)(2,1)S(1)}, u32[]{:S(2)}, u32[]{:S(2)}) collective-permute-start(bf16[128,896]{1,0:T(8,128)(2,1)S(1)} %fusion.38), channel_id=1, source_target_pairs={{0,1},{3,2},{4,5},{7,6},{8,9},{11,10},{12,13},{15,14},{16,17},{19,... | collective-permute-start | bytes 688136 | tf_op jit(solution)/shard_map/ppermute | solution.py:66
  112.8 14.5 %collective-permute-start.19 = (bf16[128,896]{1,0:T(8,128)(2,1)S(1)}, bf16[128,896]{1,0:T(8,128)(2,1)S(1)}, u32[]{:S(2)}, u32[]{:S(2)}) collective-permute-start(bf16[128,896]{1,0:T(8,128)(2,1)S(1)} %fusion.37), channel_id=1, source_target_pairs={{1,0},{2,1},{3,2},{5,4},{6,5},{7,6},{9,8},{10,9},{11,10},{13,12},{... | collective-permute-start | bytes 688136 | tf_op jit(solution)/shard_map/ppermute | solution.py:66
  114.7 12.6 %collective-permute-start.18 = (bf16[128,896]{1,0:T(8,128)(2,1)S(1)}, bf16[128,896]{1,0:T(8,128)(2,1)S(1)}, u32[]{:S(2)}, u32[]{:S(2)}) collective-permute-start(bf16[128,896]{1,0:T(8,128)(2,1)S(1)} %fusion.36), channel_id=1, source_target_pairs={{0,1},{1,2},{2,3},{4,5},{5,6},{6,7},{8,9},{9,10},{10,11},{12,13},{... | collective-permute-start | bytes 688136 | tf_op jit(solution)/shard_map/ppermute | solution.py:66
  123.1 14.0 %collective-permute-start.21 = (bf16[128,896]{1,0:T(8,128)(2,1)S(1)}, bf16[128,896]{1,0:T(8,128)(2,1)S(1)}, u32[]{:S(2)}, u32[]{:S(2)}) collective-permute-start(bf16[128,896]{1,0:T(8,128)(2,1)S(1)} %fusion.30), channel_id=1, source_target_pairs={{0,2},{1,3},{2,0},{3,1},{4,6},{5,7},{6,4},{7,5},{8,10},{9,11},{10,... | collective-permute-start | bytes 688136 | tf_op jit(solution)/shard_map/ppermute | solution.py:66
  137.4 1.8 copy-start.4
  139.2 2.0 copy-start.2
  144.1 16.4 %collective-permute-start.5 = (bf16[128,896]{1,0:T(8,128)(2,1)S(1)}, bf16[128,896]{1,0:T(8,128)(2,1)S(1)}, u32[]{:S(2)}, u32[]{:S(2)}) collective-permute-start(bf16[128,896]{1,0:T(8,128)(2,1)S(1)} %fusion.35), channel_id=1, source_target_pairs={{0,1},{3,2},{4,5},{7,6},{8,9},{11,10},{12,13},{15,14},{16,17},{19,... | collective-permute-start | bytes 688136 | tf_op jit(solution)/shard_map/ppermute | solution.py:66
  145.7 15.5 %collective-permute-start.4 = (bf16[128,896]{1,0:T(8,128)(2,1)S(1)}, bf16[128,896]{1,0:T(8,128)(2,1)S(1)}, u32[]{:S(2)}, u32[]{:S(2)}) collective-permute-start(bf16[128,896]{1,0:T(8,128)(2,1)S(1)} %fusion.34), channel_id=1, source_target_pairs={{1,0},{2,1},{3,2},{5,4},{6,5},{7,6},{9,8},{10,9},{11,10},{13,12},{... | collective-permute-start | bytes 688136 | tf_op jit(solution)/shard_map/ppermute | solution.py:66
  147.3 5.8 %copy-start.16 = (f32[896,256]{1,0:T(8,128)S(1)}, f32[896,256]{1,0:T(8,128)}, u32[]{:S(2)}) copy-start(f32[896,256]{1,0:T(8,128)} %fusion.117) | copy-start | bytes 2752516
  147.3 5.8 %copy-start.17 = (f32[896,256]{1,0:T(8,128)S(1)}, f32[896,256]{1,0:T(8,128)}, u32[]{:S(2)}) copy-start(f32[896,256]{1,0:T(8,128)} %fusion.121) | copy-start | bytes 2752516
  147.3 14.0 %collective-permute-start.3 = (bf16[128,896]{1,0:T(8,128)(2,1)S(1)}, bf16[128,896]{1,0:T(8,128)(2,1)S(1)}, u32[]{:S(2)}, u32[]{:S(2)}) collective-permute-start(bf16[128,896]{1,0:T(8,128)(2,1)S(1)} %fusion.33), channel_id=1, source_target_pairs={{0,1},{1,2},{2,3},{4,5},{5,6},{6,7},{8,9},{9,10},{10,11},{12,13},{... | collective-permute-start | bytes 688136 | tf_op jit(solution)/shard_map/ppermute | solution.py:66
  153.0 4.8 %copy-start.5 = (bf16[128,3584]{1,0:T(8,128)(2,1)}, bf16[128,3584]{1,0:T(8,128)(2,1)S(1)}, u32[]{:S(2)}) copy-start(bf16[128,3584]{1,0:T(8,128)(2,1)S(1)} %get-tuple-element.13) | copy-start | bytes 2752516
  153.1 5.8 %copy-start.7 = (bf16[128,3584]{1,0:T(8,128)(2,1)}, bf16[128,3584]{1,0:T(8,128)(2,1)S(1)}, u32[]{:S(2)}) copy-start(bf16[128,3584]{1,0:T(8,128)(2,1)S(1)} %get-tuple-element.12) | copy-start | bytes 2752516
  153.1 3.4 %copy-start.14 = (f32[896,256]{1,0:T(8,128)S(1)}, f32[896,256]{1,0:T(8,128)}, u32[]{:S(2)}) copy-start(f32[896,256]{1,0:T(8,128)} %fusion.115) | copy-start | bytes 2752516
  153.1 3.4 %copy-start.15 = (f32[896,256]{1,0:T(8,128)S(1)}, f32[896,256]{1,0:T(8,128)}, u32[]{:S(2)}) copy-start(f32[896,256]{1,0:T(8,128)} %fusion.119) | copy-start | bytes 2752516
  154.5 4.4 %copy-start.18 = (f32[256,896]{1,0:T(8,128)S(1)}, f32[256,896]{1,0:T(8,128)}, u32[]{:S(2)}) copy-start(f32[256,896]{1,0:T(8,128)} %fusion.107) | copy-start | bytes 2752516
  154.5 4.4 %copy-start.19 = (f32[256,896]{1,0:T(8,128)S(1)}, f32[256,896]{1,0:T(8,128)}, u32[]{:S(2)}) copy-start(f32[256,896]{1,0:T(8,128)} %fusion.109) | copy-start | bytes 2752516
  154.5 28.7 %collective-permute-start.22 = (bf16[1792,256]{1,0:T(8,128)(2,1)}, bf16[1792,256]{1,0:T(8,128)(2,1)}, u32[]{:S(2)}, u32[]{:S(2)}) collective-permute-start(bf16[1792,256]{1,0:T(8,128)(2,1)} %fusion.12), channel_id=1, source_target_pairs={{0,128},{128,0},{1,129},{129,1},{2,130},{130,2},{3,131},{131,3},{4... | collective-permute-start | bytes 2752520 | tf_op jit(solution)/shard_map/ppermute | solution.py:48
  157.8 28.4 %collective-permute-start.23 = (bf16[1792,256]{1,0:T(8,128)(2,1)}, bf16[1792,256]{1,0:T(8,128)(2,1)}, u32[]{:S(2)}, u32[]{:S(2)}) collective-permute-start(bf16[1792,256]{1,0:T(8,128)(2,1)} %fusion.15), channel_id=1, source_target_pairs={{0,128},{128,0},{1,129},{129,1},{2,130},{130,2},{3,131},{131,3},{4... | collective-permute-start | bytes 2752520 | tf_op jit(solution)/shard_map/ppermute | solution.py:48
  160.8 12.9 %collective-permute-start.6 = (bf16[128,896]{1,0:T(8,128)(2,1)S(1)}, bf16[128,896]{1,0:T(8,128)(2,1)S(1)}, u32[]{:S(2)}, u32[]{:S(2)}) collective-permute-start(bf16[128,896]{1,0:T(8,128)(2,1)S(1)} %fusion.28), channel_id=1, source_target_pairs={{0,2},{1,3},{2,0},{3,1},{4,6},{5,7},{6,4},{7,5},{8,10},{9,11},{10,... | collective-permute-start | bytes 688136 | tf_op jit(solution)/shard_map/ppermute | solution.py:66
  161.2 27.7 %collective-permute-start.24 = (bf16[256,1792]{1,0:T(8,128)(2,1)}, bf16[256,1792]{1,0:T(8,128)(2,1)}, u32[]{:S(2)}, u32[]{:S(2)}) collective-permute-start(bf16[256,1792]{1,0:T(8,128)(2,1)} %fusion.18), channel_id=1, source_target_pairs={{0,128},{128,0},{1,129},{129,1},{2,130},{130,2},{3,131},{131,3},{4... | collective-permute-start | bytes 2752520 | tf_op jit(solution)/shard_map/ppermute | solution.py:48
  174.1 9.1 %copy-start.6 = (bf16[128,3584]{1,0:T(8,128)(2,1)S(1)}, bf16[128,3584]{1,0:T(8,128)(2,1)}, u32[]{:S(2)}) copy-start(bf16[128,3584]{1,0:T(8,128)(2,1)} %copy-done.5) | copy-start | bytes 2752516
  174.1 9.1 %copy-start.11 = (f32[896,256]{1,0:T(8,128)S(1)}, f32[896,256]{1,0:T(8,128)}, u32[]{:S(2)}) copy-start(f32[896,256]{1,0:T(8,128)} %fusion.125) | copy-start | bytes 2752516
  175.0 22.5 %all-to-all-start.3 = ((bf16[32,8,896]{2,1,0:T(8,128)(2,1)}), bf16[32,8,896]{2,1,0:T(8,128)(2,1)S(1)}, u32[]{:S(2)}, u32[]{:S(2)}) async-start(bf16[32,8,896]{2,1,0:T(8,128)(2,1)} %bitcast.19), calls=%async_computation.3 | async-start | bytes 917504 | tf_op jit(solution)/shard_map/all_to_all | solution.py:62
  183.2 3.0 %copy-start.9 = (f32[896,256]{1,0:T(8,128)S(1)}, f32[896,256]{1,0:T(8,128)}, u32[]{:S(2)}) copy-start(f32[896,256]{1,0:T(8,128)} %fusion.123) | copy-start | bytes 2752516
  183.2 3.0 %copy-start.10 = (f32[896,256]{1,0:T(8,128)S(1)}, f32[896,256]{1,0:T(8,128)}, u32[]{:S(2)}) copy-start(f32[896,256]{1,0:T(8,128)} %fusion.127) | copy-start | bytes 2752516
  186.2 2.7 %copy-start.8 = (bf16[128,3584]{1,0:T(8,128)(2,1)S(1)}, bf16[128,3584]{1,0:T(8,128)(2,1)}, u32[]{:S(2)}) copy-start(bf16[128,3584]{1,0:T(8,128)(2,1)} %copy-done.7) | copy-start | bytes 2752516
  186.2 2.7 %copy-start.12 = (f32[256,896]{1,0:T(8,128)S(1)}, f32[256,896]{1,0:T(8,128)}, u32[]{:S(2)}) copy-start(f32[256,896]{1,0:T(8,128)} %fusion.111) | copy-start | bytes 2752516

commit v4 on v2

--- a/solution.py
+++ b/solution.py
@@ -46,6 +46,11 @@
     return lax.ppermute(x, axis, [(0, 1), (1, 0)])
 
 
+def mirrored(x):
+    last = 2 * lax.axis_size("tensor") - 1
+    return lax.ppermute(x, ("zh", "tensor"), [(z, last - z) for z in range(last + 1)])
+
+
 def both_halves(mine, axis):
     other = swap(mine, "dp")
     first = lax.axis_index("dp") == 0
@@ -74,14 +79,13 @@
     return act, d_gate, d_up
 
 
-def reduced_rows(d_gate, d_up, gate_full, up_full, part):
+def reduced_rows(d_gate, d_up, gate_full, up_full, part, owned):
     n = lax.axis_size("tensor")
     t = lax.axis_index("tensor")
 
-    def row_part(index):
-        return dot(d_gate, cut(gate_full, index, part, 0), 1, 1) + dot(
-            d_up, cut(up_full, index, part, 0), 1, 1
-        )
+    def row_part(rank):
+        g, u = cut(gate_full, owned(rank), part, 0), cut(up_full, owned(rank), part, 0)
+        return dot(d_gate, g, 1, 1) + dot(d_up, u, 1, 1)
 
     received = [rotated(row_part((t + s) % n).astype(BF), s) for s in (2, 1, 3)]
     total = row_part(t)
@@ -111,8 +115,8 @@
         far_picker, factor[rows:], cut(layer_in, t, part, 1), cut(grad_out, t, part, 1), cols
     )
     far_got = exchange(far_sent, "col")
-    far_in = swap(far_got[:, :CAP].reshape(rows, part), "zh")
-    far_grad = swap(far_got[:, CAP:].reshape(rows, part), "zh")
+    far_in = mirrored(far_got[:, :CAP].reshape(rows, part))
+    far_grad = mirrored(far_got[:, CAP:].reshape(rows, part))
 
     near_got = exchange(picked(near_picker, factor[:rows], layer_in, grad_out, cols), "col")
     near_in = near_got[:, :CAP].reshape(rows, width)
@@ -130,32 +134,31 @@
         dot(near_in, up_full, 1, 0),
         dot(near_grad, down_full, 1, 1),
     )
-    near_rows = reduced_rows(d_gate, d_up, gate_full, up_full, part)
+    near_rows = reduced_rows(d_gate, d_up, gate_full, up_full, part, lambda r: r)
 
     gate = up = dhid = 0.0
     for s in range(n):
-        q = (t - s) % n
+        q = n - 1 - (t - s) % n
         gate = gate + dot(far_ins[s], cut(gate_full, q, part, 0), 1, 0)
         up = up + dot(far_ins[s], cut(up_full, q, part, 0), 1, 0)
         dhid = dhid + dot(far_grads[s], cut(down_full, q, part, 1), 1, 1)
     far_act, far_d_gate, far_d_up = unit_gradients(gate, up, dhid)
-    far_rows = reduced_rows(far_d_gate, far_d_up, gate_full, up_full, part)
-
-    first = my_zh == 0
-    back = jnp.stack(
-        [jnp.where(first, near_rows, far_rows), jnp.where(first, far_rows, near_rows)]
-    )
-    back = exchange(back.reshape(2 * cols, CAP, part), ("zh", "col"))
-    back = back.reshape(2, rows, part)
-    total = dot(near_picker, cut(back, my_zh, 1, 0)[0], 0, 0) + dot(
-        far_picker, cut(back, 1 - my_zh, 1, 0)[0], 0, 0
-    )
-    total = total.astype(BF)
+    far_rows = reduced_rows(
+        far_d_gate, far_d_up, gate_full, up_full, part, lambda r: n - 1 - r
+    )
+
+    def returned(x):
+        return exchange(x.reshape(cols, CAP, part), "col").reshape(rows, part)
+
+    far_back = returned(far_rows)
+    far_back = mirrored(far_back)
+    near_back = returned(near_rows)
+    total = (dot(near_picker, near_back, 0, 0) + dot(far_picker, far_back, 0, 0)).astype(BF)
 
     far_in_all, far_grad_all = jnp.stack(far_ins), jnp.stack(far_grads)
 
     def quarter(stacked, q):
-        return cut(stacked, (t - q) % n, 1, 0)[0]
+        return cut(stacked, (t + q + 1) % n, 1, 0)[0]
 
     def in_term(h, near_d, far_d):
         near = dot(cut(near_in, h, half, 1), near_d, 0, 0)

time: 202 us -> 229 us (1.13)
  waiting for transfers between devices: 58 us -> 88 us
  starting transfers between devices: 48.1 us -> 39.6 us
  matrix products: 44.3 us -> 49.5 us
  blocking collectives: 36.1 us -> 38.7 us
    ppermute x0 -> x3, waiting for transfers between devices: none -> 16.1 us  [mirrored(): lax.ppermute(x, ('zh', 'tensor'), [(z, last - z) for z in range(last + 1)])]
    all_to_all x2 -> x3, waiting for transfers between devices: 5.35 us -> 19.2 us  [exchange(): return lax.all_to_all(x, axes, split_axis=0, concat_axis=0, tiled=True)]
    ppermute x12, starting transfers between devices: 23.9 us -> 13.7 us  [rotated(): return lax.ppermute(x, 'tensor', [(i, (i + step) % n) for i in range(n)])]
    ppermute x0 -> x3, starting transfers between devices: none -> 8.9 us  [mirrored(): lax.ppermute(x, ('zh', 'tensor'), [(z, last - z) for z in range(last + 1)])]
    ppermute x12, waiting for transfers between devices: 45 us -> 52.7 us  [rotated(): return lax.ppermute(x, 'tensor', [(i, (i + step) % n) for i in range(n)])]
    ppermute x8 -> x6, waiting for transfers between devices: 7.69 us -> 0.02 us  [swap(): return lax.ppermute(x, axis, [(0, 1), (1, 0)])]
    ppermute x8 -> x6, starting transfers between devices: 7.39 us -> 0.11 us  [swap(): return lax.ppermute(x, axis, [(0, 1), (1, 0)])]
    dot_general x51, matrix products: 42 us -> 47.2 us  [dot(): lax.dot_general(a, b, (((ca,), (cb,)), ((), ())), preferred_element_type=...]
  transfers between devices with their start and end apart: 22 -> 24, of which waited for: 11 -> 15; matrix products, arithmetic and copies ran while one was open for 21% -> 20% of each run, Pallas kernels for 0% -> 0%
where the time goes in v4:
time: 229 us; the launch traced here: 228 us
  waiting for transfers between devices  88 us (38%)
  matrix products  49.5 us (22%)
  starting transfers between devices  39.6 us (17%)
  blocking collectives  38.7 us (17%)
  other arithmetic  6.29 us (3%)
  local copies, waits for them, and re-layouts  4.89 us (2%)
    ppermute x12, waiting for transfers between devices, rotated(): return lax.ppermute(x, 'tensor', [(i, (i + step) % n) for i in range(n)])  52.7 us
    dot_general x51, matrix products, dot(): lax.dot_general(a, b, (((ca,), (cb,)), ((), ())), preferred_element_type=...  47.2 us
    all_gather x1, blocking collectives, inner(): total = lax.all_gather(total, 'tensor', axis=0, tiled=False)  21.8 us
    all_to_all x3, waiting for transfers between devices, exchange(): return lax.all_to_all(x, axes, split_axis=0, concat_axis=0, tiled=True)  19.2 us
    all_to_all x3, starting transfers between devices, exchange(): return lax.all_to_all(x, axes, split_axis=0, concat_axis=0, tiled=True)  16.9 us
    all_to_all x1, blocking collectives, exchange(): return lax.all_to_all(x, axes, split_axis=0, concat_axis=0, tiled=True)  16.8 us
    ppermute x3, waiting for transfers between devices, mirrored(): lax.ppermute(x, ('zh', 'tensor'), [(z, last - z) for z in range(last + 1)])  16.1 us
    ppermute x12, starting transfers between devices, rotated(): return lax.ppermute(x, 'tensor', [(i, (i + step) % n) for i in range(n)])  13.7 us
  transfers between devices with their start and end apart: 24, of which 15 were waited for; matrix products, arithmetic and copies ran while one was open for 20% of the time, Pallas kernels for 0%

profile of v4, /device:TPU:2, one launch (start us, length us, event | category | flops | bytes accessed | tf_op | source)
XLA Modules:
  0.0 228.3 jit_solution(392151408200133286)
XLA Ops:
  0.7 0.9 fusion.128
  2.1 1.2 fusion.37
  3.6 16.8 %all_to_all.20 = bf16[16,16,896]{2,1,0:T(8,128)(2,1)S(1)} all-to-all(bf16[16,16,896]{2,1,0:T(8,128)(2,1)S(1)} %pad_maximum_fusion.6), channel_id=1, replica_groups=mesh['dp'=2,'zh'=2,'col'=16,'tensor'=4] {'col'}, dimensions={0} | all-to-all | bytes 917504 | tf_op jit(solution)/shard_map/all_to_all | solution.py:65
  20.5 5.9 %collective-permute-start.10 = (bf16[128,896]{1,0:T(8,128)(2,1)S(1)}, bf16[128,896]{1,0:T(8,128)(2,1)S(1)}, u32[]{:S(2)}, u32[]{:S(2)}) collective-permute-start(bf16[128,896]{1,0:T(8,128)(2,1)S(1)} %get-tuple-element.22), channel_id=1, source_target_pairs={{0,67},{1,66},{2,65},{3,64},{64,3},{65,2},{66,1},{67,0},{4,71},{5,... | collective-permute-start | bytes 688136 | tf_op jit(solution)/shard_map/ppermute | solution.py:51
  26.7 14.7 %collective-permute-done.10 = bf16[128,896]{1,0:T(8,128)(2,1)S(1)} collective-permute-done((bf16[128,896]{1,0:T(8,128)(2,1)S(1)}, bf16[128,896]{1,0:T(8,128)(2,1)S(1)}, u32[]{:S(2)}, u32[]{:S(2)}) %collective-permute-start.10) | collective-permute-done | bytes 229408 | tf_op jit(solution)/shard_map/ppermute | solution.py:51
  41.4 1.9 collective-permute-start.13
  43.4 0.5 collective-permute-start.12
  43.9 0.4 fusion.2
  44.3 1.3 collective-permute-done.6
  46.0 9.9 %collective-permute-done.13 = bf16[128,896]{1,0:T(8,128)(2,1)S(1)} collective-permute-done((bf16[128,896]{1,0:T(8,128)(2,1)S(1)}, bf16[128,896]{1,0:T(8,128)(2,1)S(1)}, u32[]{:S(2)}, u32[]{:S(2)}) %collective-permute-start.13) | collective-permute-done | bytes 229408 | tf_op jit(solution)/shard_map/ppermute | solution.py:70
  56.0 2.0 collective-permute-start.7
  58.0 4.6 %collective-permute-done.12 = bf16[128,896]{1,0:T(8,128)(2,1)S(1)} collective-permute-done((bf16[128,896]{1,0:T(8,128)(2,1)S(1)}, bf16[128,896]{1,0:T(8,128)(2,1)S(1)}, u32[]{:S(2)}, u32[]{:S(2)}) %collective-permute-start.12) | collective-permute-done | bytes 229408 | tf_op jit(solution)/shard_map/ppermute | solution.py:70
  62.6 1.4 pad_maximum_fusion
  64.2 3.8 %collective-permute-done.9 = bf16[128,896]{1,0:T(8,128)(2,1)S(1)} collective-permute-done((bf16[128,896]{1,0:T(8,128)(2,1)S(1)}, bf16[128,896]{1,0:T(8,128)(2,1)S(1)}, u32[]{:S(2)}, u32[]{:S(2)}) %collective-permute-start.9) | collective-permute-done | bytes 229408 | tf_op jit(solution)/shard_map/ppermute | solution.py:70
  68.1 1.0 collective-permute-done.7
  69.0 10.8 %collective-permute-done.8 = bf16[128,896]{1,0:T(8,128)(2,1)S(1)} collective-permute-done((bf16[128,896]{1,0:T(8,128)(2,1)S(1)}, bf16[128,896]{1,0:T(8,128)(2,1)S(1)}, u32[]{:S(2)}, u32[]{:S(2)}) %collective-permute-start.8) | collective-permute-done | bytes 229408 | tf_op jit(solution)/shard_map/ppermute | solution.py:70
  79.9 1.1 pad_maximum_fusion.5
  81.0 2.0 broadcast_select_fusion.1
  84.1 0.5 copy-done.30
  87.8 1.3 fusion.97
  89.1 1.2 fusion.99
  90.6 4.9 %collective-permute-start.16 = (bf16[128,896]{1,0:T(8,128)(2,1)S(1)}, bf16[128,896]{1,0:T(8,128)(2,1)S(1)}, u32[]{:S(2)}, u32[]{:S(2)}) collective-permute-start(bf16[128,896]{1,0:T(8,128)(2,1)S(1)} %fusion.33), channel_id=1, source_target_pairs={{0,3},{1,0},{2,1},{3,2},{4,7},{5,4},{6,5},{7,6},{8,11},{9,8},{10,9... | collective-permute-start | bytes 688136 | tf_op jit(solution)/shard_map/ppermute | solution.py:70
  96.8 0.6 collective-permute-start.14
  97.4 1.2 fusion.103
  99.0 2.5 %collective-permute-done.16 = bf16[128,896]{1,0:T(8,128)(2,1)S(1)} collective-permute-done((bf16[128,896]{1,0:T(8,128)(2,1)S(1)}, bf16[128,896]{1,0:T(8,128)(2,1)S(1)}, u32[]{:S(2)}, u32[]{:S(2)}) %collective-permute-start.16) | collective-permute-done | bytes 229408 | tf_op jit(solution)/shard_map/ppermute | solution.py:70
  101.5 5.1 %collective-permute-done.15 = bf16[128,896]{1,0:T(8,128)(2,1)S(1)} collective-permute-done((bf16[128,896]{1,0:T(8,128)(2,1)S(1)}, bf16[128,896]{1,0:T(8,128)(2,1)S(1)}, u32[]{:S(2)}, u32[]{:S(2)}) %collective-permute-start.15) | collective-permute-done | bytes 229408 | tf_op jit(solution)/shard_map/ppermute | solution.py:70
  106.5 7.0 %collective-permute-done.14 = bf16[128,896]{1,0:T(8,128)(2,1)S(1)} collective-permute-done((bf16[128,896]{1,0:T(8,128)(2,1)S(1)}, bf16[128,896]{1,0:T(8,128)(2,1)S(1)}, u32[]{:S(2)}, u32[]{:S(2)}) %collective-permute-start.14) | collective-permute-done | bytes 229408 | tf_op jit(solution)/shard_map/ppermute | solution.py:70
  113.5 1.0 fusion.35
  114.5 5.4 %all-to-all-start.3 = ((bf16[16,8,896]{2,1,0:T(8,128)(2,1)}), bf16[16,8,896]{2,1,0:T(8,128)(2,1)}, u32[]{:S(2)}, u32[]{:S(2)}) async-start(bf16[16,8,896]{2,1,0:T(8,128)(2,1)} %fusion.35), calls=%async_computation.3 | async-start | bytes 458752 | tf_op jit(solution)/shard_map/all_to_all | solution.py:65
  119.9 2.2 fusion.101
  122.2 5.1 %all-to-all-done.3 = bf16[16,8,896]{2,1,0:T(8,128)(2,1)} async-done(((bf16[16,8,896]{2,1,0:T(8,128)(2,1)}), bf16[16,8,896]{2,1,0:T(8,128)(2,1)}, u32[]{:S(2)}, u32[]{:S(2)}) %all-to-all-start.3) | async-done | bytes 229408 | tf_op jit(solution)/shard_map/all_to_all | solution.py:65
  127.3 5.6 %all-to-all-start = ((bf16[16,16,3584]{2,1,0:T(8,128)(2,1)}), bf16[16,16,3584]{2,1,0:T(8,128)(2,1)}, u32[]{:S(2)}, u32[]{:S(2)}) async-start(bf16[16,16,3584]{2,1,0:T(8,128)(2,1)} %pad_maximum_fusion), calls=%async_computation | async-start | bytes 3670016 | tf_op jit(solution)/shard_map/all_to_all | solution.py:65
  132.9 2.3 fusion.107
  135.2 2.3 fusion.105
  137.4 1.2 fusion.111
  138.7 1.2 fusion.109
  139.9 1.3 fusion.89
  141.2 1.3 fusion.91
  142.4 1.2 fusion.93
  143.7 2.9 %collective-permute-start.17 = (bf16[128,896]{1,0:T(8,128)(2,1)}, bf16[128,896]{1,0:T(8,128)(2,1)}, u32[]{:S(2)}, u32[]{:S(2)}) collective-permute-start(bf16[128,896]{1,0:T(8,128)(2,1)} %bitcast.18), channel_id=1, source_target_pairs={{0,67},{1,66},{2,65},{3,64},{64,3},{65,2},{66,1},{67,0},{4,71},{5,... | collective-permute-start | bytes 688136 | tf_op jit(solution)/shard_map/ppermute | solution.py:51
  146.5 9.2 %all-to-all-done = bf16[16,16,3584]{2,1,0:T(8,128)(2,1)} async-done(((bf16[16,16,3584]{2,1,0:T(8,128)(2,1)}), bf16[16,16,3584]{2,1,0:T(8,128)(2,1)}, u32[]{:S(2)}, u32[]{:S(2)}) %all-to-all-start) | async-done | bytes 1835040 | tf_op jit(solution)/shard_map/all_to_all | solution.py:65
  155.7 1.7 fusion.195
  157.5 2.0 fusion.194
  159.5 1.6 multiply_convert_fusion.1
  161.7 2.7 %collective-permute-start.5 = (bf16[128,896]{1,0:T(8,128)(2,1)S(1)}, bf16[128,896]{1,0:T(8,128)(2,1)S(1)}, u32[]{:S(2)}, u32[]{:S(2)}) collective-permute-start(bf16[128,896]{1,0:T(8,128)(2,1)S(1)} %fusion.30), channel_id=1, source_target_pairs={{0,3},{1,0},{2,1},{3,2},{4,7},{5,4},{6,5},{7,6},{8,11},{9,8},{10,9... | collective-permute-start | bytes 688136 | tf_op jit(solution)/shard_map/ppermute | solution.py:70
  166.0 0.7 collective-permute-start.3
  166.6 1.6 slice_bitcast_fusion.1
  168.3 1.4 fusion.11
  169.6 0.5 copy-done.18
  170.1 0.6 copy-done.21
  170.7 1.4 fusion.14
  172.0 1.4 fusion.17
  173.8 1.4 collective-permute-done.4
  175.2 6.6 %collective-permute-done.3 = bf16[128,896]{1,0:T(8,128)(2,1)S(1)} collective-permute-done((bf16[128,896]{1,0:T(8,128)(2,1)S(1)}, bf16[128,896]{1,0:T(8,128)(2,1)S(1)}, u32[]{:S(2)}, u32[]{:S(2)}) %collective-permute-start.3) | collective-permute-done | bytes 229408 | tf_op jit(solution)/shard_map/ppermute | solution.py:70
  181.8 1.0 fusion.36
  182.8 5.9 %all-to-all-start.1 = ((bf16[16,8,896]{2,1,0:T(8,128)(2,1)}), bf16[16,8,896]{2,1,0:T(8,128)(2,1)S(1)}, u32[]{:S(2)}, u32[]{:S(2)}) async-start(bf16[16,8,896]{2,1,0:T(8,128)(2,1)} %fusion.36), calls=%async_computation.1 | async-start | bytes 458752 | tf_op jit(solution)/shard_map/all_to_all | solution.py:65
  188.7 2.2 fusion.95
  190.9 5.0 %all-to-all-done.1 = bf16[16,8,896]{2,1,0:T(8,128)(2,1)S(1)} async-done(((bf16[16,8,896]{2,1,0:T(8,128)(2,1)}), bf16[16,8,896]{2,1,0:T(8,128)(2,1)S(1)}, u32[]{:S(2)}, u32[]{:S(2)}) %all-to-all-start.1) | async-done | bytes 229408 | tf_op jit(solution)/shard_map/all_to_all | solution.py:65
  196.1 1.2 fusion.27
  197.4 2.7 %add_convert_fusion.2 = bf16[1792,256]{1,0:T(8,128)(2,1)} fusion(bf16[1792,256]{1,0:T(8,128)(2,1)} %collective-permute-done.18, f32[896,256]{1,0:T(8,128)S(1)} %copy-done.14, f32[896,256]{1,0:T(8,128)S(1)} %copy-done.15, bf16[128,256]{1,0:T(8,128)(2,1)S(1)} %get-tuple-element.28, bf16[128,3584]{1,0:T(8,128)(2,1)S(1)} %copy-done.6, s32[]{:T(128)S(6)} %select_n.222), kind=kOutput, calls=%fused_computation.32 | convolution fusion | flops 121110528 | bytes 4194308 | tf_op jit(solution)/shard_map/dot_general | solution.py:14
  200.1 2.7 %add_convert_fusion.1 = bf16[1792,256]{1,0:T(8,128)(2,1)} fusion(bf16[1792,256]{1,0:T(8,128)(2,1)} %collective-permute-done.19, f32[896,256]{1,0:T(8,128)S(1)} %copy-done.11, f32[896,256]{1,0:T(8,128)S(1)} %copy-done.13, bf16[128,256]{1,0:T(8,128)(2,1)S(1)} %get-tuple-element.29, bf16[128,3584]{1,0:T(8,128)(2,1)S(1)} %copy-done.6, s32[]{:T(128)S(6)} %select_n.222), kind=kOutput, calls=%fused_computation.31 | convolution fusion | flops 121110528 | bytes 4194308 | tf_op jit(solution)/shard_map/dot_general | solution.py:14
  202.9 2.6 %add_convert_fusion = bf16[256,1792]{1,0:T(8,128)(2,1)} fusion(bf16[256,1792]{1,0:T(8,128)(2,1)} %collective-permute-done.20, f32[256,896]{1,0:T(8,128)S(1)} %copy-done.12, f32[256,896]{1,0:T(8,128)S(1)} %copy-done.16, bf16[128,256]{1,0:T(8,128)(2,1)S(1)} %get-tuple-element.27, bf16[128,3584]{1,0:T(8,128)(2,1)S(1)} %copy-done.10, s32[]{:T(128)S(6)} %select_n.222), kind=kOutput, calls=%fused_computation.30 | convolution fusion | flops 121110528 | bytes 4194308 | tf_op jit(solution)/shard_map/dot_general | solution.py:14
  205.5 21.8 %all-gather = bf16[512,896]{1,0:T(8,128)(2,1)S(1)} all-gather(bf16[128,896]{1,0:T(8,128)(2,1)S(1)} %fusion.27), channel_id=2, replica_groups=mesh['dp'=2,'zh'=2,'col'=16,'tensor'=4] {'tensor'}, dimensions={0}, use_global_device_ids=true | all-gather | bytes 1146880 | tf_op jit(solution)/shard_map/all_gather | solution.py:183
  227.3 1.0 copy.23
  (140 shorter events, 10.7 us)
Async XLA Ops:
  0.6 2.7 %copy-start = (bf16[128,3584]{1,0:T(8,128)(2,1)S(1)}, bf16[128,3584]{1,0:T(8,128)(2,1)}, u32[]{:S(2)}) copy-start(bf16[128,3584]{1,0:T(8,128)(2,1)} %param.7) | copy-start | bytes 2752516
  3.6 42.0 %copy-start.24 = (bf16[128,3584]{1,0:T(8,128)(2,1)S(1)}, bf16[128,3584]{1,0:T(8,128)(2,1)}, u32[]{:S(2)}) copy-start(bf16[128,3584]{1,0:T(8,128)(2,1)} %param.8) | copy-start | bytes 2752516
  20.5 20.9 %collective-permute-start.10 = (bf16[128,896]{1,0:T(8,128)(2,1)S(1)}, bf16[128,896]{1,0:T(8,128)(2,1)S(1)}, u32[]{:S(2)}, u32[]{:S(2)}) collective-permute-start(bf16[128,896]{1,0:T(8,128)(2,1)S(1)} %get-tuple-element.22), channel_id=1, source_target_pairs={{0,67},{1,66},{2,65},{3,64},{64,3},{65,2},{66,1},{67,0},{4,71},{5,... | collective-permute-start | bytes 688136 | tf_op jit(solution)/shard_map/ppermute | solution.py:51
  26.4 19.2 %collective-permute-start.6 = (bf16[128,896]{1,0:T(8,128)(2,1)S(1)}, bf16[128,896]{1,0:T(8,128)(2,1)S(1)}, u32[]{:S(2)}, u32[]{:S(2)}) collective-permute-start(bf16[128,896]{1,0:T(8,128)(2,1)S(1)} %get-tuple-element.23), channel_id=1, source_target_pairs={{0,67},{1,66},{2,65},{3,64},{64,3},{65,2},{66,1},{67,0},{4,71},{5,... | collective-permute-start | bytes 688136 | tf_op jit(solution)/shard_map/ppermute | solution.py:51
  26.5 54.5 %collective-permute-start.2 = (bf16[1792,256]{1,0:T(8,128)(2,1)}, bf16[1792,256]{1,0:T(8,128)(2,1)}, u32[]{:S(2)}, u32[]{:S(2)}) collective-permute-start(bf16[1792,256]{1,0:T(8,128)(2,1)} %bitcast.9), channel_id=1, source_target_pairs={{0,128},{128,0},{1,129},{129,1},{2,130},{130,2},{3,131},{131,3},{4... | collective-permute-start | bytes 2752520 | tf_op jit(solution)/shard_map/ppermute | solution.py:46
  41.4 14.5 %collective-permute-start.13 = (bf16[128,896]{1,0:T(8,128)(2,1)S(1)}, bf16[128,896]{1,0:T(8,128)(2,1)S(1)}, u32[]{:S(2)}, u32[]{:S(2)}) collective-permute-start(bf16[128,896]{1,0:T(8,128)(2,1)S(1)} %collective-permute-done.10), channel_id=1, source_target_pairs={{0,3},{1,0},{2,1},{3,2},{4,7},{5,4},{6,5},{7,6},{8,11},{9,8},{10,9... | collective-permute-start | bytes 688136 | tf_op jit(solution)/shard_map/ppermute | solution.py:70
  43.3 12.6 %collective-permute-start.11 = (bf16[128,896]{1,0:T(8,128)(2,1)S(1)}, bf16[128,896]{1,0:T(8,128)(2,1)S(1)}, u32[]{:S(2)}, u32[]{:S(2)}) collective-permute-start(bf16[128,896]{1,0:T(8,128)(2,1)S(1)} %collective-permute-done.10), channel_id=1, source_target_pairs={{0,1},{1,2},{2,3},{3,0},{4,5},{5,6},{6,7},{7,4},{8,9},{9,10},{10,1... | collective-permute-start | bytes 688136 | tf_op jit(solution)/shard_map/ppermute | solution.py:70
  43.4 19.2 %collective-permute-start.12 = (bf16[128,896]{1,0:T(8,128)(2,1)S(1)}, bf16[128,896]{1,0:T(8,128)(2,1)S(1)}, u32[]{:S(2)}, u32[]{:S(2)}) collective-permute-start(bf16[128,896]{1,0:T(8,128)(2,1)S(1)} %collective-permute-done.10), channel_id=1, source_target_pairs={{0,2},{1,3},{2,0},{3,1},{4,6},{5,7},{6,4},{7,5},{8,10},{9,11},{10,... | collective-permute-start | bytes 688136 | tf_op jit(solution)/shard_map/ppermute | solution.py:70
  45.6 34.2 %copy-start.25 = (bf16[128,896]{1,0:T(8,128)(2,1)}, bf16[128,896]{1,0:T(8,128)(2,1)S(1)}, u32[]{:S(2)}) copy-start(bf16[128,896]{1,0:T(8,128)(2,1)S(1)} %collective-permute-done.6) | copy-start | bytes 688132
  45.6 35.4 %collective-permute-start.1 = (bf16[1792,256]{1,0:T(8,128)(2,1)}, bf16[1792,256]{1,0:T(8,128)(2,1)}, u32[]{:S(2)}, u32[]{:S(2)}) collective-permute-start(bf16[1792,256]{1,0:T(8,128)(2,1)} %bitcast.165), channel_id=1, source_target_pairs={{0,128},{128,0},{1,129},{129,1},{2,130},{130,2},{3,131},{131,3},{4... | collective-permute-start | bytes 2752520 | tf_op jit(solution)/shard_map/ppermute | solution.py:46
  56.0 12.1 %collective-permute-start.9 = (bf16[128,896]{1,0:T(8,128)(2,1)S(1)}, bf16[128,896]{1,0:T(8,128)(2,1)S(1)}, u32[]{:S(2)}, u32[]{:S(2)}) collective-permute-start(bf16[128,896]{1,0:T(8,128)(2,1)S(1)} %collective-permute-done.6), channel_id=1, source_target_pairs={{0,3},{1,0},{2,1},{3,2},{4,7},{5,4},{6,5},{7,6},{8,11},{9,8},{10,9... | collective-permute-start | bytes 688136 | tf_op jit(solution)/shard_map/ppermute | solution.py:70
  56.0 13.1 %collective-permute-start.7 = (bf16[128,896]{1,0:T(8,128)(2,1)S(1)}, bf16[128,896]{1,0:T(8,128)(2,1)S(1)}, u32[]{:S(2)}, u32[]{:S(2)}) collective-permute-start(bf16[128,896]{1,0:T(8,128)(2,1)S(1)} %collective-permute-done.6), channel_id=1, source_target_pairs={{0,1},{1,2},{2,3},{3,0},{4,5},{5,6},{6,7},{7,4},{8,9},{9,10},{10,1... | collective-permute-start | bytes 688136 | tf_op jit(solution)/shard_map/ppermute | solution.py:70
  62.6 1.4 copy-start.31
  62.6 17.2 %collective-permute-start.8 = (bf16[128,896]{1,0:T(8,128)(2,1)S(1)}, bf16[128,896]{1,0:T(8,128)(2,1)S(1)}, u32[]{:S(2)}, u32[]{:S(2)}) collective-permute-start(bf16[128,896]{1,0:T(8,128)(2,1)S(1)} %collective-permute-done.6), channel_id=1, source_target_pairs={{0,2},{1,3},{2,0},{3,1},{4,6},{5,7},{6,4},{7,5},{8,10},{9,11},{10,... | collective-permute-start | bytes 688136 | tf_op jit(solution)/shard_map/ppermute | solution.py:70
  64.1 4.0 %copy-start.35 = (bf16[1,256,1792]{2,1,0:T(8,128)(2,1)S(1)}, bf16[1,256,1792]{2,1,0:T(8,128)(2,1)}, u32[]{:S(2)}) copy-start(bf16[1,256,1792]{2,1,0:T(8,128)(2,1)} %param.13) | copy-start | bytes 2752516
  64.1 16.9 %copy-start.36 = (bf16[1,1792,256]{2,1,0:T(8,128)(2,1)S(1)}, bf16[1,1792,256]{2,1,0:T(8,128)(2,1)}, u32[]{:S(2)}) copy-start(bf16[1,1792,256]{2,1,0:T(8,128)(2,1)} %param.12) | copy-start | bytes 2752516
  64.2 33.2 %copy-start.7 = (bf16[4,128,896]{2,1,0:T(8,128)(2,1)}, bf16[4,128,896]{2,1,0:T(8,128)(2,1)S(1)}, u32[]{:S(2)}) copy-start(bf16[4,128,896]{2,1,0:T(8,128)(2,1)S(1)} %pad_maximum_fusion.4) | copy-start | bytes 2752516
  68.1 14.9 %copy-start.29 = (bf16[128,896]{1,0:T(8,128)(2,1)}, bf16[128,896]{1,0:T(8,128)(2,1)S(1)}, u32[]{:S(2)}) copy-start(bf16[128,896]{1,0:T(8,128)(2,1)S(1)} %collective-permute-done.9) | copy-start | bytes 688132
  68.1 15.1 %collective-permute-start = (bf16[256,1792]{1,0:T(8,128)(2,1)S(1)}, bf16[256,1792]{1,0:T(8,128)(2,1)S(1)}, u32[]{:S(2)}, u32[]{:S(2)}) collective-permute-start(bf16[256,1792]{1,0:T(8,128)(2,1)S(1)} %bitcast.164), channel_id=1, source_target_pairs={{0,128},{128,0},{1,129},{129,1},{2,130},{130,2},{3,131},{131,3},{4... | collective-permute-start | bytes 2752520 | tf_op jit(solution)/shard_map/ppermute | solution.py:46
  69.0 14.0 %copy-start.27 = (bf16[128,896]{1,0:T(8,128)(2,1)}, bf16[128,896]{1,0:T(8,128)(2,1)S(1)}, u32[]{:S(2)}) copy-start(bf16[128,896]{1,0:T(8,128)(2,1)S(1)} %collective-permute-done.7) | copy-start | bytes 688132
  79.9 3.2 %copy-start.33 = (bf16[128,896]{1,0:T(8,128)(2,1)}, bf16[128,896]{1,0:T(8,128)(2,1)S(1)}, u32[]{:S(2)}) copy-start(bf16[128,896]{1,0:T(8,128)(2,1)S(1)} %collective-permute-done.8) | copy-start | bytes 688132
  83.4 3.5 %copy-start.3 = (bf16[256,3584]{1,0:T(8,128)(2,1)}, bf16[256,3584]{1,0:T(8,128)(2,1)S(1)}, u32[]{:S(2)}) copy-start(bf16[256,3584]{1,0:T(8,128)(2,1)S(1)} %pad_maximum_fusion.1) | copy-start | bytes 5505028
  83.4 1.2 copy-start.30
  83.6 15.1 %copy-start.1 = (bf16[3584,256]{1,0:T(8,128)(2,1)}, bf16[3584,256]{1,0:T(8,128)(2,1)S(1)}, u32[]{:S(2)}) copy-start(bf16[3584,256]{1,0:T(8,128)(2,1)S(1)} %pad_maximum_fusion.2) | copy-start | bytes 5505028
  83.6 1.4 copy-start.26
  85.0 1.1 copy-start.28
  85.6 1.1 copy-start.32
  85.8 1.1 copy-start.34
  90.6 10.8 %collective-permute-start.16 = (bf16[128,896]{1,0:T(8,128)(2,1)S(1)}, bf16[128,896]{1,0:T(8,128)(2,1)S(1)}, u32[]{:S(2)}, u32[]{:S(2)}) collective-permute-start(bf16[128,896]{1,0:T(8,128)(2,1)S(1)} %fusion.33), channel_id=1, source_target_pairs={{0,3},{1,0},{2,1},{3,2},{4,7},{5,4},{6,5},{7,6},{8,11},{9,8},{10,9... | collective-permute-start | bytes 688136 | tf_op jit(solution)/shard_map/ppermute | solution.py:70
  96.1 10.5 %collective-permute-start.15 = (bf16[128,896]{1,0:T(8,128)(2,1)S(1)}, bf16[128,896]{1,0:T(8,128)(2,1)S(1)}, u32[]{:S(2)}, u32[]{:S(2)}) collective-permute-start(bf16[128,896]{1,0:T(8,128)(2,1)S(1)} %fusion.32), channel_id=1, source_target_pairs={{0,1},{1,2},{2,3},{3,0},{4,5},{5,6},{6,7},{7,4},{8,9},{9,10},{10,1... | collective-permute-start | bytes 688136 | tf_op jit(solution)/shard_map/ppermute | solution.py:70
  96.8 16.7 %collective-permute-start.14 = (bf16[128,896]{1,0:T(8,128)(2,1)S(1)}, bf16[128,896]{1,0:T(8,128)(2,1)S(1)}, u32[]{:S(2)}, u32[]{:S(2)}) collective-permute-start(bf16[128,896]{1,0:T(8,128)(2,1)S(1)} %fusion.31), channel_id=1, source_target_pairs={{0,2},{1,3},{2,0},{3,1},{4,6},{5,7},{6,4},{7,5},{8,10},{9,11},{10,... | collective-permute-start | bytes 688136 | tf_op jit(solution)/shard_map/ppermute | solution.py:70
  114.5 12.7 %all-to-all-start.3 = ((bf16[16,8,896]{2,1,0:T(8,128)(2,1)}), bf16[16,8,896]{2,1,0:T(8,128)(2,1)}, u32[]{:S(2)}, u32[]{:S(2)}) async-start(bf16[16,8,896]{2,1,0:T(8,128)(2,1)} %fusion.35), calls=%async_computation.3 | async-start | bytes 458752 | tf_op jit(solution)/shard_map/all_to_all | solution.py:65
  127.3 28.4 %all-to-all-start = ((bf16[16,16,3584]{2,1,0:T(8,128)(2,1)}), bf16[16,16,3584]{2,1,0:T(8,128)(2,1)}, u32[]{:S(2)}, u32[]{:S(2)}) async-start(bf16[16,16,3584]{2,1,0:T(8,128)(2,1)} %pad_maximum_fusion), calls=%async_computation | async-start | bytes 3670016 | tf_op jit(solution)/shard_map/all_to_all | solution.py:65
  132.9 4.5 %copy-start.8 = (bf16[4,128,896]{2,1,0:T(8,128)(2,1)S(1)}, bf16[4,128,896]{2,1,0:T(8,128)(2,1)}, u32[]{:S(2)}) copy-start(bf16[4,128,896]{2,1,0:T(8,128)(2,1)} %copy-done.7) | copy-start | bytes 2752516
  135.2 4.8 %copy-start.17 = (bf16[4,128,896]{2,1,0:T(8,128)(2,1)S(1)}, bf16[4,128,896]{2,1,0:T(8,128)(2,1)}, u32[]{:S(2)}) copy-start(bf16[4,128,896]{2,1,0:T(8,128)(2,1)} %pad_maximum_fusion.5) | copy-start | bytes 2752516
  143.7 52.4 %collective-permute-start.17 = (bf16[128,896]{1,0:T(8,128)(2,1)}, bf16[128,896]{1,0:T(8,128)(2,1)}, u32[]{:S(2)}, u32[]{:S(2)}) collective-permute-start(bf16[128,896]{1,0:T(8,128)(2,1)} %bitcast.18), channel_id=1, source_target_pairs={{0,67},{1,66},{2,65},{3,64},{64,3},{65,2},{66,1},{67,0},{4,71},{5,... | collective-permute-start | bytes 688136 | tf_op jit(solution)/shard_map/ppermute | solution.py:51
  155.7 1.8 copy-start.4
  157.5 2.0 copy-start.2
  161.7 12.0 %collective-permute-start.5 = (bf16[128,896]{1,0:T(8,128)(2,1)S(1)}, bf16[128,896]{1,0:T(8,128)(2,1)S(1)}, u32[]{:S(2)}, u32[]{:S(2)}) collective-permute-start(bf16[128,896]{1,0:T(8,128)(2,1)S(1)} %fusion.30), channel_id=1, source_target_pairs={{0,3},{1,0},{2,1},{3,2},{4,7},{5,4},{6,5},{7,6},{8,11},{9,8},{10,9... | collective-permute-start | bytes 688136 | tf_op jit(solution)/shard_map/ppermute | solution.py:70
  165.0 10.2 %collective-permute-start.4 = (bf16[128,896]{1,0:T(8,128)(2,1)S(1)}, bf16[128,896]{1,0:T(8,128)(2,1)S(1)}, u32[]{:S(2)}, u32[]{:S(2)}) collective-permute-start(bf16[128,896]{1,0:T(8,128)(2,1)S(1)} %fusion.29), channel_id=1, source_target_pairs={{0,1},{1,2},{2,3},{3,0},{4,5},{5,6},{6,7},{7,4},{8,9},{9,10},{10,1... | collective-permute-start | bytes 688136 | tf_op jit(solution)/shard_map/ppermute | solution.py:70
  165.9 2.3 %copy-start.19 = (f32[896,256]{1,0:T(8,128)S(1)}, f32[896,256]{1,0:T(8,128)}, u32[]{:S(2)}) copy-start(f32[896,256]{1,0:T(8,128)} %fusion.99) | copy-start | bytes 2752516
  166.0 2.3 %copy-start.20 = (f32[896,256]{1,0:T(8,128)S(1)}, f32[896,256]{1,0:T(8,128)}, u32[]{:S(2)}) copy-start(f32[896,256]{1,0:T(8,128)} %fusion.103) | copy-start | bytes 2752516
  166.0 15.8 %collective-permute-start.3 = (bf16[128,896]{1,0:T(8,128)(2,1)S(1)}, bf16[128,896]{1,0:T(8,128)(2,1)S(1)}, u32[]{:S(2)}, u32[]{:S(2)}) collective-permute-start(bf16[128,896]{1,0:T(8,128)(2,1)S(1)} %fusion.28), channel_id=1, source_target_pairs={{0,2},{1,3},{2,0},{3,1},{4,6},{5,7},{6,4},{7,5},{8,10},{9,11},{10,... | collective-permute-start | bytes 688136 | tf_op jit(solution)/shard_map/ppermute | solution.py:70
  168.2 3.8 %copy-start.5 = (bf16[128,3584]{1,0:T(8,128)(2,1)}, bf16[128,3584]{1,0:T(8,128)(2,1)S(1)}, u32[]{:S(2)}) copy-start(bf16[128,3584]{1,0:T(8,128)(2,1)S(1)} %get-tuple-element.15) | copy-start | bytes 2752516
  168.2 3.8 %copy-start.9 = (bf16[128,3584]{1,0:T(8,128)(2,1)}, bf16[128,3584]{1,0:T(8,128)(2,1)S(1)}, u32[]{:S(2)}) copy-start(bf16[128,3584]{1,0:T(8,128)(2,1)S(1)} %get-tuple-element.14) | copy-start | bytes 2752516
  168.2 1.9 copy-start.18
  168.2 2.4 %copy-start.21 = (f32[896,256]{1,0:T(8,128)S(1)}, f32[896,256]{1,0:T(8,128)}, u32[]{:S(2)}) copy-start(f32[896,256]{1,0:T(8,128)} %fusion.101) | copy-start | bytes 2752516
  169.6 2.4 %copy-start.22 = (f32[256,896]{1,0:T(8,128)S(1)}, f32[256,896]{1,0:T(8,128)}, u32[]{:S(2)}) copy-start(f32[256,896]{1,0:T(8,128)} %fusion.89) | copy-start | bytes 2752516
  169.6 2.4 %copy-start.23 = (f32[256,896]{1,0:T(8,128)S(1)}, f32[256,896]{1,0:T(8,128)}, u32[]{:S(2)}) copy-start(f32[256,896]{1,0:T(8,128)} %fusion.91) | copy-start | bytes 2752516
  169.6 27.7 %collective-permute-start.18 = (bf16[1792,256]{1,0:T(8,128)(2,1)}, bf16[1792,256]{1,0:T(8,128)(2,1)}, u32[]{:S(2)}, u32[]{:S(2)}) collective-permute-start(bf16[1792,256]{1,0:T(8,128)(2,1)} %fusion.11), channel_id=1, source_target_pairs={{0,128},{128,0},{1,129},{129,1},{2,130},{130,2},{3,131},{131,3},{4... | collective-permute-start | bytes 2752520 | tf_op jit(solution)/shard_map/ppermute | solution.py:46
  173.7 26.4 %collective-permute-start.19 = (bf16[1792,256]{1,0:T(8,128)(2,1)}, bf16[1792,256]{1,0:T(8,128)(2,1)}, u32[]{:S(2)}, u32[]{:S(2)}) collective-permute-start(bf16[1792,256]{1,0:T(8,128)(2,1)} %fusion.14), channel_id=1, source_target_pairs={{0,128},{128,0},{1,129},{129,1},{2,130},{130,2},{3,131},{131,3},{4... | collective-permute-start | bytes 2752520 | tf_op jit(solution)/shard_map/ppermute | solution.py:46
  175.2 27.7 %collective-permute-start.20 = (bf16[256,1792]{1,0:T(8,128)(2,1)}, bf16[256,1792]{1,0:T(8,128)(2,1)}, u32[]{:S(2)}, u32[]{:S(2)}) collective-permute-start(bf16[256,1792]{1,0:T(8,128)(2,1)} %fusion.17), channel_id=1, source_target_pairs={{0,128},{128,0},{1,129},{129,1},{2,130},{130,2},{3,131},{131,3},{4... | collective-permute-start | bytes 2752520 | tf_op jit(solution)/shard_map/ppermute | solution.py:46
  182.8 14.6 %copy-start.6 = (bf16[128,3584]{1,0:T(8,128)(2,1)S(1)}, bf16[128,3584]{1,0:T(8,128)(2,1)}, u32[]{:S(2)}) copy-start(bf16[128,3584]{1,0:T(8,128)(2,1)} %copy-done.5) | copy-start | bytes 2752516
  182.8 14.6 %copy-start.14 = (f32[896,256]{1,0:T(8,128)S(1)}, f32[896,256]{1,0:T(8,128)}, u32[]{:S(2)}) copy-start(f32[896,256]{1,0:T(8,128)} %fusion.107) | copy-start | bytes 2752516
  182.8 13.1 %all-to-all-start.1 = ((bf16[16,8,896]{2,1,0:T(8,128)(2,1)}), bf16[16,8,896]{2,1,0:T(8,128)(2,1)S(1)}, u32[]{:S(2)}, u32[]{:S(2)}) async-start(bf16[16,8,896]{2,1,0:T(8,128)(2,1)} %fusion.36), calls=%async_computation.1 | async-start | bytes 458752 | tf_op jit(solution)/shard_map/all_to_all | solution.py:65
  195.8 1.5 copy-start.15
  197.3 2.8 %copy-start.11 = (f32[896,256]{1,0:T(8,128)S(1)}, f32[896,256]{1,0:T(8,128)}, u32[]{:S(2)}) copy-start(f32[896,256]{1,0:T(8,128)} %fusion.105) | copy-start | bytes 2752516
  197.3 2.8 %copy-start.13 = (f32[896,256]{1,0:T(8,128)S(1)}, f32[896,256]{1,0:T(8,128)}, u32[]{:S(2)}) copy-start(f32[896,256]{1,0:T(8,128)} %fusion.109) | copy-start | bytes 2752516
  200.1 2.8 %copy-start.10 = (bf16[128,3584]{1,0:T(8,128)(2,1)S(1)}, bf16[128,3584]{1,0:T(8,128)(2,1)}, u32[]{:S(2)}) copy-start(bf16[128,3584]{1,0:T(8,128)(2,1)} %copy-done.9) | copy-start | bytes 2752516
  200.1 2.8 %copy-start.12 = (f32[256,896]{1,0:T(8,128)S(1)}, f32[256,896]{1,0:T(8,128)}, u32[]{:S(2)}) copy-start(f32[256,896]{1,0:T(8,128)} %fusion.93) | copy-start | bytes 2752516
  200.1 2.8 %copy-start.16 = (f32[256,896]{1,0:T(8,128)S(1)}, f32[256,896]{1,0:T(8,128)}, u32[]{:S(2)}) copy-start(f32[256,896]{1,0:T(8,128)} %fusion.95) | copy-start | bytes 2752516

commit v5 on v4

--- a/solution.py
+++ b/solution.py
@@ -134,7 +134,10 @@
         dot(near_in, up_full, 1, 0),
         dot(near_grad, down_full, 1, 1),
     )
-    near_rows = reduced_rows(d_gate, d_up, gate_full, up_full, part, lambda r: r)
+    near_rows = (dot(d_gate, gate_full, 1, 1) + dot(d_up, up_full, 1, 1)).astype(BF)
+    near_back = exchange(near_rows.reshape(cols, CAP, width), "col").reshape(rows, width)
+    near_sum = dot(near_picker, near_back, 0, 0).astype(BF)
+    near_parts = [rotated(cut(near_sum, (t + s) % n, part, 1), s) for s in (2, 1, 3)]
 
     gate = up = dhid = 0.0
     for s in range(n):
@@ -152,10 +155,13 @@
 
     far_back = returned(far_rows)
     far_back = mirrored(far_back)
-    near_back = returned(near_rows)
-    total = (dot(near_picker, near_back, 0, 0) + dot(far_picker, far_back, 0, 0)).astype(BF)
-
-    far_in_all, far_grad_all = jnp.stack(far_ins), jnp.stack(far_grads)
+    total = cut(near_sum, t, part, 1).astype(F32)
+    for piece in near_parts:
+        total = total + piece.astype(F32)
+    total = (total + dot(far_picker, far_back, 0, 0)).astype(BF)
+
+    far_in_all = jnp.stack(far_ins)
+    far_grad_all = jnp.stack(far_grads)
 
     def quarter(stacked, q):
         return cut(stacked, (t + q + 1) % n, 1, 0)[0]

time: 229 us -> 203 us (0.89)
  the two profiles are of different devices: /device:TPU:2 before, /device:TPU:1 now
where the time goes in v5:
time: 203 us; the launch traced here: 202 us
  waiting for transfers between devices  57.9 us (29%)
  matrix products  47.8 us (24%)
  starting transfers between devices  47.8 us (24%)
  blocking collectives  34.9 us (17%)
  local copies, waits for them, and re-layouts  6.18 us (3%)
  other arithmetic  5.57 us (3%)
    dot_general x45, matrix products, dot(): lax.dot_general(a, b, (((ca,), (cb,)), ((), ())), preferred_element_type=...  45.5 us
    ppermute x12, waiting for transfers between devices, rotated(): return lax.ppermute(x, 'tensor', [(i, (i + step) % n) for i in range(n)])  40 us
    all_to_all x3, starting transfers between devices, exchange(): return lax.all_to_all(x, axes, split_axis=0, concat_axis=0, tiled=True)  18.2 us
    all_to_all x1, blocking collectives, exchange(): return lax.all_to_all(x, axes, split_axis=0, concat_axis=0, tiled=True)  17.4 us
    all_gather x1, blocking collectives, inner(): total = lax.all_gather(total, 'tensor', axis=0, tiled=False)  17.4 us
    ppermute x3, waiting for transfers between devices, mirrored(): lax.ppermute(x, ('zh', 'tensor'), [(z, last - z) for z in range(last + 1)])  15.7 us
    ppermute x12, starting transfers between devices, rotated(): return lax.ppermute(x, 'tensor', [(i, (i + step) % n) for i in range(n)])  11.5 us
    ppermute x6, starting transfers between devices, swap(): return lax.ppermute(x, axis, [(0, 1), (1, 0)])  10.1 us
  transfers between devices with their start and end apart: 24, of which 10 were waited for; matrix products, arithmetic and copies ran while one was open for 27% of the time, Pallas kernels for 0%

profile of v5, /device:TPU:1, one launch (start us, length us, event | category | flops | bytes accessed | tf_op | source)
XLA Modules:
  0.0 201.5 jit_solution(11413879186650502851)
XLA Ops:
  0.7 0.9 fusion.110
  2.1 1.2 fusion.31
  3.6 17.4 %all_to_all.20 = bf16[16,16,896]{2,1,0:T(8,128)(2,1)S(1)} all-to-all(bf16[16,16,896]{2,1,0:T(8,128)(2,1)S(1)} %pad_maximum_fusion.6), channel_id=1, replica_groups=mesh['dp'=2,'zh'=2,'col'=16,'tensor'=4] {'col'}, dimensions={0} | all-to-all | bytes 917504 | tf_op jit(solution)/shard_map/all_to_all | solution.py:65
  21.1 5.7 %collective-permute-start.10 = (bf16[128,896]{1,0:T(8,128)(2,1)S(1)}, bf16[128,896]{1,0:T(8,128)(2,1)S(1)}, u32[]{:S(2)}, u32[]{:S(2)}) collective-permute-start(bf16[128,896]{1,0:T(8,128)(2,1)S(1)} %get-tuple-element.25), channel_id=1, source_target_pairs={{0,67},{1,66},{2,65},{3,64},{64,3},{65,2},{66,1},{67,0},{4,71},{5,... | collective-permute-start | bytes 688136 | tf_op jit(solution)/shard_map/ppermute | solution.py:51
  26.9 2.1 %collective-permute-start.2 = (bf16[1792,256]{1,0:T(8,128)(2,1)}, bf16[1792,256]{1,0:T(8,128)(2,1)}, u32[]{:S(2)}, u32[]{:S(2)}) collective-permute-start(bf16[1792,256]{1,0:T(8,128)(2,1)} %bitcast.9), channel_id=1, source_target_pairs={{0,128},{128,0},{1,129},{129,1},{2,130},{130,2},{3,131},{131,3},{4... | collective-permute-start | bytes 2752520 | tf_op jit(solution)/shard_map/ppermute | solution.py:46
  29.1 13.1 %collective-permute-done.10 = bf16[128,896]{1,0:T(8,128)(2,1)S(1)} collective-permute-done((bf16[128,896]{1,0:T(8,128)(2,1)S(1)}, bf16[128,896]{1,0:T(8,128)(2,1)S(1)}, u32[]{:S(2)}, u32[]{:S(2)}) %collective-permute-start.10) | collective-permute-done | bytes 229408 | tf_op jit(solution)/shard_map/ppermute | solution.py:51
  42.2 1.6 collective-permute-start.13
  44.1 0.4 fusion.5
  44.5 2.6 %collective-permute-done.6 = bf16[128,896]{1,0:T(8,128)(2,1)S(1)} collective-permute-done((bf16[128,896]{1,0:T(8,128)(2,1)S(1)}, bf16[128,896]{1,0:T(8,128)(2,1)S(1)}, u32[]{:S(2)}, u32[]{:S(2)}) %collective-permute-start.6) | collective-permute-done | bytes 229408 | tf_op jit(solution)/shard_map/ppermute | solution.py:51
  47.1 0.9 collective-permute-start.1
  48.1 0.4 fusion.4
  48.5 5.3 %collective-permute-done.13 = bf16[128,896]{1,0:T(8,128)(2,1)S(1)} collective-permute-done((bf16[128,896]{1,0:T(8,128)(2,1)S(1)}, bf16[128,896]{1,0:T(8,128)(2,1)S(1)}, u32[]{:S(2)}, u32[]{:S(2)}) %collective-permute-start.13) | collective-permute-done | bytes 229408 | tf_op jit(solution)/shard_map/ppermute | solution.py:70
  53.8 1.5 collective-permute-start.7
  55.3 4.4 %collective-permute-done.12 = bf16[128,896]{1,0:T(8,128)(2,1)S(1)} collective-permute-done((bf16[128,896]{1,0:T(8,128)(2,1)S(1)}, bf16[128,896]{1,0:T(8,128)(2,1)S(1)}, u32[]{:S(2)}, u32[]{:S(2)}) %collective-permute-start.12) | collective-permute-done | bytes 229408 | tf_op jit(solution)/shard_map/ppermute | solution.py:70
  59.7 0.5 collective-permute-start.8
  60.1 1.4 pad_maximum_fusion
  61.5 4.4 %all-to-all-start = ((bf16[16,16,3584]{2,1,0:T(8,128)(2,1)}), bf16[16,16,3584]{2,1,0:T(8,128)(2,1)}, u32[]{:S(2)}, u32[]{:S(2)}) async-start(bf16[16,16,3584]{2,1,0:T(8,128)(2,1)} %pad_maximum_fusion), calls=%async_computation | async-start | bytes 3670016 | tf_op jit(solution)/shard_map/all_to_all | solution.py:65
  66.4 1.1 copy-done.30
  67.5 4.9 %collective-permute-start = (bf16[256,1792]{1,0:T(8,128)(2,1)S(1)}, bf16[256,1792]{1,0:T(8,128)(2,1)S(1)}, u32[]{:S(2)}, u32[]{:S(2)}) collective-permute-start(bf16[256,1792]{1,0:T(8,128)(2,1)S(1)} %bitcast.164), channel_id=1, source_target_pairs={{0,128},{128,0},{1,129},{129,1},{2,130},{130,2},{3,131},{131,3},{4... | collective-permute-start | bytes 2752520 | tf_op jit(solution)/shard_map/ppermute | solution.py:46
  72.4 7.9 %collective-permute-done.8 = bf16[128,896]{1,0:T(8,128)(2,1)S(1)} collective-permute-done((bf16[128,896]{1,0:T(8,128)(2,1)S(1)}, bf16[128,896]{1,0:T(8,128)(2,1)S(1)}, u32[]{:S(2)}, u32[]{:S(2)}) %collective-permute-start.8) | collective-permute-done | bytes 229408 | tf_op jit(solution)/shard_map/ppermute | solution.py:70
  80.5 2.3 %broadcast_select_fusion.1 = (bf16[1792,256]{1,0:T(8,128)(2,1)S(1)}, bf16[1792,256]{1,0:T(8,128)(2,1)S(1)}, bf16[1792,256]{1,0:T(8,128)(2,1)S(1)}, bf16[1792,256]{1,0:T(8,128)(2,1)S(1)}) fusion(bf16[1792,256]{1,0:T(8,128)(2,1)} %collective-permute-done.2, pred[]{:T(512)S(6)} %eq.60, bf16[1,1792,256]{2,1,0:T(8,128)(2,1)} %param.11, ...), kind=kLoop, calls=%fused_computation.70 | loop fusion | flops 1835008 | bytes 7340033 | tf_op jit(solution)/shard_map/jit(_where)/select_n | solution.py:59
  83.9 0.5 copy-done.25
  85.9 0.3 convolution_add_fusion.16
  87.3 1.2 fusion.82
  88.6 1.2 fusion.86
  89.8 1.3 fusion.80
  91.1 1.3 fusion.84
  92.4 1.3 fusion.90
  93.6 1.3 fusion.88
  95.5 4.7 %collective-permute-start.16 = (bf16[128,896]{1,0:T(8,128)(2,1)S(1)}, bf16[128,896]{1,0:T(8,128)(2,1)S(1)}, u32[]{:S(2)}, u32[]{:S(2)}) collective-permute-start(bf16[128,896]{1,0:T(8,128)(2,1)S(1)} %fusion.28), channel_id=1, source_target_pairs={{0,3},{1,0},{2,1},{3,2},{4,7},{5,4},{6,5},{7,6},{8,11},{9,8},{10,9... | collective-permute-start | bytes 688136 | tf_op jit(solution)/shard_map/ppermute | solution.py:70
  101.5 0.4 collective-permute-start.14
  101.9 1.3 fusion.94
  103.2 1.2 fusion.92
  104.4 1.2 fusion.72
  105.7 1.2 fusion.74
  106.9 1.3 fusion.76
  108.5 1.3 collective-permute-done.15
  109.8 10.2 %collective-permute-done.14 = bf16[128,896]{1,0:T(8,128)(2,1)S(1)} collective-permute-done((bf16[128,896]{1,0:T(8,128)(2,1)S(1)}, bf16[128,896]{1,0:T(8,128)(2,1)S(1)}, u32[]{:S(2)}, u32[]{:S(2)}) %collective-permute-start.14) | collective-permute-done | bytes 229408 | tf_op jit(solution)/shard_map/ppermute | solution.py:70
  120.0 1.0 fusion.30
  121.0 7.0 %all-to-all-start.3 = ((bf16[16,8,896]{2,1,0:T(8,128)(2,1)}), bf16[16,8,896]{2,1,0:T(8,128)(2,1)S(1)}, u32[]{:S(2)}, u32[]{:S(2)}) async-start(bf16[16,8,896]{2,1,0:T(8,128)(2,1)} %fusion.30), calls=%async_computation.3 | async-start | bytes 458752 | tf_op jit(solution)/shard_map/all_to_all | solution.py:65
  128.0 1.7 fusion.172
  129.7 2.0 %fusion.171 = f32[128,256]{1,0:T(8,128)S(1)} fusion(bf16[256,3584]{1,0:T(8,128)(2,1)S(1)} %copy-done.4, bf16[16,16,3584]{2,1,0:T(8,128)(2,1)} %all-to-all-done), kind=kOutput, calls=%fused_computation.232 | convolution fusion | flops 234881024 | bytes 2883584 | tf_op jit(solution)/shard_map/dot_general | solution.py:14
  131.8 1.6 multiply_convert_fusion.1
  133.4 0.7 fusion.176
  134.1 2.8 %slice_bitcast_fusion.1 = (bf16[128,3584]{1,0:T(8,128)(2,1)}, bf16[128,3584]{1,0:T(8,128)(2,1)}) fusion(bf16[16,16,3584]{2,1,0:T(8,128)(2,1)} %all-to-all-done), kind=kLoop, calls=%fused_computation.65 | loop fusion | bytes 3670016 | tf_op jit(solution)/shard_map/reshape | solution.py:123
  136.9 1.7 fusion.3
  138.6 6.8 %all-to-all-start.1 = ((bf16[16,8,3584]{2,1,0:T(8,128)(2,1)}), bf16[16,8,3584]{2,1,0:T(8,128)(2,1)}, u32[]{:S(2)}, u32[]{:S(2)}) async-start(bf16[16,8,3584]{2,1,0:T(8,128)(2,1)} %fusion.3), calls=%async_computation.1 | async-start | bytes 1835008 | tf_op jit(solution)/shard_map/all_to_all | solution.py:65
  145.5 2.7 %fusion.14 = bf16[1792,256]{1,0:T(8,128)(2,1)} fusion(bf16[128,256]{1,0:T(8,128)(2,1)S(1)} %get-tuple-element.31, f32[896,256]{1,0:T(8,128)S(1)} %copy-done.16, f32[896,256]{1,0:T(8,128)} %fusion.86, bf16[128,3584]{1,0:T(8,128)(2,1)S(1)} %copy-done.5, s32[]{:T(128)S(6)} %select_n.223), kind=kOutput, calls=%fused_computation.24 | convolution fusion | flops 119275520 | bytes 3276804 | tf_op jit(solution)/shard_map/dot_general | solution.py:14
  148.2 1.7 collective-permute-start.18
  149.9 2.2 %fusion.78 = f32[256,896]{1,0:T(8,128)} fusion(bf16[128,256]{1,0:T(8,128)(2,1)S(1)} %get-tuple-element.27, bf16[4,128,896]{2,1,0:T(8,128)(2,1)} %copy-done.13, s32[]{:T(128)S(6)} %select_n.220), kind=kOutput, calls=%fused_computation.121 | convolution fusion | flops 58720256 | bytes 1212420 | tf_op jit(solution)/shard_map/dot_general | solution.py:14
  152.1 2.1 %collective-permute-start.17 = (bf16[128,896]{1,0:T(8,128)(2,1)}, bf16[128,896]{1,0:T(8,128)(2,1)S(1)}, u32[]{:S(2)}, u32[]{:S(2)}) collective-permute-start(bf16[128,896]{1,0:T(8,128)(2,1)} %bitcast.166), channel_id=1, source_target_pairs={{0,67},{1,66},{2,65},{3,64},{64,3},{65,2},{66,1},{67,0},{4,71},{5,... | collective-permute-start | bytes 688136 | tf_op jit(solution)/shard_map/ppermute | solution.py:51
  154.2 1.4 fusion.17
  155.8 1.4 fusion.20
  157.4 2.1 %all-to-all-done.1 = bf16[16,8,3584]{2,1,0:T(8,128)(2,1)} async-done(((bf16[16,8,3584]{2,1,0:T(8,128)(2,1)}), bf16[16,8,3584]{2,1,0:T(8,128)(2,1)}, u32[]{:S(2)}, u32[]{:S(2)}) %all-to-all-start.1) | async-done | bytes 917536 | tf_op jit(solution)/shard_map/all_to_all | solution.py:65
  159.6 1.8 fusion
  161.4 2.2 %collective-permute-start.5 = (bf16[128,896]{1,0:T(8,128)(2,1)S(1)}, bf16[128,896]{1,0:T(8,128)(2,1)S(1)}, u32[]{:S(2)}, u32[]{:S(2)}) collective-permute-start(bf16[128,896]{1,0:T(8,128)(2,1)S(1)} %get-tuple-element.23), channel_id=1, source_target_pairs={{0,3},{1,0},{2,1},{3,2},{4,7},{5,4},{6,5},{7,6},{8,11},{9,8},{10,9... | collective-permute-start | bytes 688136 | tf_op jit(solution)/shard_map/ppermute | solution.py:70
  163.7 2.7 %add_convert_fusion.2 = bf16[1792,256]{1,0:T(8,128)(2,1)} fusion(bf16[1792,256]{1,0:T(8,128)(2,1)} %collective-permute-done.18, f32[896,256]{1,0:T(8,128)S(1)} %copy-done.8, f32[896,256]{1,0:T(8,128)S(1)} %copy-done.11, bf16[128,256]{1,0:T(8,128)(2,1)S(1)} %get-tuple-element.31, bf16[128,3584]{1,0:T(8,128)(2,1)S(1)} %copy-done.5, s32[]{:T(128)S(6)} %select_n.218), kind=kOutput, calls=%fused_computation.37 | convolution fusion | flops 121110528 | bytes 4194308 | tf_op jit(solution)/shard_map/dot_general | solution.py:14
  166.4 0.3 collective-permute-start.3
  166.7 2.7 %add_convert_fusion.1 = bf16[1792,256]{1,0:T(8,128)(2,1)} fusion(bf16[1792,256]{1,0:T(8,128)(2,1)} %collective-permute-done.19, f32[896,256]{1,0:T(8,128)S(1)} %copy-done.7, f32[896,256]{1,0:T(8,128)S(1)} %copy-done.10, bf16[128,256]{1,0:T(8,128)(2,1)S(1)} %get-tuple-element.32, bf16[128,3584]{1,0:T(8,128)(2,1)S(1)} %copy-done.5, s32[]{:T(128)S(6)} %select_n.218), kind=kOutput, calls=%fused_computation.36 | convolution fusion | flops 121110528 | bytes 4194308 | tf_op jit(solution)/shard_map/dot_general | solution.py:14
  169.4 2.6 %add_convert_fusion = bf16[256,1792]{1,0:T(8,128)(2,1)} fusion(bf16[256,1792]{1,0:T(8,128)(2,1)} %collective-permute-done.20, f32[256,896]{1,0:T(8,128)S(1)} %copy-done.9, f32[256,896]{1,0:T(8,128)S(1)} %copy-done.12, bf16[128,256]{1,0:T(8,128)(2,1)S(1)} %get-tuple-element.30, bf16[128,3584]{1,0:T(8,128)(2,1)S(1)} %copy-done.6, s32[]{:T(128)S(6)} %select_n.218), kind=kOutput, calls=%fused_computation.35 | convolution fusion | flops 121110528 | bytes 4194308 | tf_op jit(solution)/shard_map/dot_general | solution.py:14
  172.1 1.0 collective-permute-done.4
  173.0 9.8 %collective-permute-done.3 = bf16[128,896]{1,0:T(8,128)(2,1)S(1)} collective-permute-done((bf16[128,896]{1,0:T(8,128)(2,1)S(1)}, bf16[128,896]{1,0:T(8,128)(2,1)S(1)}, u32[]{:S(2)}, u32[]{:S(2)}) %collective-permute-start.3) | collective-permute-done | bytes 229408 | tf_op jit(solution)/shard_map/ppermute | solution.py:70
  183.1 17.4 %all-gather = bf16[512,896]{1,0:T(8,128)(2,1)S(1)} all-gather(bf16[128,896]{1,0:T(8,128)(2,1)S(1)} %add_convert_fusion.3), channel_id=2, replica_groups=mesh['dp'=2,'zh'=2,'col'=16,'tensor'=4] {'tensor'}, dimensions={0}, use_global_device_ids=true | all-gather | bytes 1146880 | tf_op jit(solution)/shard_map/all_gather | solution.py:189
  200.5 1.0 copy.23
  (127 shorter events, 8.4 us)
Async XLA Ops:
  0.6 2.7 %copy-start = (bf16[128,3584]{1,0:T(8,128)(2,1)S(1)}, bf16[128,3584]{1,0:T(8,128)(2,1)}, u32[]{:S(2)}) copy-start(bf16[128,3584]{1,0:T(8,128)(2,1)} %param.7) | copy-start | bytes 2752516
  3.6 44.5 %copy-start.19 = (bf16[128,3584]{1,0:T(8,128)(2,1)S(1)}, bf16[128,3584]{1,0:T(8,128)(2,1)}, u32[]{:S(2)}) copy-start(bf16[128,3584]{1,0:T(8,128)(2,1)} %param.8) | copy-start | bytes 2752516
  21.1 21.1 %collective-permute-start.10 = (bf16[128,896]{1,0:T(8,128)(2,1)S(1)}, bf16[128,896]{1,0:T(8,128)(2,1)S(1)}, u32[]{:S(2)}, u32[]{:S(2)}) collective-permute-start(bf16[128,896]{1,0:T(8,128)(2,1)S(1)} %get-tuple-element.25), channel_id=1, source_target_pairs={{0,67},{1,66},{2,65},{3,64},{64,3},{65,2},{66,1},{67,0},{4,71},{5,... | collective-permute-start | bytes 688136 | tf_op jit(solution)/shard_map/ppermute | solution.py:51
  26.8 20.4 %collective-permute-start.6 = (bf16[128,896]{1,0:T(8,128)(2,1)S(1)}, bf16[128,896]{1,0:T(8,128)(2,1)S(1)}, u32[]{:S(2)}, u32[]{:S(2)}) collective-permute-start(bf16[128,896]{1,0:T(8,128)(2,1)S(1)} %get-tuple-element.26), channel_id=1, source_target_pairs={{0,67},{1,66},{2,65},{3,64},{64,3},{65,2},{66,1},{67,0},{4,71},{5,... | collective-permute-start | bytes 688136 | tf_op jit(solution)/shard_map/ppermute | solution.py:51
  26.9 53.6 %collective-permute-start.2 = (bf16[1792,256]{1,0:T(8,128)(2,1)}, bf16[1792,256]{1,0:T(8,128)(2,1)}, u32[]{:S(2)}, u32[]{:S(2)}) collective-permute-start(bf16[1792,256]{1,0:T(8,128)(2,1)} %bitcast.9), channel_id=1, source_target_pairs={{0,128},{128,0},{1,129},{129,1},{2,130},{130,2},{3,131},{131,3},{4... | collective-permute-start | bytes 2752520 | tf_op jit(solution)/shard_map/ppermute | solution.py:46
  42.2 11.6 %collective-permute-start.13 = (bf16[128,896]{1,0:T(8,128)(2,1)S(1)}, bf16[128,896]{1,0:T(8,128)(2,1)S(1)}, u32[]{:S(2)}, u32[]{:S(2)}) collective-permute-start(bf16[128,896]{1,0:T(8,128)(2,1)S(1)} %collective-permute-done.10), channel_id=1, source_target_pairs={{0,3},{1,0},{2,1},{3,2},{4,7},{5,4},{6,5},{7,6},{8,11},{9,8},{10,9... | collective-permute-start | bytes 688136 | tf_op jit(solution)/shard_map/ppermute | solution.py:70
  43.8 10.0 %collective-permute-start.11 = (bf16[128,896]{1,0:T(8,128)(2,1)S(1)}, bf16[128,896]{1,0:T(8,128)(2,1)S(1)}, u32[]{:S(2)}, u32[]{:S(2)}) collective-permute-start(bf16[128,896]{1,0:T(8,128)(2,1)S(1)} %collective-permute-done.10), channel_id=1, source_target_pairs={{0,1},{1,2},{2,3},{3,0},{4,5},{5,6},{6,7},{7,4},{8,9},{9,10},{10,1... | collective-permute-start | bytes 688136 | tf_op jit(solution)/shard_map/ppermute | solution.py:70
  43.8 15.8 %collective-permute-start.12 = (bf16[128,896]{1,0:T(8,128)(2,1)S(1)}, bf16[128,896]{1,0:T(8,128)(2,1)S(1)}, u32[]{:S(2)}, u32[]{:S(2)}) collective-permute-start(bf16[128,896]{1,0:T(8,128)(2,1)S(1)} %collective-permute-done.10), channel_id=1, source_target_pairs={{0,2},{1,3},{2,0},{3,1},{4,6},{5,7},{6,4},{7,5},{8,10},{9,11},{10,... | collective-permute-start | bytes 688136 | tf_op jit(solution)/shard_map/ppermute | solution.py:70
  47.1 33.2 %copy-start.20 = (bf16[128,896]{1,0:T(8,128)(2,1)}, bf16[128,896]{1,0:T(8,128)(2,1)S(1)}, u32[]{:S(2)}) copy-start(bf16[128,896]{1,0:T(8,128)(2,1)S(1)} %collective-permute-done.6) | copy-start | bytes 688132
  47.1 33.4 %collective-permute-start.1 = (bf16[1792,256]{1,0:T(8,128)(2,1)}, bf16[1792,256]{1,0:T(8,128)(2,1)}, u32[]{:S(2)}, u32[]{:S(2)}) collective-permute-start(bf16[1792,256]{1,0:T(8,128)(2,1)} %bitcast.165), channel_id=1, source_target_pairs={{0,128},{128,0},{1,129},{129,1},{2,130},{130,2},{3,131},{131,3},{4... | collective-permute-start | bytes 2752520 | tf_op jit(solution)/shard_map/ppermute | solution.py:46
  53.8 12.6 %collective-permute-start.9 = (bf16[128,896]{1,0:T(8,128)(2,1)S(1)}, bf16[128,896]{1,0:T(8,128)(2,1)S(1)}, u32[]{:S(2)}, u32[]{:S(2)}) collective-permute-start(bf16[128,896]{1,0:T(8,128)(2,1)S(1)} %collective-permute-done.6), channel_id=1, source_target_pairs={{0,3},{1,0},{2,1},{3,2},{4,7},{5,4},{6,5},{7,6},{8,11},{9,8},{10,9... | collective-permute-start | bytes 688136 | tf_op jit(solution)/shard_map/ppermute | solution.py:70
  53.8 18.6 %collective-permute-start.7 = (bf16[128,896]{1,0:T(8,128)(2,1)S(1)}, bf16[128,896]{1,0:T(8,128)(2,1)S(1)}, u32[]{:S(2)}, u32[]{:S(2)}) collective-permute-start(bf16[128,896]{1,0:T(8,128)(2,1)S(1)} %collective-permute-done.6), channel_id=1, source_target_pairs={{0,1},{1,2},{2,3},{3,0},{4,5},{5,6},{6,7},{7,4},{8,9},{9,10},{10,1... | collective-permute-start | bytes 688136 | tf_op jit(solution)/shard_map/ppermute | solution.py:70
  59.7 6.6 %copy-start.26 = (bf16[128,896]{1,0:T(8,128)(2,1)}, bf16[128,896]{1,0:T(8,128)(2,1)S(1)}, u32[]{:S(2)}) copy-start(bf16[128,896]{1,0:T(8,128)(2,1)S(1)} %collective-permute-done.12) | copy-start | bytes 688132
  59.7 20.7 %collective-permute-start.8 = (bf16[128,896]{1,0:T(8,128)(2,1)S(1)}, bf16[128,896]{1,0:T(8,128)(2,1)S(1)}, u32[]{:S(2)}, u32[]{:S(2)}) collective-permute-start(bf16[128,896]{1,0:T(8,128)(2,1)S(1)} %collective-permute-done.6), channel_id=1, source_target_pairs={{0,2},{1,3},{2,0},{3,1},{4,6},{5,7},{6,4},{7,5},{8,10},{9,11},{10,... | collective-permute-start | bytes 688136 | tf_op jit(solution)/shard_map/ppermute | solution.py:70
  61.5 59.5 %all-to-all-start = ((bf16[16,16,3584]{2,1,0:T(8,128)(2,1)}), bf16[16,16,3584]{2,1,0:T(8,128)(2,1)}, u32[]{:S(2)}, u32[]{:S(2)}) async-start(bf16[16,16,3584]{2,1,0:T(8,128)(2,1)} %pad_maximum_fusion), calls=%async_computation | async-start | bytes 3670016 | tf_op jit(solution)/shard_map/all_to_all | solution.py:65
  66.2 1.3 copy-start.30
  66.2 14.3 %copy-start.31 = (bf16[1,1792,256]{2,1,0:T(8,128)(2,1)S(1)}, bf16[1,1792,256]{2,1,0:T(8,128)(2,1)}, u32[]{:S(2)}) copy-start(bf16[1,1792,256]{2,1,0:T(8,128)(2,1)} %param.12) | copy-start | bytes 2752516
  66.4 16.4 %copy-start.24 = (bf16[128,896]{1,0:T(8,128)(2,1)}, bf16[128,896]{1,0:T(8,128)(2,1)S(1)}, u32[]{:S(2)}) copy-start(bf16[128,896]{1,0:T(8,128)(2,1)S(1)} %collective-permute-done.9) | copy-start | bytes 688132
  67.5 15.5 %collective-permute-start = (bf16[256,1792]{1,0:T(8,128)(2,1)S(1)}, bf16[256,1792]{1,0:T(8,128)(2,1)S(1)}, u32[]{:S(2)}, u32[]{:S(2)}) collective-permute-start(bf16[256,1792]{1,0:T(8,128)(2,1)S(1)} %bitcast.164), channel_id=1, source_target_pairs={{0,128},{128,0},{1,129},{129,1},{2,130},{130,2},{3,131},{131,3},{4... | collective-permute-start | bytes 2752520 | tf_op jit(solution)/shard_map/ppermute | solution.py:46
  72.4 10.4 %copy-start.22 = (bf16[128,896]{1,0:T(8,128)(2,1)}, bf16[128,896]{1,0:T(8,128)(2,1)S(1)}, u32[]{:S(2)}) copy-start(bf16[128,896]{1,0:T(8,128)(2,1)S(1)} %collective-permute-done.7) | copy-start | bytes 688132
  80.3 2.5 %copy-start.28 = (bf16[128,896]{1,0:T(8,128)(2,1)}, bf16[128,896]{1,0:T(8,128)(2,1)S(1)}, u32[]{:S(2)}) copy-start(bf16[128,896]{1,0:T(8,128)(2,1)S(1)} %collective-permute-done.8) | copy-start | bytes 688132
  80.5 26.4 %copy-start.13 = (bf16[4,128,896]{2,1,0:T(8,128)(2,1)}, bf16[4,128,896]{2,1,0:T(8,128)(2,1)S(1)}, u32[]{:S(2)}) copy-start(bf16[4,128,896]{2,1,0:T(8,128)(2,1)S(1)} %pad_maximum_fusion.5) | copy-start | bytes 2752516
  83.2 3.5 %copy-start.3 = (bf16[256,3584]{1,0:T(8,128)(2,1)}, bf16[256,3584]{1,0:T(8,128)(2,1)S(1)}, u32[]{:S(2)}) copy-start(bf16[256,3584]{1,0:T(8,128)(2,1)S(1)} %pad_maximum_fusion.1) | copy-start | bytes 5505028
  83.2 1.2 copy-start.25
  83.4 24.8 %copy-start.1 = (bf16[3584,256]{1,0:T(8,128)(2,1)}, bf16[3584,256]{1,0:T(8,128)(2,1)S(1)}, u32[]{:S(2)}) copy-start(bf16[3584,256]{1,0:T(8,128)(2,1)S(1)} %pad_maximum_fusion.2) | copy-start | bytes 5505028
  83.4 1.4 copy-start.21
  84.8 1.1 copy-start.23
  85.4 1.1 copy-start.27
  85.7 1.1 copy-start.29
  95.5 12.9 %collective-permute-start.16 = (bf16[128,896]{1,0:T(8,128)(2,1)S(1)}, bf16[128,896]{1,0:T(8,128)(2,1)S(1)}, u32[]{:S(2)}, u32[]{:S(2)}) collective-permute-start(bf16[128,896]{1,0:T(8,128)(2,1)S(1)} %fusion.28), channel_id=1, source_target_pairs={{0,3},{1,0},{2,1},{3,2},{4,7},{5,4},{6,5},{7,6},{8,11},{9,8},{10,9... | collective-permute-start | bytes 688136 | tf_op jit(solution)/shard_map/ppermute | solution.py:70
  100.8 8.9 %collective-permute-start.15 = (bf16[128,896]{1,0:T(8,128)(2,1)S(1)}, bf16[128,896]{1,0:T(8,128)(2,1)S(1)}, u32[]{:S(2)}, u32[]{:S(2)}) collective-permute-start(bf16[128,896]{1,0:T(8,128)(2,1)S(1)} %fusion.27), channel_id=1, source_target_pairs={{0,1},{1,2},{2,3},{3,0},{4,5},{5,6},{6,7},{7,4},{8,9},{9,10},{10,1... | collective-permute-start | bytes 688136 | tf_op jit(solution)/shard_map/ppermute | solution.py:70
  101.5 18.4 %collective-permute-start.14 = (bf16[128,896]{1,0:T(8,128)(2,1)S(1)}, bf16[128,896]{1,0:T(8,128)(2,1)S(1)}, u32[]{:S(2)}, u32[]{:S(2)}) collective-permute-start(bf16[128,896]{1,0:T(8,128)(2,1)S(1)} %fusion.26), channel_id=1, source_target_pairs={{0,2},{1,3},{2,0},{3,1},{4,6},{5,7},{6,4},{7,5},{8,10},{9,11},{10,... | collective-permute-start | bytes 688136 | tf_op jit(solution)/shard_map/ppermute | solution.py:70
  121.0 17.6 %all-to-all-start.3 = ((bf16[16,8,896]{2,1,0:T(8,128)(2,1)}), bf16[16,8,896]{2,1,0:T(8,128)(2,1)S(1)}, u32[]{:S(2)}, u32[]{:S(2)}) async-start(bf16[16,8,896]{2,1,0:T(8,128)(2,1)} %fusion.30), calls=%async_computation.3 | async-start | bytes 458752 | tf_op jit(solution)/shard_map/all_to_all | solution.py:65
  128.0 1.8 copy-start.4
  129.7 2.0 %copy-start.2 = (bf16[3584,256]{1,0:T(8,128)(2,1)S(1)}, bf16[3584,256]{1,0:T(8,128)(2,1)}, u32[]{:S(2)}) copy-start(bf16[3584,256]{1,0:T(8,128)(2,1)} %copy-done.1) | copy-start | bytes 5505028
  138.6 6.9 %copy-start.5 = (bf16[128,3584]{1,0:T(8,128)(2,1)S(1)}, bf16[128,3584]{1,0:T(8,128)(2,1)}, u32[]{:S(2)}) copy-start(bf16[128,3584]{1,0:T(8,128)(2,1)} %get-tuple-element.15) | copy-start | bytes 2752516
  138.6 6.9 %copy-start.16 = (f32[896,256]{1,0:T(8,128)S(1)}, f32[896,256]{1,0:T(8,128)}, u32[]{:S(2)}) copy-start(f32[896,256]{1,0:T(8,128)} %fusion.82) | copy-start | bytes 2752516
  138.6 13.5 %copy-start.32 = (bf16[16,8,896]{2,1,0:T(8,128)(2,1)}, bf16[16,8,896]{2,1,0:T(8,128)(2,1)S(1)}, u32[]{:S(2)}) copy-start(bf16[16,8,896]{2,1,0:T(8,128)(2,1)S(1)} %all-to-all-done.3) | copy-start | bytes 688132
  138.6 21.0 %all-to-all-start.1 = ((bf16[16,8,3584]{2,1,0:T(8,128)(2,1)}), bf16[16,8,3584]{2,1,0:T(8,128)(2,1)}, u32[]{:S(2)}, u32[]{:S(2)}) async-start(bf16[16,8,3584]{2,1,0:T(8,128)(2,1)} %fusion.3), calls=%async_computation.1 | async-start | bytes 1835008 | tf_op jit(solution)/shard_map/all_to_all | solution.py:65
  145.5 8.7 %copy-start.14 = (f32[896,256]{1,0:T(8,128)S(1)}, f32[896,256]{1,0:T(8,128)}, u32[]{:S(2)}) copy-start(f32[896,256]{1,0:T(8,128)} %fusion.80) | copy-start | bytes 2752516
  145.5 8.7 %copy-start.15 = (f32[896,256]{1,0:T(8,128)S(1)}, f32[896,256]{1,0:T(8,128)}, u32[]{:S(2)}) copy-start(f32[896,256]{1,0:T(8,128)} %fusion.84) | copy-start | bytes 2752516
  148.2 15.5 %collective-permute-start.18 = (bf16[1792,256]{1,0:T(8,128)(2,1)}, bf16[1792,256]{1,0:T(8,128)(2,1)}, u32[]{:S(2)}, u32[]{:S(2)}) collective-permute-start(bf16[1792,256]{1,0:T(8,128)(2,1)} %fusion.14), channel_id=1, source_target_pairs={{0,128},{128,0},{1,129},{129,1},{2,130},{130,2},{3,131},{131,3},{4... | collective-permute-start | bytes 2752520 | tf_op jit(solution)/shard_map/ppermute | solution.py:46
  152.1 3.8 %copy-start.6 = (bf16[128,3584]{1,0:T(8,128)(2,1)S(1)}, bf16[128,3584]{1,0:T(8,128)(2,1)}, u32[]{:S(2)}) copy-start(bf16[128,3584]{1,0:T(8,128)(2,1)} %get-tuple-element.14) | copy-start | bytes 2752516
  152.1 3.8 %copy-start.17 = (f32[256,896]{1,0:T(8,128)S(1)}, f32[256,896]{1,0:T(8,128)}, u32[]{:S(2)}) copy-start(f32[256,896]{1,0:T(8,128)} %fusion.72) | copy-start | bytes 2752516
  152.1 3.8 %copy-start.18 = (f32[256,896]{1,0:T(8,128)S(1)}, f32[256,896]{1,0:T(8,128)}, u32[]{:S(2)}) copy-start(f32[256,896]{1,0:T(8,128)} %fusion.74) | copy-start | bytes 2752516
  152.1 20.0 %collective-permute-start.17 = (bf16[128,896]{1,0:T(8,128)(2,1)}, bf16[128,896]{1,0:T(8,128)(2,1)S(1)}, u32[]{:S(2)}, u32[]{:S(2)}) collective-permute-start(bf16[128,896]{1,0:T(8,128)(2,1)} %bitcast.166), channel_id=1, source_target_pairs={{0,67},{1,66},{2,65},{3,64},{64,3},{65,2},{66,1},{67,0},{4,71},{5,... | collective-permute-start | bytes 688136 | tf_op jit(solution)/shard_map/ppermute | solution.py:51
  155.6 10.8 %collective-permute-start.19 = (bf16[1792,256]{1,0:T(8,128)(2,1)}, bf16[1792,256]{1,0:T(8,128)(2,1)}, u32[]{:S(2)}, u32[]{:S(2)}) collective-permute-start(bf16[1792,256]{1,0:T(8,128)(2,1)} %fusion.17), channel_id=1, source_target_pairs={{0,128},{128,0},{1,129},{129,1},{2,130},{130,2},{3,131},{131,3},{4... | collective-permute-start | bytes 2752520 | tf_op jit(solution)/shard_map/ppermute | solution.py:46
  157.2 12.2 %collective-permute-start.20 = (bf16[256,1792]{1,0:T(8,128)(2,1)}, bf16[256,1792]{1,0:T(8,128)(2,1)}, u32[]{:S(2)}, u32[]{:S(2)}) collective-permute-start(bf16[256,1792]{1,0:T(8,128)(2,1)} %fusion.20), channel_id=1, source_target_pairs={{0,128},{128,0},{1,129},{129,1},{2,130},{130,2},{3,131},{131,3},{4... | collective-permute-start | bytes 2752520 | tf_op jit(solution)/shard_map/ppermute | solution.py:46
  159.6 4.1 %copy-start.8 = (f32[896,256]{1,0:T(8,128)S(1)}, f32[896,256]{1,0:T(8,128)}, u32[]{:S(2)}) copy-start(f32[896,256]{1,0:T(8,128)} %fusion.90) | copy-start | bytes 2752516
  159.6 4.1 %copy-start.11 = (f32[896,256]{1,0:T(8,128)S(1)}, f32[896,256]{1,0:T(8,128)}, u32[]{:S(2)}) copy-start(f32[896,256]{1,0:T(8,128)} %fusion.94) | copy-start | bytes 2752516
  161.4 10.6 %collective-permute-start.5 = (bf16[128,896]{1,0:T(8,128)(2,1)S(1)}, bf16[128,896]{1,0:T(8,128)(2,1)S(1)}, u32[]{:S(2)}, u32[]{:S(2)}) collective-permute-start(bf16[128,896]{1,0:T(8,128)(2,1)S(1)} %get-tuple-element.23), channel_id=1, source_target_pairs={{0,3},{1,0},{2,1},{3,2},{4,7},{5,4},{6,5},{7,6},{8,11},{9,8},{10,9... | collective-permute-start | bytes 688136 | tf_op jit(solution)/shard_map/ppermute | solution.py:70
  163.6 3.1 %copy-start.7 = (f32[896,256]{1,0:T(8,128)S(1)}, f32[896,256]{1,0:T(8,128)}, u32[]{:S(2)}) copy-start(f32[896,256]{1,0:T(8,128)} %fusion.88) | copy-start | bytes 2752516
  163.6 3.1 %copy-start.10 = (f32[896,256]{1,0:T(8,128)S(1)}, f32[896,256]{1,0:T(8,128)}, u32[]{:S(2)}) copy-start(f32[896,256]{1,0:T(8,128)} %fusion.92) | copy-start | bytes 2752516
  163.6 9.4 %collective-permute-start.4 = (bf16[128,896]{1,0:T(8,128)(2,1)S(1)}, bf16[128,896]{1,0:T(8,128)(2,1)S(1)}, u32[]{:S(2)}, u32[]{:S(2)}) collective-permute-start(bf16[128,896]{1,0:T(8,128)(2,1)S(1)} %get-tuple-element.24), channel_id=1, source_target_pairs={{0,1},{1,2},{2,3},{3,0},{4,5},{5,6},{6,7},{7,4},{8,9},{9,10},{10,1... | collective-permute-start | bytes 688136 | tf_op jit(solution)/shard_map/ppermute | solution.py:70
  166.4 3.1 %copy-start.9 = (f32[256,896]{1,0:T(8,128)S(1)}, f32[256,896]{1,0:T(8,128)}, u32[]{:S(2)}) copy-start(f32[256,896]{1,0:T(8,128)} %fusion.76) | copy-start | bytes 2752516
  166.4 3.1 %copy-start.12 = (f32[256,896]{1,0:T(8,128)S(1)}, f32[256,896]{1,0:T(8,128)}, u32[]{:S(2)}) copy-start(f32[256,896]{1,0:T(8,128)} %fusion.78) | copy-start | bytes 2752516
  166.4 16.5 %collective-permute-start.3 = (bf16[128,896]{1,0:T(8,128)(2,1)S(1)}, bf16[128,896]{1,0:T(8,128)(2,1)S(1)}, u32[]{:S(2)}, u32[]{:S(2)}) collective-permute-start(bf16[128,896]{1,0:T(8,128)(2,1)S(1)} %get-tuple-element.22), channel_id=1, source_target_pairs={{0,2},{1,3},{2,0},{3,1},{4,6},{5,7},{6,4},{7,5},{8,10},{9,11},{10,... | collective-permute-start | bytes 688136 | tf_op jit(solution)/shard_map/ppermute | solution.py:70
